TPU v7x, 32 devices: a whole 2x2x4 slice. The times are simulated.
32 devices in a mesh: leaf: 4 (over y, x), blk: 8 (over z, core).
Axes of the slice: x: 2, y: 2, z: 4, core: 2. Of those that a mesh axis runs over, the one named last changes fastest.
Arguments:
- leaf_rhs: bfloat16 [10240, 256], P(('leaf', 'blk')), may hold values from -6 to 6
- leaf_inverse: bfloat16 [10240, 2560], P(('leaf', 'blk')), may hold values from -0.125 to 0.125
- leaf_lower: bfloat16 [4096, 2560], P(('leaf', 'blk')), may hold values from -0.125 to 0.125
- sep_rhs: bfloat16 [2, 2048, 256], P(None, ('leaf', 'blk')), may hold values from -6 to 6
- sep_inverse: bfloat16 [2048, 3072], P(('leaf', 'blk'))
- sep_lower: bfloat16 [4096, 1024], P(('leaf', 'blk'))
- slot_map: int32 [2, 32, 2], P(None, ('leaf', 'blk')), may hold values from 0 to 5, as said below
Outputs:
- leaf_solution: bfloat16 [10240, 256], P(('leaf', 'blk'))
- sep_solution: bfloat16 [2, 2048, 256], P(None, ('leaf', 'blk'))
Inputs may be any that keep to these rules, and one draw needn't show every extreme that they name: For every level below the top, slot_map[h-1, q] holds two different numbers of 0 to 5; at the top level it holds 0 and 1 in some order.
All inputs are finite; a program needn't handle non-finite values.
Results may differ from a plain program's by a relative error of at most 0.015.
Values may be sent and summed in bfloat16 or wider, within the bound.
No kernel may reach another device: no remote copies, remote signals or barrier semaphores. Data moves between devices by JAX's collectives and lax.ppermute only.
A program may use at most 128 MiB of HBM per device.

v0:
```python
import jax
import jax.numpy as jnp
from jax import lax
from jax.experimental import pallas as pl
from jax.experimental.pallas import tpu as pltpu
from jax.sharding import PartitionSpec as P


DIRECT_LIMIT = 16


def exchange(value, leaf_mask, blk_mask):
    leaves = lax.axis_size("leaf")
    blks = lax.axis_size("blk")
    pairs = [
        (k * blks + b, (k ^ leaf_mask) * blks + (b ^ blk_mask))
        for k in range(leaves)
        for b in range(blks)
    ]
    return lax.ppermute(value, ("leaf", "blk"), pairs)


def product(matrix, vectors):
    return jnp.dot(matrix, vectors, preferred_element_type=jnp.float32)


def leaf_solve(pieces, near, far):
    count = len(pieces)
    rows, half = pieces[0].shape
    dtype = pieces[0].dtype

    def body(*refs):
        piece_refs = refs[:count]
        near_ref, far_ref = refs[count : count + 2]
        all_ref, mine_ref, other_ref = refs[count + 2 : count + 5]
        rhs, near_vmem, far_vmem, sems = refs[count + 5 :]
        b = lax.axis_index("blk")
        core = b % 2
        copies = []
        for mask in range(count):
            where = pl.multiple_of((b ^ mask) * rows, 16)
            copies.append(
                pltpu.make_async_copy(
                    piece_refs[mask], rhs.at[pl.ds(where, rows)], sems.at[mask]
                )
            )
        near_copy = pltpu.make_async_copy(near_ref, near_vmem, sems.at[count])
        far_copy = pltpu.make_async_copy(far_ref, far_vmem, sems.at[count + 1])
        for copy in copies:
            copy.start()
        near_copy.start()
        far_copy.start()
        for copy in copies:
            copy.wait()
        near_copy.wait()
        mine = jnp.dot(near_vmem[...], rhs[...], preferred_element_type=jnp.float32).astype(dtype)
        mine_ref[...] = mine
        all_ref[pl.ds(pl.multiple_of(core * rows, 16), rows)] = mine
        far_copy.wait()
        other = jnp.dot(far_vmem[...], rhs[...], preferred_element_type=jnp.float32).astype(dtype)
        other_ref[...] = other
        all_ref[pl.ds(pl.multiple_of((1 - core) * rows, 16), rows)] = other

    vmem = pl.BlockSpec(memory_space=pltpu.VMEM)
    return pl.pallas_call(
        body,
        in_specs=[pl.BlockSpec(memory_space=pl.ANY)] * (count + 2),
        out_specs=[vmem] * 3,
        out_shape=[
            jax.ShapeDtypeStruct((2 * rows, half), dtype),
            jax.ShapeDtypeStruct((rows, half), dtype),
            jax.ShapeDtypeStruct((rows, half), dtype),
        ],
        scratch_shapes=[
            pltpu.VMEM((count * rows, half), dtype),
            pltpu.VMEM(near.shape, dtype),
            pltpu.VMEM(far.shape, dtype),
            pltpu.SemaphoreType.DMA((count + 2,)),
        ],
        cost_estimate=pl.CostEstimate(
            flops=4 * rows * count * rows * half, bytes_accessed=2 * near.size * 2, transcendentals=0
        ),
        name="leaf_solve",
    )(*pieces, near, far)


def on_device(leaf_rhs, leaf_inverse, leaf_lower, sep_rhs, sep_inverse, sep_lower, slot_map):
    leaves = lax.axis_size("leaf")
    blks = lax.axis_size("blk")
    chips = blks // 2
    k = lax.axis_index("leaf")
    b = lax.axis_index("blk")
    z = b // 2
    core = b % 2
    half = leaf_rhs.shape[1] // 2
    levels, pivots = sep_rhs.shape[0], sep_rhs.shape[1]
    base_width = pivots * blks
    rows = leaf_rhs.shape[0]
    dtype = leaf_rhs.dtype

    def columns_of(value, which):
        return lax.dynamic_slice_in_dim(value, which * half, half, value.ndim - 1)

    def in_order(mine, other, axis=0):
        first = jnp.where(core == 0, mine, other)
        second = jnp.where(core == 0, other, mine)
        return jnp.concatenate([first, second], axis=axis)

    def put(buffer, piece, index):
        return lax.dynamic_update_slice_in_dim(buffer, piece, index * piece.shape[0], 0)

    own_half = columns_of(leaf_rhs, core)
    other_half = columns_of(leaf_rhs, 1 - core)
    arrived = [own_half]
    for mask in range(1, blks):
        arrived.append(exchange(own_half if mask % 2 == 0 else other_half, 0, mask))
    inverse_other = exchange(leaf_inverse, 0, 1)
    lower_other = exchange(leaf_lower, 0, 1)
    slot_other = exchange(slot_map, 0, 1)
    sep_rhs_other = exchange(columns_of(sep_rhs, 1 - core), 0, 1)
    sep_lower_other = exchange(sep_lower, 0, 1)
    sep_inverse_other = exchange(sep_inverse, 0, 1)

    slots = in_order(slot_map, slot_other, 1)
    seps = in_order(columns_of(sep_rhs, core), sep_rhs_other, 1)

    s_all, s_mine, s_other = leaf_solve(arrived, leaf_inverse, inverse_other)
    got = [(m, exchange(s_all, 0, m)) for m in range(blks - 2, 0, -2)]
    s_full = put(jnp.zeros((blks * rows, half), dtype), s_all, z)
    for m, value in got:
        s_full = put(s_full, value, z ^ (m // 2))

    inv_chip = in_order(sep_inverse, sep_inverse_other)
    low_chip = in_order(sep_lower, sep_lower_other)

    top_mask = 2 ** (levels - 1)
    top_offset = base_width * (2**levels - 2)
    top = sep_inverse[:, top_offset:]

    def leaf_columns(leaf_index):
        near = lax.dynamic_slice_in_dim(top, leaf_index * base_width, base_width, 1)
        far = lax.dynamic_slice_in_dim(top, (leaf_index ^ top_mask) * base_width, base_width, 1)
        return jnp.concatenate([near, far], axis=1)

    paired = levels > 1
    blocks = [leaf_columns(k)[None]]
    for a in range(1, leaves):
        block = leaf_columns(k ^ a)[None]
        if a == 1 and paired:
            block = jnp.concatenate([sep_inverse[None, :, : 2 * base_width], block])
        blocks.append(exchange(block, a, 0))
    mine = jnp.concatenate(blocks)
    other = exchange(mine, 0, 1)
    if paired:
        their_slots = exchange(slots[0], 1, 0)
        their_sep = exchange(seps[0], 1, 0)
        inv_theirs = in_order(mine[1], other[1])
        mine = jnp.concatenate([mine[:1], mine[2:]])
        other = jnp.concatenate([other[:1], other[2:]])
    first = jnp.where(core == 0, mine, other)
    second = jnp.where(core == 0, other, mine)
    top_rows = jnp.stack([first, second], axis=1).reshape(-1, 2 * base_width)

    update = -in_order(product(leaf_lower, s_full), product(lower_other, s_full))
    leaf_back = exchange(s_other, 0, 1)
    leaf_solution = in_order(s_mine, leaf_back, 1)

    def gather_z(piece):
        pieces = [piece] + [exchange(piece, 0, m) for m in range(2, blks, 2)]
        result = jnp.zeros((chips,) + piece.shape, piece.dtype)
        for m, value in enumerate(pieces):
            result = lax.dynamic_update_slice_in_dim(result, value[None], z ^ m, 0)
        return result

    def gather_node(piece, height):
        members = 2**height
        place = k % members
        if members * chips <= DIRECT_LIMIT:
            result = jnp.zeros((members * chips,) + piece.shape, piece.dtype)
            pieces = []
            for a in range(members):
                for m in range(chips):
                    value = piece if a == 0 and m == 0 else exchange(piece, a, 2 * m)
                    pieces.append(((place ^ a) * chips + (z ^ m), value))
            for where, value in pieces:
                result = lax.dynamic_update_slice_in_dim(result, value[None], where, 0)
            return result.reshape(-1, piece.shape[-1])
        joined = piece[None]
        for bit in range(height):
            theirs = exchange(joined, 2**bit, 0)
            upper = (k // 2**bit) % 2 == 1
            joined = jnp.concatenate(
                [jnp.where(upper, theirs, joined), jnp.where(upper, joined, theirs)], axis=0
            )
        return jnp.swapaxes(gather_z(joined), 0, 1).reshape(-1, piece.shape[-1])

    def mix(slot_rows, targets, count):
        result = []
        for t in count:
            hit = (targets == t)[:, :, None, None]
            result.append(jnp.sum(jnp.where(hit, slot_rows, 0), axis=1).reshape(-1, half))
        return result

    def rest_rows(front):
        slots_of = [value.reshape(2, pivots, half) for value in front]
        return jnp.stack(slots_of, axis=1).reshape(-1, half)

    solutions = []
    for height in range(1, levels):
        mask = 2 ** (height - 1)
        offset = base_width * (2**height - 2)
        width = base_width * 2**height
        targets = slots[height - 1]
        slot_rows = update.reshape(2, 2, pivots, half)
        theirs = exchange(slot_rows.astype(dtype), mask, 0).astype(jnp.float32)
        their_targets = their_slots if height == 1 else exchange(targets, mask, 0)
        own = mix(slot_rows, targets, range(3))
        sent = mix(theirs, their_targets, range(3, 6))
        pivot = (seps[height - 1].astype(jnp.float32) + own[0] + sent[0]).astype(dtype)
        rest = rest_rows([own[1] + sent[1], own[2] + sent[2]])
        inverse_here = inv_chip[:, offset : offset + width]
        if height == 1:
            upper = k % 2 == 1

            def by_leaf(near, far):
                return jnp.stack([jnp.where(upper, far, near), jnp.where(upper, near, far)])

            (their_own,) = mix(theirs, their_targets, range(1))
            (their_sent,) = mix(slot_rows, targets, range(3, 4))
            their_pivot = (their_sep.astype(jnp.float32) + their_own + their_sent).astype(dtype)
            pivots_all = gather_z(by_leaf(pivot, their_pivot))
            pivots_all = jnp.swapaxes(pivots_all, 0, 1).reshape(-1, half)
            solved = product(inverse_here, pivots_all).astype(dtype)
            their_solved = product(inv_theirs, pivots_all).astype(dtype)
            solved_all = gather_z(by_leaf(solved, their_solved))
            solved_all = jnp.swapaxes(solved_all, 0, 1).reshape(-1, half)
        else:
            solved = product(inverse_here, gather_node(pivot, height)).astype(dtype)
            solved_all = gather_node(solved, height)
        solutions.append(solved)
        update = rest - product(low_chip[:, offset : offset + width], solved_all)

    own, sent = mix(update.reshape(2, 2, pivots, half), slots[levels - 1], range(2))
    own = own + seps[levels - 1].astype(jnp.float32)
    parts = gather_z(jnp.stack([own, sent]).astype(dtype))
    contributions = jnp.swapaxes(parts, 0, 1).reshape(-1, half)
    partial = product(top_rows, contributions).reshape(leaves, 2 * pivots, half)
    rounded = partial.astype(dtype)
    total = partial[0]
    for a in range(1, leaves):
        total = total + exchange(rounded[a], a, 0).astype(jnp.float32)
    solutions.append(total.astype(dtype))

    outs = []
    for solved in solutions:
        mine = lax.dynamic_slice_in_dim(solved, core * pivots, pivots, 0)
        other = lax.dynamic_slice_in_dim(solved, (1 - core) * pivots, pivots, 0)
        outs.append(in_order(mine, exchange(other, 0, 1), 1))
    return leaf_solution, jnp.stack(outs)


def solution(mesh):
    return jax.shard_map(
        on_device,
        mesh=mesh,
        in_specs=(
            P(("leaf", "blk"), None),
            P(("leaf", "blk"), None),
            P(("leaf", "blk"), None),
            P(None, ("leaf", "blk"), None),
            P(("leaf", "blk"), None),
            P(("leaf", "blk"), None),
            P(None, ("leaf", "blk"), None),
        ),
        out_specs=(P(("leaf", "blk"), None), P(None, ("leaf", "blk"), None)),
        check_vma=False,
    )
```

profile of v0, /device:TPU:0, one launch (start us, length us, event | category | flops | bytes accessed | tf_op | source)
XLA Modules:
  0.0 116.8 jit_solution(14197854205379259138)
XLA Ops:
  0.7 1.6 %constant_dynamic-slice_fusion.10 = (bf16[320,128]{1,0:T(8,128)(2,1)}, bf16[320,128]{1,0:T(8,128)(2,1)S(1)}) fusion(bf16[320,256]{1,0:T(8,128)(2,1)} %param.7, s32[]{:T(128)S(6)} %select_n.281, s32[]{:T(128)S(6)} %select_n.280), kind=kLoop, calls=%fused_computation.119 | loop fusion | bytes 327688 | tf_op jit(solution)/shard_map/dynamic_slice | solution.py:102
  2.8 1.4 %constant_dynamic-slice_fusion.9 = bf16[2,64,128]{2,1,0:T(8,128)(2,1)} fusion(bf16[2,64,256]{2,1,0:T(8,128)(2,1)} %param.10, s32[]{:T(128)S(6)} %select_n.281), kind=kLoop, calls=%fused_computation.118 | loop fusion | bytes 65540 | tf_op jit(solution)/shard_map/dynamic_slice | solution.py:102
  6.5 3.0 %collective-permute-start.24 = (bf16[1,64,1024]{2,1,0:T(8,128)(2,1)}, bf16[1,64,1024]{2,1,0:T(8,128)(2,1)S(1)}, u32[]{:S(2)}, u32[]{:S(2)}) collective-permute-start(bf16[1,64,1024]{2,1,0:T(8,128)(2,1)} %get-tuple-element.56), channel_id=1, source_target_pairs={{0,16},{1,17},{2,18},{3,19},{4,20},{5,21},{6,22},{7,23},{8,24},{9,... | collective-permute-start | bytes 393224 | tf_op jit(solution)/shard_map/ppermute | solution.py:20
  11.0 1.5 %collective-permute-start.13 = (s32[2,2]{1,0:T(2,128)S(1)}, s32[2,2]{1,0:T(2,128)S(1)}, u32[]{:S(2)}, u32[]{:S(2)}) collective-permute-start(s32[2,2]{1,0:T(2,128)S(1)} %get-tuple-element.22), channel_id=1, source_target_pairs={{0,8},{1,9},{2,10},{3,11},{4,12},{5,13},{6,14},{7,15},{8,0},{9,1},... | collective-permute-start | bytes 56 | tf_op jit(solution)/shard_map/ppermute | solution.py:20
  14.5 1.5 %collective-permute-start.23 = (bf16[2,64,1024]{2,1,0:T(8,128)(2,1)S(1)}, bf16[2,64,1024]{2,1,0:T(8,128)(2,1)S(1)}, u32[]{:S(2)}, u32[]{:S(2)}) collective-permute-start(bf16[2,64,1024]{2,1,0:T(8,128)(2,1)S(1)} %pad_maximum_fusion.8), channel_id=1, source_target_pairs={{0,8},{1,9},{2,10},{3,11},{4,12},{5,13},{6,14},{7,15},{8,0},{9,1},... | collective-permute-start | bytes 786440 | tf_op jit(solution)/shard_map/ppermute | solution.py:20
  19.1 1.9 %collective-permute-start.2 = (bf16[320,128]{1,0:T(8,128)(2,1)}, bf16[320,128]{1,0:T(8,128)(2,1)S(1)}, u32[]{:S(2)}, u32[]{:S(2)}) collective-permute-start(bf16[320,128]{1,0:T(8,128)(2,1)} %get-tuple-element.41), channel_id=1, source_target_pairs={{0,3},{1,2},{2,1},{3,0},{4,7},{5,6},{6,5},{7,4},{8,11},{9,10},{10,... | collective-permute-start | bytes 245768 | tf_op jit(solution)/shard_map/ppermute | solution.py:20
  20.9 4.1 %collective-permute-done.25 = bf16[1,64,1024]{2,1,0:T(8,128)(2,1)S(1)} collective-permute-done((bf16[1,64,1024]{2,1,0:T(8,128)(2,1)S(1)}, bf16[1,64,1024]{2,1,0:T(8,128)(2,1)S(1)}, u32[]{:S(2)}, u32[]{:S(2)}) %collective-permute-start.25) | collective-permute-done | bytes 131104 | tf_op jit(solution)/shard_map/ppermute | solution.py:20
  25.0 1.6 %collective-permute-start.1 = (bf16[320,128]{1,0:T(8,128)(2,1)S(1)}, bf16[320,128]{1,0:T(8,128)(2,1)S(1)}, u32[]{:S(2)}, u32[]{:S(2)}) collective-permute-start(bf16[320,128]{1,0:T(8,128)(2,1)S(1)} %get-tuple-element.42.refs_0_), channel_id=1, source_target_pairs={{0,2},{1,3},{2,0},{3,1},{4,6},{5,7},{6,4},{7,5},{8,10},{9,11},{10,... | collective-permute-start | bytes 245768 | tf_op jit(solution)/shard_map/ppermute | solution.py:20
  28.4 2.7 %collective-permute-done.26 = bf16[5,64,1024]{2,1,0:T(8,128)(2,1)S(1)} collective-permute-done((bf16[5,64,1024]{2,1,0:T(8,128)(2,1)S(1)}, bf16[5,64,1024]{2,1,0:T(8,128)(2,1)S(1)}, u32[]{:S(2)}, u32[]{:S(2)}) %collective-permute-start.26) | collective-permute-done | bytes 655392 | tf_op jit(solution)/shard_map/ppermute | solution.py:20
  31.0 2.6 %collective-permute-start.3 = (bf16[320,128]{1,0:T(8,128)(2,1)S(1)}, bf16[320,128]{1,0:T(8,128)(2,1)S(1)}, u32[]{:S(2)}, u32[]{:S(2)}) collective-permute-start(bf16[320,128]{1,0:T(8,128)(2,1)S(1)} %get-tuple-element.42.refs_0_), channel_id=1, source_target_pairs={{0,4},{1,5},{2,6},{3,7},{4,0},{5,1},{6,2},{7,3},{8,12},{9,13},{10,... | collective-permute-start | bytes 245768 | tf_op jit(solution)/shard_map/ppermute | solution.py:20
  34.6 2.3 %collective-permute-start.5 = (bf16[320,128]{1,0:T(8,128)(2,1)S(1)}, bf16[320,128]{1,0:T(8,128)(2,1)S(1)}, u32[]{:S(2)}, u32[]{:S(2)}) collective-permute-start(bf16[320,128]{1,0:T(8,128)(2,1)S(1)} %get-tuple-element.42.refs_0_), channel_id=1, source_target_pairs={{0,6},{1,7},{2,4},{3,5},{4,2},{5,3},{6,0},{7,1},{8,14},{9,15},{10,... | collective-permute-start | bytes 245768 | tf_op jit(solution)/shard_map/ppermute | solution.py:20
  36.9 1.3 %collective-permute-start.6 = (bf16[320,128]{1,0:T(8,128)(2,1)}, bf16[320,128]{1,0:T(8,128)(2,1)S(1)}, u32[]{:S(2)}, u32[]{:S(2)}) collective-permute-start(bf16[320,128]{1,0:T(8,128)(2,1)} %get-tuple-element.41), channel_id=1, source_target_pairs={{0,7},{1,6},{2,5},{3,4},{4,3},{5,2},{6,1},{7,0},{8,15},{9,14},{10,... | collective-permute-start | bytes 245768 | tf_op jit(solution)/shard_map/ppermute | solution.py:20
  38.8 6.8 %collective-permute-done.4.refs_5_ = bf16[320,128]{1,0:T(8,128)(2,1)S(1)} collective-permute-done((bf16[320,128]{1,0:T(8,128)(2,1)}, bf16[320,128]{1,0:T(8,128)(2,1)S(1)}, u32[]{:S(2)}, u32[]{:S(2)}) %collective-permute-start.4) | collective-permute-done | bytes 81952 | tf_op jit(solution)/shard_map/ppermute | solution.py:20
  47.7 4.5 %leaf_solve.1 = (bf16[640,128]{1,0:T(8,128)(2,1)}, bf16[320,128]{1,0:T(8,128)(2,1)}, bf16[320,128]{1,0:T(8,128)(2,1)}) custom-call(bf16[320,128]{1,0:T(8,128)(2,1)} %copy-done.2, bf16[320,128]{1,0:T(8,128)(2,1)} %collective-permute-done.refs_1_, bf16[320,128]{1,0:T(8,128)(2,1)} %copy-done.13, bf16[320,128]{1,0:T(8,128)(2,1)} %copy-done.12, ...), custom_call_target="tpu_custom_call" | custom-call | flops 419430400 | bytes 3276800 | tf_op jit(solution)/shard_map/leaf_solve/pallas_call | solution.py:65
  52.2 1.5 %collective-permute-start.14 = (bf16[640,128]{1,0:T(8,128)(2,1)}, bf16[640,128]{1,0:T(8,128)(2,1)S(1)}, u32[]{:S(2)}, u32[]{:S(2)}) collective-permute-start(bf16[640,128]{1,0:T(8,128)(2,1)} %get-tuple-element.7), channel_id=1, source_target_pairs={{0,6},{1,7},{2,4},{3,5},{4,2},{5,3},{6,0},{7,1},{8,14},{9,15},{10,... | collective-permute-start | bytes 491528 | tf_op jit(solution)/shard_map/ppermute | solution.py:20
  53.7 2.6 %collective-permute-start.15 = (bf16[640,128]{1,0:T(8,128)(2,1)}, bf16[640,128]{1,0:T(8,128)(2,1)S(1)}, u32[]{:S(2)}, u32[]{:S(2)}) collective-permute-start(bf16[640,128]{1,0:T(8,128)(2,1)} %get-tuple-element.7), channel_id=1, source_target_pairs={{0,4},{1,5},{2,6},{3,7},{4,0},{5,1},{6,2},{7,3},{8,12},{9,13},{10,... | collective-permute-start | bytes 491528 | tf_op jit(solution)/shard_map/ppermute | solution.py:20
  59.0 2.4 %collective-permute-done.14 = bf16[640,128]{1,0:T(8,128)(2,1)S(1)} collective-permute-done((bf16[640,128]{1,0:T(8,128)(2,1)}, bf16[640,128]{1,0:T(8,128)(2,1)S(1)}, u32[]{:S(2)}, u32[]{:S(2)}) %collective-permute-start.14) | collective-permute-done | bytes 163872 | tf_op jit(solution)/shard_map/ppermute | solution.py:20
  61.5 9.3 %collective-permute-done.15 = bf16[640,128]{1,0:T(8,128)(2,1)S(1)} collective-permute-done((bf16[640,128]{1,0:T(8,128)(2,1)}, bf16[640,128]{1,0:T(8,128)(2,1)S(1)}, u32[]{:S(2)}, u32[]{:S(2)}) %collective-permute-start.15) | collective-permute-done | bytes 163872 | tf_op jit(solution)/shard_map/ppermute | solution.py:20
  70.9 1.4 %fusion.35 = f32[128,128]{0,1:T(8,128)S(1)} fusion(bf16[128,2560]{1,0:T(8,128)(2,1)} %collective-permute-done.17, bf16[2560,128]{1,0:T(8,128)(2,1)S(1)} %constant_dynamic-update-slice_fusion), kind=kOutput, calls=%fused_computation.144 | convolution fusion | flops 83886080 | bytes 1376256 | tf_op jit(solution)/shard_map/dot_general | solution.py:24
  72.3 1.4 %select_bitcast_fusion.3 = (f32[128,128]{1,0:T(8,128)S(1)}, f32[128,128]{1,0:T(8,128)S(1)}) fusion(f32[128,128]{0,1:T(8,128)S(1)} %fusion.35, pred[]{:T(512)S(6)} %eq.88, bf16[128,2560]{1,0:T(8,128)(2,1)} %param.9, bf16[2560,128]{1,0:T(8,128)(2,1)S(1)} %constant_dynamic-update-slice_fusion), kind=kOutput, calls=%fused_computation.89 | convolution fusion | flops 83918848 | bytes 1507329 | tf_op jit(solution)/shard_map/dot_general | solution.py:24
  75.2 3.0 %collective-permute-done.18 = bf16[2,2,64,128]{3,2,1,0:T(8,128)(2,1)S(1)} collective-permute-done((bf16[2,2,64,128]{3,2,1,0:T(8,128)(2,1)S(1)}, bf16[2,2,64,128]{3,2,1,0:T(8,128)(2,1)S(1)}, u32[]{:S(2)}, u32[]{:S(2)}) %collective-permute-start.18) | collective-permute-done | bytes 65568 | tf_op jit(solution)/shard_map/ppermute | solution.py:20
  79.3 2.9 %collective-permute-start.20 = (bf16[2,128,128]{2,1,0:T(8,128)(2,1)S(1)}, bf16[2,128,128]{2,1,0:T(8,128)(2,1)S(1)}, u32[]{:S(2)}, u32[]{:S(2)}) collective-permute-start(bf16[2,128,128]{2,1,0:T(8,128)(2,1)S(1)} %pad_maximum_fusion.12), channel_id=1, source_target_pairs={{0,4},{1,5},{2,6},{3,7},{4,0},{5,1},{6,2},{7,3},{8,12},{9,13},{10,... | collective-permute-start | bytes 196616 | tf_op jit(solution)/shard_map/ppermute | solution.py:20
  82.1 1.5 %collective-permute-start.21 = (bf16[2,128,128]{2,1,0:T(8,128)(2,1)S(1)}, bf16[2,128,128]{2,1,0:T(8,128)(2,1)S(1)}, u32[]{:S(2)}, u32[]{:S(2)}) collective-permute-start(bf16[2,128,128]{2,1,0:T(8,128)(2,1)S(1)} %pad_maximum_fusion.12), channel_id=1, source_target_pairs={{0,6},{1,7},{2,4},{3,5},{4,2},{5,3},{6,0},{7,1},{8,14},{9,15},{10,... | collective-permute-start | bytes 196616 | tf_op jit(solution)/shard_map/ppermute | solution.py:20
  84.8 3.4 %collective-permute-done.21 = bf16[2,128,128]{2,1,0:T(8,128)(2,1)S(1)} collective-permute-done((bf16[2,128,128]{2,1,0:T(8,128)(2,1)S(1)}, bf16[2,128,128]{2,1,0:T(8,128)(2,1)S(1)}, u32[]{:S(2)}, u32[]{:S(2)}) %collective-permute-start.21) | collective-permute-done | bytes 65568 | tf_op jit(solution)/shard_map/ppermute | solution.py:20
  88.8 2.0 %collective-permute-start.29 = (bf16[2,128,128]{2,1,0:T(8,128)(2,1)S(1)}, bf16[2,128,128]{2,1,0:T(8,128)(2,1)S(1)}, u32[]{:S(2)}, u32[]{:S(2)}) collective-permute-start(bf16[2,128,128]{2,1,0:T(8,128)(2,1)S(1)} %pad_maximum_fusion.13), channel_id=1, source_target_pairs={{0,4},{1,5},{2,6},{3,7},{4,0},{5,1},{6,2},{7,3},{8,12},{9,13},{10,... | collective-permute-start | bytes 196616 | tf_op jit(solution)/shard_map/ppermute | solution.py:20
  90.9 2.3 %collective-permute-start.30 = (bf16[2,128,128]{2,1,0:T(8,128)(2,1)S(1)}, bf16[2,128,128]{2,1,0:T(8,128)(2,1)S(1)}, u32[]{:S(2)}, u32[]{:S(2)}) collective-permute-start(bf16[2,128,128]{2,1,0:T(8,128)(2,1)S(1)} %pad_maximum_fusion.13), channel_id=1, source_target_pairs={{0,6},{1,7},{2,4},{3,5},{4,2},{5,3},{6,0},{7,1},{8,14},{9,15},{10,... | collective-permute-start | bytes 196616 | tf_op jit(solution)/shard_map/ppermute | solution.py:20
  94.3 2.7 %collective-permute-done.30 = bf16[2,128,128]{2,1,0:T(8,128)(2,1)S(1)} collective-permute-done((bf16[2,128,128]{2,1,0:T(8,128)(2,1)S(1)}, bf16[2,128,128]{2,1,0:T(8,128)(2,1)S(1)}, u32[]{:S(2)}, u32[]{:S(2)}) %collective-permute-start.30) | collective-permute-done | bytes 65568 | tf_op jit(solution)/shard_map/ppermute | solution.py:20
  97.6 3.6 %collective-permute-start.32 = (bf16[2,128,128]{2,1,0:T(8,128)(2,1)S(1)}, bf16[2,128,128]{2,1,0:T(8,128)(2,1)S(1)}, u32[]{:S(2)}, u32[]{:S(2)}) collective-permute-start(bf16[2,128,128]{2,1,0:T(8,128)(2,1)S(1)} %pad_maximum_fusion.14), channel_id=1, source_target_pairs={{0,4},{1,5},{2,6},{3,7},{4,0},{5,1},{6,2},{7,3},{8,12},{9,13},{10,... | collective-permute-start | bytes 196616 | tf_op jit(solution)/shard_map/ppermute | solution.py:20
  102.0 1.3 %collective-permute-done.32 = bf16[2,128,128]{2,1,0:T(8,128)(2,1)S(1)} collective-permute-done((bf16[2,128,128]{2,1,0:T(8,128)(2,1)S(1)}, bf16[2,128,128]{2,1,0:T(8,128)(2,1)S(1)}, u32[]{:S(2)}, u32[]{:S(2)}) %collective-permute-start.32) | collective-permute-done | bytes 65568 | tf_op jit(solution)/shard_map/ppermute | solution.py:20
  103.4 3.8 %collective-permute-done.33 = bf16[2,128,128]{2,1,0:T(8,128)(2,1)S(1)} collective-permute-done((bf16[2,128,128]{2,1,0:T(8,128)(2,1)S(1)}, bf16[2,128,128]{2,1,0:T(8,128)(2,1)S(1)}, u32[]{:S(2)}, u32[]{:S(2)}) %collective-permute-start.33) | collective-permute-done | bytes 65568 | tf_op jit(solution)/shard_map/ppermute | solution.py:20
  108.2 1.7 %collective-permute-start.35 = (bf16[128,128]{1,0:T(8,128)(2,1)S(1)}, bf16[128,128]{1,0:T(8,128)(2,1)S(1)}, u32[]{:S(2)}, u32[]{:S(2)}) collective-permute-start(bf16[128,128]{1,0:T(8,128)(2,1)S(1)} %get-tuple-element.45), channel_id=1, source_target_pairs={{0,16},{1,17},{2,18},{3,19},{4,20},{5,21},{6,22},{7,23},{8,24},{9,... | collective-permute-start | bytes 98312 | tf_op jit(solution)/shard_map/ppermute | solution.py:20
  112.2 2.6 %collective-permute-done.36 = bf16[128,128]{1,0:T(8,128)(2,1)S(1)} collective-permute-done((bf16[128,128]{1,0:T(8,128)(2,1)S(1)}, bf16[128,128]{1,0:T(8,128)(2,1)S(1)}, u32[]{:S(2)}, u32[]{:S(2)}) %collective-permute-start.36) | collective-permute-done | bytes 32800 | tf_op jit(solution)/shard_map/ppermute | solution.py:20
  (174 shorter events, 29.2 us)
Async XLA Ops:
  2.3 32.2 %collective-permute-start = (bf16[320,128]{1,0:T(8,128)(2,1)}, bf16[320,128]{1,0:T(8,128)(2,1)}, u32[]{:S(2)}, u32[]{:S(2)}) collective-permute-start(bf16[320,128]{1,0:T(8,128)(2,1)} %get-tuple-element.41), channel_id=1, source_target_pairs={{0,1},{1,0},{2,3},{3,2},{4,5},{5,4},{6,7},{7,6},{8,9},{9,8},{10,11... | collective-permute-start | bytes 245768 | tf_op jit(solution)/shard_map/ppermute | solution.py:20
  2.8 6.9 %collective-permute-start.12 = (s32[2,1,2]{2,1,0:T(1,128)}, s32[2,1,2]{2,1,0:T(1,128)}, u32[]{:S(2)}, u32[]{:S(2)}) collective-permute-start(s32[2,1,2]{2,1,0:T(1,128)} %param.13), channel_id=1, source_target_pairs={{0,1},{1,0},{2,3},{3,2},{4,5},{5,4},{6,7},{7,6},{8,9},{9,8},{10,11... | collective-permute-start | bytes 56 | tf_op jit(solution)/shard_map/ppermute | solution.py:20
  4.2 12.4 %collective-permute-start.10 = (bf16[2,64,128]{2,1,0:T(8,128)(2,1)}, bf16[2,64,128]{2,1,0:T(8,128)(2,1)}, u32[]{:S(2)}, u32[]{:S(2)}) collective-permute-start(bf16[2,64,128]{2,1,0:T(8,128)(2,1)} %constant_dynamic-slice_fusion.9), channel_id=1, source_target_pairs={{0,1},{1,0},{2,3},{3,2},{4,5},{5,4},{6,7},{7,6},{8,9},{9,8},{10,11... | collective-permute-start | bytes 98312 | tf_op jit(solution)/shard_map/ppermute | solution.py:20
  4.7 22.1 %collective-permute-start.9 = (bf16[64,3072]{1,0:T(8,128)(2,1)}, bf16[64,3072]{1,0:T(8,128)(2,1)}, u32[]{:S(2)}, u32[]{:S(2)}) collective-permute-start(bf16[64,3072]{1,0:T(8,128)(2,1)} %param.11), channel_id=1, source_target_pairs={{0,1},{1,0},{2,3},{3,2},{4,5},{5,4},{6,7},{7,6},{8,9},{9,8},{10,11... | collective-permute-start | bytes 1179656 | tf_op jit(solution)/shard_map/ppermute | solution.py:20
  6.5 12.6 %collective-permute-start.24 = (bf16[1,64,1024]{2,1,0:T(8,128)(2,1)}, bf16[1,64,1024]{2,1,0:T(8,128)(2,1)S(1)}, u32[]{:S(2)}, u32[]{:S(2)}) collective-permute-start(bf16[1,64,1024]{2,1,0:T(8,128)(2,1)} %get-tuple-element.56), channel_id=1, source_target_pairs={{0,16},{1,17},{2,18},{3,19},{4,20},{5,21},{6,22},{7,23},{8,24},{9,... | collective-permute-start | bytes 393224 | tf_op jit(solution)/shard_map/ppermute | solution.py:20
  14.5 12.1 %collective-permute-start.23 = (bf16[2,64,1024]{2,1,0:T(8,128)(2,1)S(1)}, bf16[2,64,1024]{2,1,0:T(8,128)(2,1)S(1)}, u32[]{:S(2)}, u32[]{:S(2)}) collective-permute-start(bf16[2,64,1024]{2,1,0:T(8,128)(2,1)S(1)} %pad_maximum_fusion.8), channel_id=1, source_target_pairs={{0,8},{1,9},{2,10},{3,11},{4,12},{5,13},{6,14},{7,15},{8,0},{9,1},... | collective-permute-start | bytes 786440 | tf_op jit(solution)/shard_map/ppermute | solution.py:20
  18.2 6.8 %collective-permute-start.25 = (bf16[1,64,1024]{2,1,0:T(8,128)(2,1)S(1)}, bf16[1,64,1024]{2,1,0:T(8,128)(2,1)S(1)}, u32[]{:S(2)}, u32[]{:S(2)}) collective-permute-start(bf16[1,64,1024]{2,1,0:T(8,128)(2,1)S(1)} %maximum_bitcast_fusion.2), channel_id=1, source_target_pairs={{0,24},{1,25},{2,26},{3,27},{4,28},{5,29},{6,30},{7,31},{8,16},{9,... | collective-permute-start | bytes 393224 | tf_op jit(solution)/shard_map/ppermute | solution.py:20
  19.1 17.8 %collective-permute-start.2 = (bf16[320,128]{1,0:T(8,128)(2,1)}, bf16[320,128]{1,0:T(8,128)(2,1)S(1)}, u32[]{:S(2)}, u32[]{:S(2)}) collective-permute-start(bf16[320,128]{1,0:T(8,128)(2,1)} %get-tuple-element.41), channel_id=1, source_target_pairs={{0,3},{1,2},{2,1},{3,0},{4,7},{5,6},{6,5},{7,4},{8,11},{9,10},{10,... | collective-permute-start | bytes 245768 | tf_op jit(solution)/shard_map/ppermute | solution.py:20
  25.0 9.6 %collective-permute-start.1 = (bf16[320,128]{1,0:T(8,128)(2,1)S(1)}, bf16[320,128]{1,0:T(8,128)(2,1)S(1)}, u32[]{:S(2)}, u32[]{:S(2)}) collective-permute-start(bf16[320,128]{1,0:T(8,128)(2,1)S(1)} %get-tuple-element.42.refs_0_), channel_id=1, source_target_pairs={{0,2},{1,3},{2,0},{3,1},{4,6},{5,7},{6,4},{7,5},{8,10},{9,11},{10,... | collective-permute-start | bytes 245768 | tf_op jit(solution)/shard_map/ppermute | solution.py:20
  26.6 21.1 %collective-permute-start.7 = (bf16[320,2560]{1,0:T(8,128)(2,1)S(1)}, bf16[320,2560]{1,0:T(8,128)(2,1)}, u32[]{:S(2)}, u32[]{:S(2)}) collective-permute-start(bf16[320,2560]{1,0:T(8,128)(2,1)S(1)} %copy-done), channel_id=1, source_target_pairs={{0,1},{1,0},{2,3},{3,2},{4,5},{5,4},{6,7},{7,6},{8,9},{9,8},{10,11... | collective-permute-start | bytes 4915208 | tf_op jit(solution)/shard_map/ppermute | solution.py:20
  26.8 4.3 %collective-permute-start.26 = (bf16[5,64,1024]{2,1,0:T(8,128)(2,1)S(1)}, bf16[5,64,1024]{2,1,0:T(8,128)(2,1)S(1)}, u32[]{:S(2)}, u32[]{:S(2)}) collective-permute-start(bf16[5,64,1024]{2,1,0:T(8,128)(2,1)S(1)} %pad_maximum_fusion.1), channel_id=1, source_target_pairs={{0,1},{1,0},{2,3},{3,2},{4,5},{5,4},{6,7},{7,6},{8,9},{9,8},{10,11... | collective-permute-start | bytes 1966088 | tf_op jit(solution)/shard_map/ppermute | solution.py:20
  31.0 7.3 %collective-permute-start.3 = (bf16[320,128]{1,0:T(8,128)(2,1)S(1)}, bf16[320,128]{1,0:T(8,128)(2,1)S(1)}, u32[]{:S(2)}, u32[]{:S(2)}) collective-permute-start(bf16[320,128]{1,0:T(8,128)(2,1)S(1)} %get-tuple-element.42.refs_0_), channel_id=1, source_target_pairs={{0,4},{1,5},{2,6},{3,7},{4,0},{5,1},{6,2},{7,3},{8,12},{9,13},{10,... | collective-permute-start | bytes 245768 | tf_op jit(solution)/shard_map/ppermute | solution.py:20
  34.5 11.1 %collective-permute-start.4 = (bf16[320,128]{1,0:T(8,128)(2,1)}, bf16[320,128]{1,0:T(8,128)(2,1)S(1)}, u32[]{:S(2)}, u32[]{:S(2)}) collective-permute-start(bf16[320,128]{1,0:T(8,128)(2,1)} %get-tuple-element.41), channel_id=1, source_target_pairs={{0,5},{1,4},{2,7},{3,6},{4,1},{5,0},{6,3},{7,2},{8,13},{9,12},{10,... | collective-permute-start | bytes 245768 | tf_op jit(solution)/shard_map/ppermute | solution.py:20
  34.6 11.8 %collective-permute-start.5 = (bf16[320,128]{1,0:T(8,128)(2,1)S(1)}, bf16[320,128]{1,0:T(8,128)(2,1)S(1)}, u32[]{:S(2)}, u32[]{:S(2)}) collective-permute-start(bf16[320,128]{1,0:T(8,128)(2,1)S(1)} %get-tuple-element.42.refs_0_), channel_id=1, source_target_pairs={{0,6},{1,7},{2,4},{3,5},{4,2},{5,3},{6,0},{7,1},{8,14},{9,15},{10,... | collective-permute-start | bytes 245768 | tf_op jit(solution)/shard_map/ppermute | solution.py:20
  36.9 9.5 %collective-permute-start.6 = (bf16[320,128]{1,0:T(8,128)(2,1)}, bf16[320,128]{1,0:T(8,128)(2,1)S(1)}, u32[]{:S(2)}, u32[]{:S(2)}) collective-permute-start(bf16[320,128]{1,0:T(8,128)(2,1)} %get-tuple-element.41), channel_id=1, source_target_pairs={{0,7},{1,6},{2,5},{3,4},{4,3},{5,2},{6,1},{7,0},{8,15},{9,14},{10,... | collective-permute-start | bytes 245768 | tf_op jit(solution)/shard_map/ppermute | solution.py:20
  38.4 32.5 %collective-permute-start.17 = (bf16[128,2560]{1,0:T(8,128)(2,1)}, bf16[128,2560]{1,0:T(8,128)(2,1)}, u32[]{:S(2)}, u32[]{:S(2)}) collective-permute-start(bf16[128,2560]{1,0:T(8,128)(2,1)} %param.9), channel_id=1, source_target_pairs={{0,1},{1,0},{2,3},{3,2},{4,5},{5,4},{6,7},{7,6},{8,9},{9,8},{10,11... | collective-permute-start | bytes 1966088 | tf_op jit(solution)/shard_map/ppermute | solution.py:20
  45.6 32.7 %collective-permute-start.11 = (bf16[128,128]{1,0:T(8,128)(2,1)}, bf16[128,128]{1,0:T(8,128)(2,1)}, u32[]{:S(2)}, u32[]{:S(2)}) collective-permute-start(bf16[128,128]{1,0:T(8,128)(2,1)} %fusion.22), channel_id=1, source_target_pairs={{0,8},{1,9},{2,10},{3,11},{4,12},{5,13},{6,14},{7,15},{8,0},{9,1},... | collective-permute-start | bytes 98312 | tf_op jit(solution)/shard_map/ppermute | solution.py:20
  52.2 9.2 %collective-permute-start.14 = (bf16[640,128]{1,0:T(8,128)(2,1)}, bf16[640,128]{1,0:T(8,128)(2,1)S(1)}, u32[]{:S(2)}, u32[]{:S(2)}) collective-permute-start(bf16[640,128]{1,0:T(8,128)(2,1)} %get-tuple-element.7), channel_id=1, source_target_pairs={{0,6},{1,7},{2,4},{3,5},{4,2},{5,3},{6,0},{7,1},{8,14},{9,15},{10,... | collective-permute-start | bytes 491528 | tf_op jit(solution)/shard_map/ppermute | solution.py:20
  53.7 17.0 %collective-permute-start.15 = (bf16[640,128]{1,0:T(8,128)(2,1)}, bf16[640,128]{1,0:T(8,128)(2,1)S(1)}, u32[]{:S(2)}, u32[]{:S(2)}) collective-permute-start(bf16[640,128]{1,0:T(8,128)(2,1)} %get-tuple-element.7), channel_id=1, source_target_pairs={{0,4},{1,5},{2,6},{3,7},{4,0},{5,1},{6,2},{7,3},{8,12},{9,13},{10,... | collective-permute-start | bytes 491528 | tf_op jit(solution)/shard_map/ppermute | solution.py:20
  57.8 13.0 %collective-permute-start.16 = (bf16[640,128]{1,0:T(8,128)(2,1)}, bf16[640,128]{1,0:T(8,128)(2,1)S(1)}, u32[]{:S(2)}, u32[]{:S(2)}) collective-permute-start(bf16[640,128]{1,0:T(8,128)(2,1)} %get-tuple-element.7), channel_id=1, source_target_pairs={{0,2},{1,3},{2,0},{3,1},{4,6},{5,7},{6,4},{7,5},{8,10},{9,11},{10,... | collective-permute-start | bytes 491528 | tf_op jit(solution)/shard_map/ppermute | solution.py:20
  73.8 4.3 %collective-permute-start.18 = (bf16[2,2,64,128]{3,2,1,0:T(8,128)(2,1)S(1)}, bf16[2,2,64,128]{3,2,1,0:T(8,128)(2,1)S(1)}, u32[]{:S(2)}, u32[]{:S(2)}) collective-permute-start(bf16[2,2,64,128]{3,2,1,0:T(8,128)(2,1)S(1)} %get-tuple-element.46), channel_id=1, source_target_pairs={{0,8},{1,9},{2,10},{3,11},{4,12},{5,13},{6,14},{7,15},{8,0},{9,1},... | collective-permute-start | bytes 196616 | tf_op jit(solution)/shard_map/ppermute | solution.py:20
  79.2 4.6 %collective-permute-start.19 = (bf16[2,128,128]{2,1,0:T(8,128)(2,1)S(1)}, bf16[2,128,128]{2,1,0:T(8,128)(2,1)S(1)}, u32[]{:S(2)}, u32[]{:S(2)}) collective-permute-start(bf16[2,128,128]{2,1,0:T(8,128)(2,1)S(1)} %pad_maximum_fusion.12), channel_id=1, source_target_pairs={{0,2},{1,3},{2,0},{3,1},{4,6},{5,7},{6,4},{7,5},{8,10},{9,11},{10,... | collective-permute-start | bytes 196616 | tf_op jit(solution)/shard_map/ppermute | solution.py:20
  79.3 5.6 %collective-permute-start.20 = (bf16[2,128,128]{2,1,0:T(8,128)(2,1)S(1)}, bf16[2,128,128]{2,1,0:T(8,128)(2,1)S(1)}, u32[]{:S(2)}, u32[]{:S(2)}) collective-permute-start(bf16[2,128,128]{2,1,0:T(8,128)(2,1)S(1)} %pad_maximum_fusion.12), channel_id=1, source_target_pairs={{0,4},{1,5},{2,6},{3,7},{4,0},{5,1},{6,2},{7,3},{8,12},{9,13},{10,... | collective-permute-start | bytes 196616 | tf_op jit(solution)/shard_map/ppermute | solution.py:20
  82.1 6.1 %collective-permute-start.21 = (bf16[2,128,128]{2,1,0:T(8,128)(2,1)S(1)}, bf16[2,128,128]{2,1,0:T(8,128)(2,1)S(1)}, u32[]{:S(2)}, u32[]{:S(2)}) collective-permute-start(bf16[2,128,128]{2,1,0:T(8,128)(2,1)S(1)} %pad_maximum_fusion.12), channel_id=1, source_target_pairs={{0,6},{1,7},{2,4},{3,5},{4,2},{5,3},{6,0},{7,1},{8,14},{9,15},{10,... | collective-permute-start | bytes 196616 | tf_op jit(solution)/shard_map/ppermute | solution.py:20
  88.7 5.5 %collective-permute-start.28 = (bf16[2,128,128]{2,1,0:T(8,128)(2,1)S(1)}, bf16[2,128,128]{2,1,0:T(8,128)(2,1)S(1)}, u32[]{:S(2)}, u32[]{:S(2)}) collective-permute-start(bf16[2,128,128]{2,1,0:T(8,128)(2,1)S(1)} %pad_maximum_fusion.13), channel_id=1, source_target_pairs={{0,2},{1,3},{2,0},{3,1},{4,6},{5,7},{6,4},{7,5},{8,10},{9,11},{10,... | collective-permute-start | bytes 196616 | tf_op jit(solution)/shard_map/ppermute | solution.py:20
  88.8 5.5 %collective-permute-start.29 = (bf16[2,128,128]{2,1,0:T(8,128)(2,1)S(1)}, bf16[2,128,128]{2,1,0:T(8,128)(2,1)S(1)}, u32[]{:S(2)}, u32[]{:S(2)}) collective-permute-start(bf16[2,128,128]{2,1,0:T(8,128)(2,1)S(1)} %pad_maximum_fusion.13), channel_id=1, source_target_pairs={{0,4},{1,5},{2,6},{3,7},{4,0},{5,1},{6,2},{7,3},{8,12},{9,13},{10,... | collective-permute-start | bytes 196616 | tf_op jit(solution)/shard_map/ppermute | solution.py:20
  90.9 6.1 %collective-permute-start.30 = (bf16[2,128,128]{2,1,0:T(8,128)(2,1)S(1)}, bf16[2,128,128]{2,1,0:T(8,128)(2,1)S(1)}, u32[]{:S(2)}, u32[]{:S(2)}) collective-permute-start(bf16[2,128,128]{2,1,0:T(8,128)(2,1)S(1)} %pad_maximum_fusion.13), channel_id=1, source_target_pairs={{0,6},{1,7},{2,4},{3,5},{4,2},{5,3},{6,0},{7,1},{8,14},{9,15},{10,... | collective-permute-start | bytes 196616 | tf_op jit(solution)/shard_map/ppermute | solution.py:20
  97.5 4.5 %collective-permute-start.31 = (bf16[2,128,128]{2,1,0:T(8,128)(2,1)S(1)}, bf16[2,128,128]{2,1,0:T(8,128)(2,1)S(1)}, u32[]{:S(2)}, u32[]{:S(2)}) collective-permute-start(bf16[2,128,128]{2,1,0:T(8,128)(2,1)S(1)} %pad_maximum_fusion.14), channel_id=1, source_target_pairs={{0,2},{1,3},{2,0},{3,1},{4,6},{5,7},{6,4},{7,5},{8,10},{9,11},{10,... | collective-permute-start | bytes 196616 | tf_op jit(solution)/shard_map/ppermute | solution.py:20
  97.6 5.8 %collective-permute-start.32 = (bf16[2,128,128]{2,1,0:T(8,128)(2,1)S(1)}, bf16[2,128,128]{2,1,0:T(8,128)(2,1)S(1)}, u32[]{:S(2)}, u32[]{:S(2)}) collective-permute-start(bf16[2,128,128]{2,1,0:T(8,128)(2,1)S(1)} %pad_maximum_fusion.14), channel_id=1, source_target_pairs={{0,4},{1,5},{2,6},{3,7},{4,0},{5,1},{6,2},{7,3},{8,12},{9,13},{10,... | collective-permute-start | bytes 196616 | tf_op jit(solution)/shard_map/ppermute | solution.py:20
  101.1 6.1 %collective-permute-start.33 = (bf16[2,128,128]{2,1,0:T(8,128)(2,1)S(1)}, bf16[2,128,128]{2,1,0:T(8,128)(2,1)S(1)}, u32[]{:S(2)}, u32[]{:S(2)}) collective-permute-start(bf16[2,128,128]{2,1,0:T(8,128)(2,1)S(1)} %pad_maximum_fusion.14), channel_id=1, source_target_pairs={{0,6},{1,7},{2,4},{3,5},{4,2},{5,3},{6,0},{7,1},{8,14},{9,15},{10,... | collective-permute-start | bytes 196616 | tf_op jit(solution)/shard_map/ppermute | solution.py:20
  110.0 4.8 %collective-permute-start.36 = (bf16[128,128]{1,0:T(8,128)(2,1)S(1)}, bf16[128,128]{1,0:T(8,128)(2,1)S(1)}, u32[]{:S(2)}, u32[]{:S(2)}) collective-permute-start(bf16[128,128]{1,0:T(8,128)(2,1)S(1)} %get-tuple-element.44), channel_id=1, source_target_pairs={{0,24},{1,25},{2,26},{3,27},{4,28},{5,29},{6,30},{7,31},{8,16},{9,... | collective-permute-start | bytes 98312 | tf_op jit(solution)/shard_map/ppermute | solution.py:20
  111.2 4.4 %collective-permute-start.22 = (bf16[64,128]{1,0:T(8,128)(2,1)S(1)}, bf16[64,128]{1,0:T(8,128)(2,1)S(1)}, u32[]{:S(2)}, u32[]{:S(2)}) collective-permute-start(bf16[64,128]{1,0:T(8,128)(2,1)S(1)} %constant_dynamic-slice_fusion.8), channel_id=1, source_target_pairs={{0,1},{1,0},{2,3},{3,2},{4,5},{5,4},{6,7},{7,6},{8,9},{9,8},{10,11... | collective-permute-start | bytes 49160 | tf_op jit(solution)/shard_map/ppermute | solution.py:20
  (34 other events, 243.0 us)
where the time goes:
time: 117 us
  waiting for transfers between devices  46.9 us (40%)
  starting transfers between devices  41.3 us (35%)
  other arithmetic  11.7 us (10%)
  local copies, waits for them, and re-layouts  6.79 us (6%)
  Pallas kernels  4.51 us (4%)
  matrix products  4 us (3%)
  between operations  1.55 us (1%)
    ppermute x38, waiting for transfers between devices, exchange(): return lax.ppermute(value, ('leaf', 'blk'), pairs)  46.9 us
    ppermute x38, starting transfers between devices, exchange(): return lax.ppermute(value, ('leaf', 'blk'), pairs)  41.3 us
    pallas_call x1, Pallas kernels, leaf_solve(): pl.pallas_call(body, in_specs=[pl.BlockSpec(memory_space=pl.ANY)] * (coun...  4.51 us
    select_n x6, other arithmetic, in_order(): first = jnp.where(core == 0, mine, other)  4.22 us
    dot_general x6, matrix products, product(): return jnp.dot(matrix, vectors, preferred_element_type=jnp.float32)  4 us
    dynamic_slice x2, local copies, waits for them, and re-layouts, columns_of(): return lax.dynamic_slice_in_dim(value, which * half, half, value.ndim - 1)  2.98 us
  transfers between devices with their start and end apart: 38, of which 19 were waited for; matrix products, arithmetic and copies ran while one was open for 14% of the time, Pallas kernels for 4%

commit v1 on v0

--- a/solution.py
+++ b/solution.py
@@ -26,6 +26,10 @@
 
 def leaf_solve(pieces, near, far):
     count = len(pieces)
+
+    def keep_in(space, value):
+        return pltpu.with_memory_space_constraint(value, space)
+
     rows, half = pieces[0].shape
     dtype = pieces[0].dtype
 
@@ -36,27 +40,20 @@
         rhs, near_vmem, far_vmem, sems = refs[count + 5 :]
         b = lax.axis_index("blk")
         core = b % 2
-        copies = []
+        copies = [
+            pltpu.make_async_copy(source, target, sems.at[i])
+            for i, (source, target) in enumerate(((near_ref, near_vmem), (far_ref, far_vmem)))
+        ]
+        for copy in copies:
+            copy.start()
         for mask in range(count):
             where = pl.multiple_of((b ^ mask) * rows, 16)
-            copies.append(
-                pltpu.make_async_copy(
-                    piece_refs[mask], rhs.at[pl.ds(where, rows)], sems.at[mask]
-                )
-            )
-        near_copy = pltpu.make_async_copy(near_ref, near_vmem, sems.at[count])
-        far_copy = pltpu.make_async_copy(far_ref, far_vmem, sems.at[count + 1])
-        for copy in copies:
-            copy.start()
-        near_copy.start()
-        far_copy.start()
-        for copy in copies:
-            copy.wait()
-        near_copy.wait()
+            rhs[pl.ds(where, rows)] = piece_refs[mask][...]
+        copies[0].wait()
         mine = jnp.dot(near_vmem[...], rhs[...], preferred_element_type=jnp.float32).astype(dtype)
         mine_ref[...] = mine
         all_ref[pl.ds(pl.multiple_of(core * rows, 16), rows)] = mine
-        far_copy.wait()
+        copies[1].wait()
         other = jnp.dot(far_vmem[...], rhs[...], preferred_element_type=jnp.float32).astype(dtype)
         other_ref[...] = other
         all_ref[pl.ds(pl.multiple_of((1 - core) * rows, 16), rows)] = other
@@ -64,24 +61,24 @@
     vmem = pl.BlockSpec(memory_space=pltpu.VMEM)
     return pl.pallas_call(
         body,
-        in_specs=[pl.BlockSpec(memory_space=pl.ANY)] * (count + 2),
+        in_specs=[vmem] * count + [pl.BlockSpec(memory_space=pltpu.HBM)] * 2,
         out_specs=[vmem] * 3,
         out_shape=[
-            jax.ShapeDtypeStruct((2 * rows, half), dtype),
-            jax.ShapeDtypeStruct((rows, half), dtype),
-            jax.ShapeDtypeStruct((rows, half), dtype),
+            pltpu.VMEM((2 * rows, half), dtype),
+            pltpu.VMEM((rows, half), dtype),
+            pltpu.VMEM((rows, half), dtype),
         ],
         scratch_shapes=[
             pltpu.VMEM((count * rows, half), dtype),
             pltpu.VMEM(near.shape, dtype),
             pltpu.VMEM(far.shape, dtype),
-            pltpu.SemaphoreType.DMA((count + 2,)),
+            pltpu.SemaphoreType.DMA((2,)),
         ],
         cost_estimate=pl.CostEstimate(
             flops=4 * rows * count * rows * half, bytes_accessed=2 * near.size * 2, transcendentals=0
         ),
         name="leaf_solve",
-    )(*pieces, near, far)
+    )(*[keep_in(pltpu.VMEM, value) for value in pieces], near, keep_in(pltpu.HBM, far))
 
 
 def on_device(leaf_rhs, leaf_inverse, leaf_lower, sep_rhs, sep_inverse, sep_lower, slot_map):
@@ -115,14 +112,11 @@
     for mask in range(1, blks):
         arrived.append(exchange(own_half if mask % 2 == 0 else other_half, 0, mask))
     inverse_other = exchange(leaf_inverse, 0, 1)
+    slot_other = exchange(slot_map, 0, 1)
+    sep_rhs_other = exchange(sep_rhs, 0, 1)
     lower_other = exchange(leaf_lower, 0, 1)
-    slot_other = exchange(slot_map, 0, 1)
-    sep_rhs_other = exchange(columns_of(sep_rhs, 1 - core), 0, 1)
     sep_lower_other = exchange(sep_lower, 0, 1)
-    sep_inverse_other = exchange(sep_inverse, 0, 1)
-
-    slots = in_order(slot_map, slot_other, 1)
-    seps = in_order(columns_of(sep_rhs, core), sep_rhs_other, 1)
+    inverse_rows = [sep_inverse] + [exchange(sep_inverse, a, 0) for a in range(1, leaves)]
 
     s_all, s_mine, s_other = leaf_solve(arrived, leaf_inverse, inverse_other)
     got = [(m, exchange(s_all, 0, m)) for m in range(blks - 2, 0, -2)]
@@ -130,45 +124,45 @@
     for m, value in got:
         s_full = put(s_full, value, z ^ (m // 2))
 
-    inv_chip = in_order(sep_inverse, sep_inverse_other)
-    low_chip = in_order(sep_lower, sep_lower_other)
-
-    top_mask = 2 ** (levels - 1)
-    top_offset = base_width * (2**levels - 2)
-    top = sep_inverse[:, top_offset:]
-
-    def leaf_columns(leaf_index):
-        near = lax.dynamic_slice_in_dim(top, leaf_index * base_width, base_width, 1)
-        far = lax.dynamic_slice_in_dim(top, (leaf_index ^ top_mask) * base_width, base_width, 1)
-        return jnp.concatenate([near, far], axis=1)
-
+    inverse_others = [exchange(value, 0, 1) for value in inverse_rows]
+    slots = in_order(slot_map, slot_other, 1)
+    seps = in_order(columns_of(sep_rhs, core), columns_of(sep_rhs_other, core), 1)
     paired = levels > 1
-    blocks = [leaf_columns(k)[None]]
-    for a in range(1, leaves):
-        block = leaf_columns(k ^ a)[None]
-        if a == 1 and paired:
-            block = jnp.concatenate([sep_inverse[None, :, : 2 * base_width], block])
-        blocks.append(exchange(block, a, 0))
-    mine = jnp.concatenate(blocks)
-    other = exchange(mine, 0, 1)
     if paired:
         their_slots = exchange(slots[0], 1, 0)
         their_sep = exchange(seps[0], 1, 0)
-        inv_theirs = in_order(mine[1], other[1])
-        mine = jnp.concatenate([mine[:1], mine[2:]])
-        other = jnp.concatenate([other[:1], other[2:]])
-    first = jnp.where(core == 0, mine, other)
-    second = jnp.where(core == 0, other, mine)
-    top_rows = jnp.stack([first, second], axis=1).reshape(-1, 2 * base_width)
+
+    top_mask = 2 ** (levels - 1)
+    top_offset = base_width * (2**levels - 2)
+    low_chip = in_order(sep_lower, sep_lower_other)
+    inv_chip = in_order(sep_inverse[:, :top_offset], inverse_others[0][:, :top_offset])
+    if paired:
+        inv_theirs = in_order(
+            inverse_rows[1][:, : 2 * base_width], inverse_others[1][:, : 2 * base_width]
+        )
+
+    def leaf_columns(value):
+        near = lax.dynamic_slice_in_dim(value, top_offset + k * base_width, base_width, 1)
+        far = lax.dynamic_slice_in_dim(
+            value, top_offset + (k ^ top_mask) * base_width, base_width, 1
+        )
+        return jnp.concatenate([near, far], axis=1)
+
+    top_rows = jnp.concatenate(
+        [
+            in_order(leaf_columns(mine), leaf_columns(other))
+            for mine, other in zip(inverse_rows, inverse_others)
+        ]
+    )
 
     update = -in_order(product(leaf_lower, s_full), product(lower_other, s_full))
     leaf_back = exchange(s_other, 0, 1)
     leaf_solution = in_order(s_mine, leaf_back, 1)
 
     def gather_z(piece):
-        pieces = [piece] + [exchange(piece, 0, m) for m in range(2, blks, 2)]
+        pieces = [piece] + [exchange(piece, 0, m) for m in range(blks - 2, 0, -2)]
         result = jnp.zeros((chips,) + piece.shape, piece.dtype)
-        for m, value in enumerate(pieces):
+        for m, value in zip([0] + list(range(chips - 1, 0, -1)), pieces):
             result = lax.dynamic_update_slice_in_dim(result, value[None], z ^ m, 0)
         return result
 

time: 117 us -> 117 us (level)
  waiting for transfers between devices: 46.9 us -> 57.4 us
  other arithmetic: 11.7 us -> 8.07 us
  local copies, waits for them, and re-layouts: 6.79 us -> 3.17 us
    ppermute x38 -> x40, waiting for transfers between devices: 46.9 us -> 57.4 us  [exchange(): return lax.ppermute(value, ('leaf', 'blk'), pairs)]
    select_n x6, other arithmetic: 4.22 us -> 2.58 us  [in_order(): first = jnp.where(core == 0, mine, other)]
    unnamed x56 -> x26, local copies, waits for them, and re-layouts: 1.34 us -> 0.06 us
    dynamic_slice x2 -> x1, local copies, waits for them, and re-layouts: 2.98 us -> 1.71 us  [columns_of(): return lax.dynamic_slice_in_dim(value, which * half, half, value.ndim - 1)]
    ppermute x38 -> x40, starting transfers between devices: 41.3 us -> 40.7 us  [exchange(): return lax.ppermute(value, ('leaf', 'blk'), pairs)]
  transfers between devices with their start and end apart: 38 -> 40, of which waited for: 19 -> 23; matrix products, arithmetic and copies ran while one was open for 14% -> 8% of each run, Pallas kernels for 4% -> 3%
where the time goes in v1:
time: 117 us
  waiting for transfers between devices  57.4 us (49%)
  starting transfers between devices  40.7 us (35%)
  other arithmetic  8.07 us (7%)
  Pallas kernels  3.44 us (3%)
  local copies, waits for them, and re-layouts  3.17 us (3%)
  matrix products  2.89 us (2%)
  between operations  1.32 us (1%)
    ppermute x40, waiting for transfers between devices, exchange(): return lax.ppermute(value, ('leaf', 'blk'), pairs)  57.4 us
    ppermute x40, starting transfers between devices, exchange(): return lax.ppermute(value, ('leaf', 'blk'), pairs)  40.7 us
    pallas_call x1, Pallas kernels, leaf_solve(): pl.pallas_call(body, in_specs=[vmem] * count + [pl.BlockSpec(memory_space...  3.44 us
    dot_general x6, matrix products, product(): return jnp.dot(matrix, vectors, preferred_element_type=jnp.float32)  2.89 us
    select_n x6, other arithmetic, in_order(): first = jnp.where(core == 0, mine, other)  2.58 us
  transfers between devices with their start and end apart: 40, of which 23 were waited for; matrix products, arithmetic and copies ran while one was open for 8% of the time, Pallas kernels for 3%

profile of v1, /device:TPU:0, one launch (start us, length us, event | category | flops | bytes accessed | tf_op | source)
XLA Modules:
  0.0 117.0 jit_solution(16990416758166709964)
XLA Ops:
  0.7 1.7 %constant_dynamic-slice_fusion.18 = (bf16[320,128]{1,0:T(8,128)(2,1)}, bf16[320,128]{1,0:T(8,128)(2,1)S(1)}) fusion(bf16[320,256]{1,0:T(8,128)(2,1)} %param.7, s32[]{:T(128)S(6)} %select_n.275, s32[]{:T(128)S(6)} %select_n.274), kind=kLoop, calls=%fused_computation.125 | loop fusion | bytes 327688 | tf_op jit(solution)/shard_map/dynamic_slice | solution.py:99
  2.9 2.7 %collective-permute-start.2 = (bf16[320,128]{1,0:T(8,128)(2,1)}, bf16[320,128]{1,0:T(8,128)(2,1)S(1)}, u32[]{:S(2)}, u32[]{:S(2)}) collective-permute-start(bf16[320,128]{1,0:T(8,128)(2,1)} %get-tuple-element.47), channel_id=1, source_target_pairs={{0,3},{1,2},{2,1},{3,0},{4,7},{5,6},{6,5},{7,4},{8,11},{9,10},{10,... | collective-permute-start | bytes 245768 | tf_op jit(solution)/shard_map/ppermute | solution.py:20
  7.7 1.6 %collective-permute-start.13 = (s32[2,2]{1,0:T(2,128)S(1)}, s32[2,2]{1,0:T(2,128)S(1)}, u32[]{:S(2)}, u32[]{:S(2)}) collective-permute-start(s32[2,2]{1,0:T(2,128)S(1)} %get-tuple-element.22), channel_id=1, source_target_pairs={{0,8},{1,9},{2,10},{3,11},{4,12},{5,13},{6,14},{7,15},{8,0},{9,1},... | collective-permute-start | bytes 56 | tf_op jit(solution)/shard_map/ppermute | solution.py:20
  9.8 1.5 %collective-permute-done.13 = s32[2,2]{1,0:T(2,128)S(1)} collective-permute-done((s32[2,2]{1,0:T(2,128)S(1)}, s32[2,2]{1,0:T(2,128)S(1)}, u32[]{:S(2)}, u32[]{:S(2)}) %collective-permute-start.13) | collective-permute-done | bytes 48 | tf_op jit(solution)/shard_map/ppermute | solution.py:20
  11.9 1.5 %collective-permute-start.23 = (bf16[64,3072]{1,0:T(8,128)(2,1)}, bf16[64,3072]{1,0:T(8,128)(2,1)S(1)}, u32[]{:S(2)}, u32[]{:S(2)}) collective-permute-start(bf16[64,3072]{1,0:T(8,128)(2,1)} %param.11), channel_id=1, source_target_pairs={{0,8},{1,9},{2,10},{3,11},{4,12},{5,13},{6,14},{7,15},{8,0},{9,1},... | collective-permute-start | bytes 1179656 | tf_op jit(solution)/shard_map/ppermute | solution.py:20
  14.8 1.5 %collective-permute-start.25 = (bf16[64,3072]{1,0:T(8,128)(2,1)}, bf16[64,3072]{1,0:T(8,128)(2,1)S(1)}, u32[]{:S(2)}, u32[]{:S(2)}) collective-permute-start(bf16[64,3072]{1,0:T(8,128)(2,1)} %param.11), channel_id=1, source_target_pairs={{0,16},{1,17},{2,18},{3,19},{4,20},{5,21},{6,22},{7,23},{8,24},{9,... | collective-permute-start | bytes 1179656 | tf_op jit(solution)/shard_map/ppermute | solution.py:20
  16.3 1.8 %broadcast_select_fusion.1 = (bf16[128,1024]{1,0:T(8,128)(2,1)}, bf16[128,1024]{1,0:T(8,128)(2,1)}) fusion(bf16[128,1024]{1,0:T(8,128)(2,1)} %param.12, bf16[128,1024]{1,0:T(8,128)(2,1)S(1)} %collective-permute-done.29, pred[]{:T(512)S(6)} %eq.94), kind=kLoop, calls=%fused_computation.13 | loop fusion | flops 262144 | bytes 1048577 | tf_op jit(solution)/shard_map/jit(_where)/select_n | solution.py:102
  18.8 5.4 %collective-permute-done.23 = bf16[64,3072]{1,0:T(8,128)(2,1)S(1)} collective-permute-done((bf16[64,3072]{1,0:T(8,128)(2,1)}, bf16[64,3072]{1,0:T(8,128)(2,1)S(1)}, u32[]{:S(2)}, u32[]{:S(2)}) %collective-permute-start.23) | collective-permute-done | bytes 393248 | tf_op jit(solution)/shard_map/ppermute | solution.py:20
  24.2 10.6 %collective-permute-done.25 = bf16[64,3072]{1,0:T(8,128)(2,1)S(1)} collective-permute-done((bf16[64,3072]{1,0:T(8,128)(2,1)}, bf16[64,3072]{1,0:T(8,128)(2,1)S(1)}, u32[]{:S(2)}, u32[]{:S(2)}) %collective-permute-start.25) | collective-permute-done | bytes 393248 | tf_op jit(solution)/shard_map/ppermute | solution.py:20
  38.2 2.6 %collective-permute-start.3 = (bf16[320,128]{1,0:T(8,128)(2,1)S(1)}, bf16[320,128]{1,0:T(8,128)(2,1)S(1)}, u32[]{:S(2)}, u32[]{:S(2)}) collective-permute-start(bf16[320,128]{1,0:T(8,128)(2,1)S(1)} %get-tuple-element.48.refs_0_), channel_id=1, source_target_pairs={{0,4},{1,5},{2,6},{3,7},{4,0},{5,1},{6,2},{7,3},{8,12},{9,13},{10,... | collective-permute-start | bytes 245768 | tf_op jit(solution)/shard_map/ppermute | solution.py:20
  41.5 2.5 %collective-permute-start.5 = (bf16[320,128]{1,0:T(8,128)(2,1)S(1)}, bf16[320,128]{1,0:T(8,128)(2,1)S(1)}, u32[]{:S(2)}, u32[]{:S(2)}) collective-permute-start(bf16[320,128]{1,0:T(8,128)(2,1)S(1)} %get-tuple-element.48.refs_0_), channel_id=1, source_target_pairs={{0,6},{1,7},{2,4},{3,5},{4,2},{5,3},{6,0},{7,1},{8,14},{9,15},{10,... | collective-permute-start | bytes 245768 | tf_op jit(solution)/shard_map/ppermute | solution.py:20
  45.6 6.8 %collective-permute-done.4.refs_5_ = bf16[320,128]{1,0:T(8,128)(2,1)S(1)} collective-permute-done((bf16[320,128]{1,0:T(8,128)(2,1)}, bf16[320,128]{1,0:T(8,128)(2,1)S(1)}, u32[]{:S(2)}, u32[]{:S(2)}) %collective-permute-start.4) | collective-permute-done | bytes 81952 | tf_op jit(solution)/shard_map/ppermute | solution.py:20
  52.9 3.4 %leaf_solve.1 = (bf16[640,128]{1,0:T(8,128)(2,1)S(1)}, bf16[320,128]{1,0:T(8,128)(2,1)S(1)}, bf16[320,128]{1,0:T(8,128)(2,1)S(1)}) custom-call(bf16[320,128]{1,0:T(8,128)(2,1)S(1)} %get-tuple-element.48.refs_0_, bf16[320,128]{1,0:T(8,128)(2,1)S(1)} %collective-permute-done.refs_1_, bf16[320,128]{1,0:T(8,128)(2,1)S(1)} %collective-permute-done.1.refs_2_, ...), custom_call_target="tpu_custom_call" | custom-call | flops 419430400 | bytes 3276800 | tf_op jit(solution)/shard_map/leaf_solve/pallas_call | solution.py:62
  56.3 2.0 %collective-permute-start.14 = (bf16[640,128]{1,0:T(8,128)(2,1)S(1)}, bf16[640,128]{1,0:T(8,128)(2,1)S(1)}, u32[]{:S(2)}, u32[]{:S(2)}) collective-permute-start(bf16[640,128]{1,0:T(8,128)(2,1)S(1)} %get-tuple-element.7), channel_id=1, source_target_pairs={{0,6},{1,7},{2,4},{3,5},{4,2},{5,3},{6,0},{7,1},{8,14},{9,15},{10,... | collective-permute-start | bytes 491528 | tf_op jit(solution)/shard_map/ppermute | solution.py:20
  58.4 3.0 %collective-permute-start.15 = (bf16[640,128]{1,0:T(8,128)(2,1)S(1)}, bf16[640,128]{1,0:T(8,128)(2,1)S(1)}, u32[]{:S(2)}, u32[]{:S(2)}) collective-permute-start(bf16[640,128]{1,0:T(8,128)(2,1)S(1)} %get-tuple-element.7), channel_id=1, source_target_pairs={{0,4},{1,5},{2,6},{3,7},{4,0},{5,1},{6,2},{7,3},{8,12},{9,13},{10,... | collective-permute-start | bytes 491528 | tf_op jit(solution)/shard_map/ppermute | solution.py:20
  62.7 1.6 %collective-permute-done.14 = bf16[640,128]{1,0:T(8,128)(2,1)S(1)} collective-permute-done((bf16[640,128]{1,0:T(8,128)(2,1)S(1)}, bf16[640,128]{1,0:T(8,128)(2,1)S(1)}, u32[]{:S(2)}, u32[]{:S(2)}) %collective-permute-start.14) | collective-permute-done | bytes 163872 | tf_op jit(solution)/shard_map/ppermute | solution.py:20
  64.2 10.4 %collective-permute-done.15 = bf16[640,128]{1,0:T(8,128)(2,1)S(1)} collective-permute-done((bf16[640,128]{1,0:T(8,128)(2,1)S(1)}, bf16[640,128]{1,0:T(8,128)(2,1)S(1)}, u32[]{:S(2)}, u32[]{:S(2)}) %collective-permute-start.15) | collective-permute-done | bytes 163872 | tf_op jit(solution)/shard_map/ppermute | solution.py:20
  76.5 1.6 %collective-permute-start.18 = (bf16[2,2,64,128]{3,2,1,0:T(8,128)(2,1)S(1)}, bf16[2,2,64,128]{3,2,1,0:T(8,128)(2,1)S(1)}, u32[]{:S(2)}, u32[]{:S(2)}) collective-permute-start(bf16[2,2,64,128]{3,2,1,0:T(8,128)(2,1)S(1)} %get-tuple-element.54), channel_id=1, source_target_pairs={{0,8},{1,9},{2,10},{3,11},{4,12},{5,13},{6,14},{7,15},{8,0},{9,1},... | collective-permute-start | bytes 196616 | tf_op jit(solution)/shard_map/ppermute | solution.py:20
  78.2 2.7 %collective-permute-done.18 = bf16[2,2,64,128]{3,2,1,0:T(8,128)(2,1)S(1)} collective-permute-done((bf16[2,2,64,128]{3,2,1,0:T(8,128)(2,1)S(1)}, bf16[2,2,64,128]{3,2,1,0:T(8,128)(2,1)S(1)}, u32[]{:S(2)}, u32[]{:S(2)}) %collective-permute-start.18) | collective-permute-done | bytes 65568 | tf_op jit(solution)/shard_map/ppermute | solution.py:20
  81.9 3.2 %collective-permute-start.19 = (bf16[2,128,128]{2,1,0:T(8,128)(2,1)S(1)}, bf16[2,128,128]{2,1,0:T(8,128)(2,1)S(1)}, u32[]{:S(2)}, u32[]{:S(2)}) collective-permute-start(bf16[2,128,128]{2,1,0:T(8,128)(2,1)S(1)} %pad_maximum_fusion.10), channel_id=1, source_target_pairs={{0,6},{1,7},{2,4},{3,5},{4,2},{5,3},{6,0},{7,1},{8,14},{9,15},{10,... | collective-permute-start | bytes 196616 | tf_op jit(solution)/shard_map/ppermute | solution.py:20
  86.5 1.6 %collective-permute-done.19 = bf16[2,128,128]{2,1,0:T(8,128)(2,1)S(1)} collective-permute-done((bf16[2,128,128]{2,1,0:T(8,128)(2,1)S(1)}, bf16[2,128,128]{2,1,0:T(8,128)(2,1)S(1)}, u32[]{:S(2)}, u32[]{:S(2)}) %collective-permute-start.19) | collective-permute-done | bytes 65568 | tf_op jit(solution)/shard_map/ppermute | solution.py:20
  88.1 2.1 %collective-permute-done.20 = bf16[2,128,128]{2,1,0:T(8,128)(2,1)S(1)} collective-permute-done((bf16[2,128,128]{2,1,0:T(8,128)(2,1)S(1)}, bf16[2,128,128]{2,1,0:T(8,128)(2,1)S(1)}, u32[]{:S(2)}, u32[]{:S(2)}) %collective-permute-start.20) | collective-permute-done | bytes 65568 | tf_op jit(solution)/shard_map/ppermute | solution.py:20
  91.1 1.8 %collective-permute-start.30 = (bf16[2,128,128]{2,1,0:T(8,128)(2,1)S(1)}, bf16[2,128,128]{2,1,0:T(8,128)(2,1)S(1)}, u32[]{:S(2)}, u32[]{:S(2)}) collective-permute-start(bf16[2,128,128]{2,1,0:T(8,128)(2,1)S(1)} %pad_maximum_fusion.11), channel_id=1, source_target_pairs={{0,6},{1,7},{2,4},{3,5},{4,2},{5,3},{6,0},{7,1},{8,14},{9,15},{10,... | collective-permute-start | bytes 196616 | tf_op jit(solution)/shard_map/ppermute | solution.py:20
  92.9 2.6 %collective-permute-start.32 = (bf16[2,128,128]{2,1,0:T(8,128)(2,1)S(1)}, bf16[2,128,128]{2,1,0:T(8,128)(2,1)S(1)}, u32[]{:S(2)}, u32[]{:S(2)}) collective-permute-start(bf16[2,128,128]{2,1,0:T(8,128)(2,1)S(1)} %pad_maximum_fusion.11), channel_id=1, source_target_pairs={{0,2},{1,3},{2,0},{3,1},{4,6},{5,7},{6,4},{7,5},{8,10},{9,11},{10,... | collective-permute-start | bytes 196616 | tf_op jit(solution)/shard_map/ppermute | solution.py:20
  95.6 1.6 %collective-permute-done.30 = bf16[2,128,128]{2,1,0:T(8,128)(2,1)S(1)} collective-permute-done((bf16[2,128,128]{2,1,0:T(8,128)(2,1)S(1)}, bf16[2,128,128]{2,1,0:T(8,128)(2,1)S(1)}, u32[]{:S(2)}, u32[]{:S(2)}) %collective-permute-start.30) | collective-permute-done | bytes 65568 | tf_op jit(solution)/shard_map/ppermute | solution.py:20
  97.2 1.4 %collective-permute-done.31 = bf16[2,128,128]{2,1,0:T(8,128)(2,1)S(1)} collective-permute-done((bf16[2,128,128]{2,1,0:T(8,128)(2,1)S(1)}, bf16[2,128,128]{2,1,0:T(8,128)(2,1)S(1)}, u32[]{:S(2)}, u32[]{:S(2)}) %collective-permute-start.31) | collective-permute-done | bytes 65568 | tf_op jit(solution)/shard_map/ppermute | solution.py:20
  99.2 2.4 %collective-permute-start.33 = (bf16[2,128,128]{2,1,0:T(8,128)(2,1)S(1)}, bf16[2,128,128]{2,1,0:T(8,128)(2,1)S(1)}, u32[]{:S(2)}, u32[]{:S(2)}) collective-permute-start(bf16[2,128,128]{2,1,0:T(8,128)(2,1)S(1)} %pad_maximum_fusion.12), channel_id=1, source_target_pairs={{0,6},{1,7},{2,4},{3,5},{4,2},{5,3},{6,0},{7,1},{8,14},{9,15},{10,... | collective-permute-start | bytes 196616 | tf_op jit(solution)/shard_map/ppermute | solution.py:20
  101.8 1.8 %collective-permute-start.35 = (bf16[2,128,128]{2,1,0:T(8,128)(2,1)S(1)}, bf16[2,128,128]{2,1,0:T(8,128)(2,1)S(1)}, u32[]{:S(2)}, u32[]{:S(2)}) collective-permute-start(bf16[2,128,128]{2,1,0:T(8,128)(2,1)S(1)} %pad_maximum_fusion.12), channel_id=1, source_target_pairs={{0,2},{1,3},{2,0},{3,1},{4,6},{5,7},{6,4},{7,5},{8,10},{9,11},{10,... | collective-permute-start | bytes 196616 | tf_op jit(solution)/shard_map/ppermute | solution.py:20
  103.7 1.6 %collective-permute-done.33 = bf16[2,128,128]{2,1,0:T(8,128)(2,1)S(1)} collective-permute-done((bf16[2,128,128]{2,1,0:T(8,128)(2,1)S(1)}, bf16[2,128,128]{2,1,0:T(8,128)(2,1)S(1)}, u32[]{:S(2)}, u32[]{:S(2)}) %collective-permute-start.33) | collective-permute-done | bytes 65568 | tf_op jit(solution)/shard_map/ppermute | solution.py:20
  105.3 1.4 %collective-permute-done.34 = bf16[2,128,128]{2,1,0:T(8,128)(2,1)S(1)} collective-permute-done((bf16[2,128,128]{2,1,0:T(8,128)(2,1)S(1)}, bf16[2,128,128]{2,1,0:T(8,128)(2,1)S(1)}, u32[]{:S(2)}, u32[]{:S(2)}) %collective-permute-start.34) | collective-permute-done | bytes 65568 | tf_op jit(solution)/shard_map/ppermute | solution.py:20
  108.7 1.5 %collective-permute-start.37 = (bf16[128,128]{1,0:T(8,128)(2,1)S(1)}, bf16[128,128]{1,0:T(8,128)(2,1)S(1)}, u32[]{:S(2)}, u32[]{:S(2)}) collective-permute-start(bf16[128,128]{1,0:T(8,128)(2,1)S(1)} %get-tuple-element.51), channel_id=1, source_target_pairs={{0,16},{1,17},{2,18},{3,19},{4,20},{5,21},{6,22},{7,23},{8,24},{9,... | collective-permute-start | bytes 98312 | tf_op jit(solution)/shard_map/ppermute | solution.py:20
  112.6 2.4 %collective-permute-done.38 = bf16[128,128]{1,0:T(8,128)(2,1)S(1)} collective-permute-done((bf16[128,128]{1,0:T(8,128)(2,1)S(1)}, bf16[128,128]{1,0:T(8,128)(2,1)S(1)}, u32[]{:S(2)}, u32[]{:S(2)}) %collective-permute-start.38) | collective-permute-done | bytes 32800 | tf_op jit(solution)/shard_map/ppermute | solution.py:20
  (151 shorter events, 25.3 us)
Async XLA Ops:
  2.4 38.4 %collective-permute-start = (bf16[320,128]{1,0:T(8,128)(2,1)}, bf16[320,128]{1,0:T(8,128)(2,1)S(1)}, u32[]{:S(2)}, u32[]{:S(2)}) collective-permute-start(bf16[320,128]{1,0:T(8,128)(2,1)} %get-tuple-element.47), channel_id=1, source_target_pairs={{0,1},{1,0},{2,3},{3,2},{4,5},{5,4},{6,7},{7,6},{8,9},{9,8},{10,11... | collective-permute-start | bytes 245768 | tf_op jit(solution)/shard_map/ppermute | solution.py:20
  2.9 41.1 %collective-permute-start.2 = (bf16[320,128]{1,0:T(8,128)(2,1)}, bf16[320,128]{1,0:T(8,128)(2,1)S(1)}, u32[]{:S(2)}, u32[]{:S(2)}) collective-permute-start(bf16[320,128]{1,0:T(8,128)(2,1)} %get-tuple-element.47), channel_id=1, source_target_pairs={{0,3},{1,2},{2,1},{3,0},{4,7},{5,6},{6,5},{7,4},{8,11},{9,10},{10,... | collective-permute-start | bytes 245768 | tf_op jit(solution)/shard_map/ppermute | solution.py:20
  5.6 6.4 %collective-permute-start.10 = (bf16[2,64,256]{2,1,0:T(8,128)(2,1)}, bf16[2,64,256]{2,1,0:T(8,128)(2,1)S(1)}, u32[]{:S(2)}, u32[]{:S(2)}) collective-permute-start(bf16[2,64,256]{2,1,0:T(8,128)(2,1)} %param.10), channel_id=1, source_target_pairs={{0,1},{1,0},{2,3},{3,2},{4,5},{5,4},{6,7},{7,6},{8,9},{9,8},{10,11... | collective-permute-start | bytes 196616 | tf_op jit(solution)/shard_map/ppermute | solution.py:20
  6.1 12.1 %collective-permute-start.9 = (bf16[64,3072]{1,0:T(8,128)(2,1)}, bf16[64,3072]{1,0:T(8,128)(2,1)S(1)}, u32[]{:S(2)}, u32[]{:S(2)}) collective-permute-start(bf16[64,3072]{1,0:T(8,128)(2,1)} %param.11), channel_id=1, source_target_pairs={{0,1},{1,0},{2,3},{3,2},{4,5},{5,4},{6,7},{7,6},{8,9},{9,8},{10,11... | collective-permute-start | bytes 1179656 | tf_op jit(solution)/shard_map/ppermute | solution.py:20
  11.9 12.2 %collective-permute-start.23 = (bf16[64,3072]{1,0:T(8,128)(2,1)}, bf16[64,3072]{1,0:T(8,128)(2,1)S(1)}, u32[]{:S(2)}, u32[]{:S(2)}) collective-permute-start(bf16[64,3072]{1,0:T(8,128)(2,1)} %param.11), channel_id=1, source_target_pairs={{0,8},{1,9},{2,10},{3,11},{4,12},{5,13},{6,14},{7,15},{8,0},{9,1},... | collective-permute-start | bytes 1179656 | tf_op jit(solution)/shard_map/ppermute | solution.py:20
  14.8 19.9 %collective-permute-start.25 = (bf16[64,3072]{1,0:T(8,128)(2,1)}, bf16[64,3072]{1,0:T(8,128)(2,1)S(1)}, u32[]{:S(2)}, u32[]{:S(2)}) collective-permute-start(bf16[64,3072]{1,0:T(8,128)(2,1)} %param.11), channel_id=1, source_target_pairs={{0,16},{1,17},{2,18},{3,19},{4,20},{5,21},{6,22},{7,23},{8,24},{9,... | collective-permute-start | bytes 1179656 | tf_op jit(solution)/shard_map/ppermute | solution.py:20
  18.2 16.6 %collective-permute-start.27 = (bf16[64,3072]{1,0:T(8,128)(2,1)S(1)}, bf16[64,3072]{1,0:T(8,128)(2,1)S(1)}, u32[]{:S(2)}, u32[]{:S(2)}) collective-permute-start(bf16[64,3072]{1,0:T(8,128)(2,1)S(1)} %copy-done.6), channel_id=1, source_target_pairs={{0,24},{1,25},{2,26},{3,27},{4,28},{5,29},{6,30},{7,31},{8,16},{9,... | collective-permute-start | bytes 1179656 | tf_op jit(solution)/shard_map/ppermute | solution.py:20
  24.1 28.7 %collective-permute-start.7 = (bf16[320,2560]{1,0:T(8,128)(2,1)S(1)}, bf16[320,2560]{1,0:T(8,128)(2,1)}, u32[]{:S(2)}, u32[]{:S(2)}) collective-permute-start(bf16[320,2560]{1,0:T(8,128)(2,1)S(1)} %copy-done), channel_id=1, source_target_pairs={{0,1},{1,0},{2,3},{3,2},{4,5},{5,4},{6,7},{7,6},{8,9},{9,8},{10,11... | collective-permute-start | bytes 4915208 | tf_op jit(solution)/shard_map/ppermute | solution.py:20
  37.0 4.5 %collective-permute-start.1 = (bf16[320,128]{1,0:T(8,128)(2,1)S(1)}, bf16[320,128]{1,0:T(8,128)(2,1)S(1)}, u32[]{:S(2)}, u32[]{:S(2)}) collective-permute-start(bf16[320,128]{1,0:T(8,128)(2,1)S(1)} %get-tuple-element.48.refs_0_), channel_id=1, source_target_pairs={{0,2},{1,3},{2,0},{3,1},{4,6},{5,7},{6,4},{7,5},{8,10},{9,11},{10,... | collective-permute-start | bytes 245768 | tf_op jit(solution)/shard_map/ppermute | solution.py:20
  38.2 6.4 %collective-permute-start.3 = (bf16[320,128]{1,0:T(8,128)(2,1)S(1)}, bf16[320,128]{1,0:T(8,128)(2,1)S(1)}, u32[]{:S(2)}, u32[]{:S(2)}) collective-permute-start(bf16[320,128]{1,0:T(8,128)(2,1)S(1)} %get-tuple-element.48.refs_0_), channel_id=1, source_target_pairs={{0,4},{1,5},{2,6},{3,7},{4,0},{5,1},{6,2},{7,3},{8,12},{9,13},{10,... | collective-permute-start | bytes 245768 | tf_op jit(solution)/shard_map/ppermute | solution.py:20
  40.8 11.5 %collective-permute-start.4 = (bf16[320,128]{1,0:T(8,128)(2,1)}, bf16[320,128]{1,0:T(8,128)(2,1)S(1)}, u32[]{:S(2)}, u32[]{:S(2)}) collective-permute-start(bf16[320,128]{1,0:T(8,128)(2,1)} %get-tuple-element.47), channel_id=1, source_target_pairs={{0,5},{1,4},{2,7},{3,6},{4,1},{5,0},{6,3},{7,2},{8,13},{9,12},{10,... | collective-permute-start | bytes 245768 | tf_op jit(solution)/shard_map/ppermute | solution.py:20
  41.5 11.4 %collective-permute-start.5 = (bf16[320,128]{1,0:T(8,128)(2,1)S(1)}, bf16[320,128]{1,0:T(8,128)(2,1)S(1)}, u32[]{:S(2)}, u32[]{:S(2)}) collective-permute-start(bf16[320,128]{1,0:T(8,128)(2,1)S(1)} %get-tuple-element.48.refs_0_), channel_id=1, source_target_pairs={{0,6},{1,7},{2,4},{3,5},{4,2},{5,3},{6,0},{7,1},{8,14},{9,15},{10,... | collective-permute-start | bytes 245768 | tf_op jit(solution)/shard_map/ppermute | solution.py:20
  44.0 8.9 %collective-permute-start.6 = (bf16[320,128]{1,0:T(8,128)(2,1)}, bf16[320,128]{1,0:T(8,128)(2,1)S(1)}, u32[]{:S(2)}, u32[]{:S(2)}) collective-permute-start(bf16[320,128]{1,0:T(8,128)(2,1)} %get-tuple-element.47), channel_id=1, source_target_pairs={{0,7},{1,6},{2,5},{3,4},{4,3},{5,2},{6,1},{7,0},{8,15},{9,14},{10,... | collective-permute-start | bytes 245768 | tf_op jit(solution)/shard_map/ppermute | solution.py:20
  44.6 30.2 %collective-permute-start.17 = (bf16[128,2560]{1,0:T(8,128)(2,1)S(1)}, bf16[128,2560]{1,0:T(8,128)(2,1)}, u32[]{:S(2)}, u32[]{:S(2)}) collective-permute-start(bf16[128,2560]{1,0:T(8,128)(2,1)S(1)} %copy-done.3), channel_id=1, source_target_pairs={{0,1},{1,0},{2,3},{3,2},{4,5},{5,4},{6,7},{7,6},{8,9},{9,8},{10,11... | collective-permute-start | bytes 1966088 | tf_op jit(solution)/shard_map/ppermute | solution.py:20
  52.3 28.7 %collective-permute-start.11 = (bf16[128,128]{1,0:T(8,128)(2,1)}, bf16[128,128]{1,0:T(8,128)(2,1)}, u32[]{:S(2)}, u32[]{:S(2)}) collective-permute-start(bf16[128,128]{1,0:T(8,128)(2,1)} %fusion.21), channel_id=1, source_target_pairs={{0,8},{1,9},{2,10},{3,11},{4,12},{5,13},{6,14},{7,15},{8,0},{9,1},... | collective-permute-start | bytes 98312 | tf_op jit(solution)/shard_map/ppermute | solution.py:20
  56.3 7.9 %collective-permute-start.14 = (bf16[640,128]{1,0:T(8,128)(2,1)S(1)}, bf16[640,128]{1,0:T(8,128)(2,1)S(1)}, u32[]{:S(2)}, u32[]{:S(2)}) collective-permute-start(bf16[640,128]{1,0:T(8,128)(2,1)S(1)} %get-tuple-element.7), channel_id=1, source_target_pairs={{0,6},{1,7},{2,4},{3,5},{4,2},{5,3},{6,0},{7,1},{8,14},{9,15},{10,... | collective-permute-start | bytes 491528 | tf_op jit(solution)/shard_map/ppermute | solution.py:20
  58.4 16.3 %collective-permute-start.15 = (bf16[640,128]{1,0:T(8,128)(2,1)S(1)}, bf16[640,128]{1,0:T(8,128)(2,1)S(1)}, u32[]{:S(2)}, u32[]{:S(2)}) collective-permute-start(bf16[640,128]{1,0:T(8,128)(2,1)S(1)} %get-tuple-element.7), channel_id=1, source_target_pairs={{0,4},{1,5},{2,6},{3,7},{4,0},{5,1},{6,2},{7,3},{8,12},{9,13},{10,... | collective-permute-start | bytes 491528 | tf_op jit(solution)/shard_map/ppermute | solution.py:20
  62.6 12.0 %collective-permute-start.16 = (bf16[640,128]{1,0:T(8,128)(2,1)S(1)}, bf16[640,128]{1,0:T(8,128)(2,1)S(1)}, u32[]{:S(2)}, u32[]{:S(2)}) collective-permute-start(bf16[640,128]{1,0:T(8,128)(2,1)S(1)} %get-tuple-element.7), channel_id=1, source_target_pairs={{0,2},{1,3},{2,0},{3,1},{4,6},{5,7},{6,4},{7,5},{8,10},{9,11},{10,... | collective-permute-start | bytes 491528 | tf_op jit(solution)/shard_map/ppermute | solution.py:20
  76.5 4.3 %collective-permute-start.18 = (bf16[2,2,64,128]{3,2,1,0:T(8,128)(2,1)S(1)}, bf16[2,2,64,128]{3,2,1,0:T(8,128)(2,1)S(1)}, u32[]{:S(2)}, u32[]{:S(2)}) collective-permute-start(bf16[2,2,64,128]{3,2,1,0:T(8,128)(2,1)S(1)} %get-tuple-element.54), channel_id=1, source_target_pairs={{0,8},{1,9},{2,10},{3,11},{4,12},{5,13},{6,14},{7,15},{8,0},{9,1},... | collective-permute-start | bytes 196616 | tf_op jit(solution)/shard_map/ppermute | solution.py:20
  81.9 6.2 %collective-permute-start.19 = (bf16[2,128,128]{2,1,0:T(8,128)(2,1)S(1)}, bf16[2,128,128]{2,1,0:T(8,128)(2,1)S(1)}, u32[]{:S(2)}, u32[]{:S(2)}) collective-permute-start(bf16[2,128,128]{2,1,0:T(8,128)(2,1)S(1)} %pad_maximum_fusion.10), channel_id=1, source_target_pairs={{0,6},{1,7},{2,4},{3,5},{4,2},{5,3},{6,0},{7,1},{8,14},{9,15},{10,... | collective-permute-start | bytes 196616 | tf_op jit(solution)/shard_map/ppermute | solution.py:20
  85.1 5.2 %collective-permute-start.20 = (bf16[2,128,128]{2,1,0:T(8,128)(2,1)S(1)}, bf16[2,128,128]{2,1,0:T(8,128)(2,1)S(1)}, u32[]{:S(2)}, u32[]{:S(2)}) collective-permute-start(bf16[2,128,128]{2,1,0:T(8,128)(2,1)S(1)} %pad_maximum_fusion.10), channel_id=1, source_target_pairs={{0,4},{1,5},{2,6},{3,7},{4,0},{5,1},{6,2},{7,3},{8,12},{9,13},{10,... | collective-permute-start | bytes 196616 | tf_op jit(solution)/shard_map/ppermute | solution.py:20
  85.1 5.5 %collective-permute-start.21 = (bf16[2,128,128]{2,1,0:T(8,128)(2,1)S(1)}, bf16[2,128,128]{2,1,0:T(8,128)(2,1)S(1)}, u32[]{:S(2)}, u32[]{:S(2)}) collective-permute-start(bf16[2,128,128]{2,1,0:T(8,128)(2,1)S(1)} %pad_maximum_fusion.10), channel_id=1, source_target_pairs={{0,2},{1,3},{2,0},{3,1},{4,6},{5,7},{6,4},{7,5},{8,10},{9,11},{10,... | collective-permute-start | bytes 196616 | tf_op jit(solution)/shard_map/ppermute | solution.py:20
  91.1 6.1 %collective-permute-start.30 = (bf16[2,128,128]{2,1,0:T(8,128)(2,1)S(1)}, bf16[2,128,128]{2,1,0:T(8,128)(2,1)S(1)}, u32[]{:S(2)}, u32[]{:S(2)}) collective-permute-start(bf16[2,128,128]{2,1,0:T(8,128)(2,1)S(1)} %pad_maximum_fusion.11), channel_id=1, source_target_pairs={{0,6},{1,7},{2,4},{3,5},{4,2},{5,3},{6,0},{7,1},{8,14},{9,15},{10,... | collective-permute-start | bytes 196616 | tf_op jit(solution)/shard_map/ppermute | solution.py:20
  92.9 5.8 %collective-permute-start.31 = (bf16[2,128,128]{2,1,0:T(8,128)(2,1)S(1)}, bf16[2,128,128]{2,1,0:T(8,128)(2,1)S(1)}, u32[]{:S(2)}, u32[]{:S(2)}) collective-permute-start(bf16[2,128,128]{2,1,0:T(8,128)(2,1)S(1)} %pad_maximum_fusion.11), channel_id=1, source_target_pairs={{0,4},{1,5},{2,6},{3,7},{4,0},{5,1},{6,2},{7,3},{8,12},{9,13},{10,... | collective-permute-start | bytes 196616 | tf_op jit(solution)/shard_map/ppermute | solution.py:20
  92.9 5.8 %collective-permute-start.32 = (bf16[2,128,128]{2,1,0:T(8,128)(2,1)S(1)}, bf16[2,128,128]{2,1,0:T(8,128)(2,1)S(1)}, u32[]{:S(2)}, u32[]{:S(2)}) collective-permute-start(bf16[2,128,128]{2,1,0:T(8,128)(2,1)S(1)} %pad_maximum_fusion.11), channel_id=1, source_target_pairs={{0,2},{1,3},{2,0},{3,1},{4,6},{5,7},{6,4},{7,5},{8,10},{9,11},{10,... | collective-permute-start | bytes 196616 | tf_op jit(solution)/shard_map/ppermute | solution.py:20
  99.2 6.1 %collective-permute-start.33 = (bf16[2,128,128]{2,1,0:T(8,128)(2,1)S(1)}, bf16[2,128,128]{2,1,0:T(8,128)(2,1)S(1)}, u32[]{:S(2)}, u32[]{:S(2)}) collective-permute-start(bf16[2,128,128]{2,1,0:T(8,128)(2,1)S(1)} %pad_maximum_fusion.12), channel_id=1, source_target_pairs={{0,6},{1,7},{2,4},{3,5},{4,2},{5,3},{6,0},{7,1},{8,14},{9,15},{10,... | collective-permute-start | bytes 196616 | tf_op jit(solution)/shard_map/ppermute | solution.py:20
  101.5 5.2 %collective-permute-start.34 = (bf16[2,128,128]{2,1,0:T(8,128)(2,1)S(1)}, bf16[2,128,128]{2,1,0:T(8,128)(2,1)S(1)}, u32[]{:S(2)}, u32[]{:S(2)}) collective-permute-start(bf16[2,128,128]{2,1,0:T(8,128)(2,1)S(1)} %pad_maximum_fusion.12), channel_id=1, source_target_pairs={{0,4},{1,5},{2,6},{3,7},{4,0},{5,1},{6,2},{7,3},{8,12},{9,13},{10,... | collective-permute-start | bytes 196616 | tf_op jit(solution)/shard_map/ppermute | solution.py:20
  101.8 5.0 %collective-permute-start.35 = (bf16[2,128,128]{2,1,0:T(8,128)(2,1)S(1)}, bf16[2,128,128]{2,1,0:T(8,128)(2,1)S(1)}, u32[]{:S(2)}, u32[]{:S(2)}) collective-permute-start(bf16[2,128,128]{2,1,0:T(8,128)(2,1)S(1)} %pad_maximum_fusion.12), channel_id=1, source_target_pairs={{0,2},{1,3},{2,0},{3,1},{4,6},{5,7},{6,4},{7,5},{8,10},{9,11},{10,... | collective-permute-start | bytes 196616 | tf_op jit(solution)/shard_map/ppermute | solution.py:20
  107.3 4.0 %collective-permute-start.36 = (bf16[128,128]{1,0:T(8,128)(2,1)S(1)}, bf16[128,128]{1,0:T(8,128)(2,1)S(1)}, u32[]{:S(2)}, u32[]{:S(2)}) collective-permute-start(bf16[128,128]{1,0:T(8,128)(2,1)S(1)} %get-tuple-element.49), channel_id=1, source_target_pairs={{0,8},{1,9},{2,10},{3,11},{4,12},{5,13},{6,14},{7,15},{8,0},{9,1},... | collective-permute-start | bytes 98312 | tf_op jit(solution)/shard_map/ppermute | solution.py:20
  108.7 3.9 %collective-permute-start.37 = (bf16[128,128]{1,0:T(8,128)(2,1)S(1)}, bf16[128,128]{1,0:T(8,128)(2,1)S(1)}, u32[]{:S(2)}, u32[]{:S(2)}) collective-permute-start(bf16[128,128]{1,0:T(8,128)(2,1)S(1)} %get-tuple-element.51), channel_id=1, source_target_pairs={{0,16},{1,17},{2,18},{3,19},{4,20},{5,21},{6,22},{7,23},{8,24},{9,... | collective-permute-start | bytes 98312 | tf_op jit(solution)/shard_map/ppermute | solution.py:20
  110.2 4.8 %collective-permute-start.38 = (bf16[128,128]{1,0:T(8,128)(2,1)S(1)}, bf16[128,128]{1,0:T(8,128)(2,1)S(1)}, u32[]{:S(2)}, u32[]{:S(2)}) collective-permute-start(bf16[128,128]{1,0:T(8,128)(2,1)S(1)} %get-tuple-element.50), channel_id=1, source_target_pairs={{0,24},{1,25},{2,26},{3,27},{4,28},{5,29},{6,30},{7,31},{8,16},{9,... | collective-permute-start | bytes 98312 | tf_op jit(solution)/shard_map/ppermute | solution.py:20
  110.9 5.0 %collective-permute-start.22 = (bf16[64,128]{1,0:T(8,128)(2,1)S(1)}, bf16[64,128]{1,0:T(8,128)(2,1)S(1)}, u32[]{:S(2)}, u32[]{:S(2)}) collective-permute-start(bf16[64,128]{1,0:T(8,128)(2,1)S(1)} %constant_dynamic-slice_fusion.17), channel_id=1, source_target_pairs={{0,1},{1,0},{2,3},{3,2},{4,5},{5,4},{6,7},{7,6},{8,9},{9,8},{10,11... | collective-permute-start | bytes 49160 | tf_op jit(solution)/shard_map/ppermute | solution.py:20
  (21 other events, 156.1 us)

commit v2 on v1

--- a/solution.py
+++ b/solution.py
@@ -24,61 +24,97 @@
     return jnp.dot(matrix, vectors, preferred_element_type=jnp.float32)
 
 
-def leaf_solve(pieces, near, far):
-    count = len(pieces)
-
-    def keep_in(space, value):
-        return pltpu.with_memory_space_constraint(value, space)
-
+def on_chip(value):
+    return pltpu.with_memory_space_constraint(value, pltpu.VMEM)
+
+
+def vmem_specs(count):
+    return [pl.BlockSpec(memory_space=pltpu.VMEM)] * count
+
+
+def leaf_partial(pieces, near, far):
+    masks = sorted(pieces)
+    count = len(masks)
     rows, half = pieces[0].shape
-    dtype = pieces[0].dtype
+    total = near.shape[1]
+    dtype = near.dtype
 
     def body(*refs):
         piece_refs = refs[:count]
-        near_ref, far_ref = refs[count : count + 2]
-        all_ref, mine_ref, other_ref = refs[count + 2 : count + 5]
-        rhs, near_vmem, far_vmem, sems = refs[count + 5 :]
+        near_ref, far_ref, sum_ref, rest_ref, rhs, near_vmem, far_vmem, sems = refs[count:]
         b = lax.axis_index("blk")
-        core = b % 2
         copies = [
             pltpu.make_async_copy(source, target, sems.at[i])
             for i, (source, target) in enumerate(((near_ref, near_vmem), (far_ref, far_vmem)))
         ]
         for copy in copies:
             copy.start()
-        for mask in range(count):
+        missing = pl.multiple_of((b // 2 ^ 1) * 2 * rows, 128)
+        rhs[pl.ds(missing, 2 * rows)] = jnp.zeros((2 * rows, half), dtype)
+        for mask, piece_ref in zip(masks, piece_refs):
             where = pl.multiple_of((b ^ mask) * rows, 16)
-            rhs[pl.ds(where, rows)] = piece_refs[mask][...]
-        copies[0].wait()
-        mine = jnp.dot(near_vmem[...], rhs[...], preferred_element_type=jnp.float32).astype(dtype)
-        mine_ref[...] = mine
-        all_ref[pl.ds(pl.multiple_of(core * rows, 16), rows)] = mine
-        copies[1].wait()
-        other = jnp.dot(far_vmem[...], rhs[...], preferred_element_type=jnp.float32).astype(dtype)
-        other_ref[...] = other
-        all_ref[pl.ds(pl.multiple_of((1 - core) * rows, 16), rows)] = other
-
-    vmem = pl.BlockSpec(memory_space=pltpu.VMEM)
+            rhs[pl.ds(where, rows)] = piece_ref[...]
+        for i, matrix in enumerate((near_vmem, far_vmem)):
+            copies[i].wait()
+            sum_ref[i] = jnp.dot(matrix[...], rhs[...], preferred_element_type=jnp.float32)
+            rest_ref[i] = matrix[:, pl.ds(missing, 2 * rows)]
+
     return pl.pallas_call(
         body,
-        in_specs=[vmem] * count + [pl.BlockSpec(memory_space=pltpu.HBM)] * 2,
-        out_specs=[vmem] * 3,
+        in_specs=vmem_specs(count) + [pl.BlockSpec(memory_space=pltpu.HBM)] * 2,
+        out_specs=vmem_specs(2),
+        out_shape=[
+            pltpu.VMEM((2, rows, half), jnp.float32),
+            pltpu.VMEM((2, rows, 2 * rows), dtype),
+        ],
+        scratch_shapes=[
+            pltpu.VMEM((total, half), dtype),
+            pltpu.VMEM(near.shape, dtype),
+            pltpu.VMEM(far.shape, dtype),
+            pltpu.SemaphoreType.DMA((2,)),
+        ],
+        cost_estimate=pl.CostEstimate(
+            flops=4 * rows * total * half, bytes_accessed=4 * near.size, transcendentals=0
+        ),
+        name="leaf_partial",
+    )(
+        *[on_chip(pieces[mask]) for mask in masks],
+        near,
+        pltpu.with_memory_space_constraint(far, pltpu.HBM),
+    )
+
+
+def leaf_finish(same, cross, sums, rest):
+    rows, half = same.shape
+    dtype = same.dtype
+
+    def body(same_ref, cross_ref, sum_ref, rest_ref, all_ref, mine_ref, other_ref, rhs):
+        core = lax.axis_index("blk") % 2
+        low = pl.multiple_of(core * rows, 16)
+        high = pl.multiple_of((1 - core) * rows, 16)
+        rhs[pl.ds(low, rows)] = same_ref[...]
+        rhs[pl.ds(high, rows)] = cross_ref[...]
+        for i, (where, out_ref) in enumerate(((low, mine_ref), (high, other_ref))):
+            value = jnp.dot(rest_ref[i], rhs[...], preferred_element_type=jnp.float32)
+            value = (value + sum_ref[i]).astype(dtype)
+            out_ref[...] = value
+            all_ref[pl.ds(where, rows)] = value
+
+    return pl.pallas_call(
+        body,
+        in_specs=vmem_specs(4),
+        out_specs=vmem_specs(3),
         out_shape=[
             pltpu.VMEM((2 * rows, half), dtype),
             pltpu.VMEM((rows, half), dtype),
             pltpu.VMEM((rows, half), dtype),
         ],
-        scratch_shapes=[
-            pltpu.VMEM((count * rows, half), dtype),
-            pltpu.VMEM(near.shape, dtype),
-            pltpu.VMEM(far.shape, dtype),
-            pltpu.SemaphoreType.DMA((2,)),
-        ],
+        scratch_shapes=[pltpu.VMEM((2 * rows, half), dtype)],
         cost_estimate=pl.CostEstimate(
-            flops=4 * rows * count * rows * half, bytes_accessed=2 * near.size * 2, transcendentals=0
+            flops=8 * rows * rows * half, bytes_accessed=0, transcendentals=0
         ),
-        name="leaf_solve",
-    )(*[keep_in(pltpu.VMEM, value) for value in pieces], near, keep_in(pltpu.HBM, far))
+        name="leaf_finish",
+    )(on_chip(same), on_chip(cross), on_chip(sums), on_chip(rest))
 
 
 def on_device(leaf_rhs, leaf_inverse, leaf_lower, sep_rhs, sep_inverse, sep_lower, slot_map):
@@ -106,19 +142,37 @@
     def put(buffer, piece, index):
         return lax.dynamic_update_slice_in_dim(buffer, piece, index * piece.shape[0], 0)
 
+    top_mask = 2 ** (levels - 1)
+    top_offset = base_width * (2**levels - 2)
+    send_whole = leaves <= DIRECT_LIMIT // 2
+
+    def leaf_columns(value, leaf):
+        near = lax.dynamic_slice_in_dim(value, top_offset + leaf * base_width, base_width, 1)
+        far = lax.dynamic_slice_in_dim(
+            value, top_offset + (leaf ^ top_mask) * base_width, base_width, 1
+        )
+        return jnp.concatenate([near, far], axis=1)
+
     own_half = columns_of(leaf_rhs, core)
     other_half = columns_of(leaf_rhs, 1 - core)
-    arrived = [own_half]
-    for mask in range(1, blks):
-        arrived.append(exchange(own_half if mask % 2 == 0 else other_half, 0, mask))
+    arrived = {0: own_half}
+    for mask in list(range(blks - 1, 3, -1)) + [1, 3, 2]:
+        arrived[mask] = exchange(own_half if mask % 2 == 0 else other_half, 0, mask)
     inverse_other = exchange(leaf_inverse, 0, 1)
     slot_other = exchange(slot_map, 0, 1)
     sep_rhs_other = exchange(sep_rhs, 0, 1)
     lower_other = exchange(leaf_lower, 0, 1)
     sep_lower_other = exchange(sep_lower, 0, 1)
-    inverse_rows = [sep_inverse] + [exchange(sep_inverse, a, 0) for a in range(1, leaves)]
-
-    s_all, s_mine, s_other = leaf_solve(arrived, leaf_inverse, inverse_other)
+    inverse_rows = [sep_inverse]
+    for a in range(1, leaves):
+        value = sep_inverse
+        if not send_whole:
+            value = jnp.concatenate([value[:, : 2 * base_width], leaf_columns(value, k ^ a)], 1)
+        inverse_rows.append(exchange(value, a, 0))
+
+    same, cross = arrived.pop(2), arrived.pop(3)
+    sums, beside = leaf_partial(arrived, leaf_inverse, inverse_other)
+    s_all, s_mine, s_other = leaf_finish(same, cross, sums, beside)
     got = [(m, exchange(s_all, 0, m)) for m in range(blks - 2, 0, -2)]
     s_full = put(jnp.zeros((blks * rows, half), dtype), s_all, z)
     for m, value in got:
@@ -132,8 +186,6 @@
         their_slots = exchange(slots[0], 1, 0)
         their_sep = exchange(seps[0], 1, 0)
 
-    top_mask = 2 ** (levels - 1)
-    top_offset = base_width * (2**levels - 2)
     low_chip = in_order(sep_lower, sep_lower_other)
     inv_chip = in_order(sep_inverse[:, :top_offset], inverse_others[0][:, :top_offset])
     if paired:
@@ -141,17 +193,13 @@
             inverse_rows[1][:, : 2 * base_width], inverse_others[1][:, : 2 * base_width]
         )
 
-    def leaf_columns(value):
-        near = lax.dynamic_slice_in_dim(value, top_offset + k * base_width, base_width, 1)
-        far = lax.dynamic_slice_in_dim(
-            value, top_offset + (k ^ top_mask) * base_width, base_width, 1
-        )
-        return jnp.concatenate([near, far], axis=1)
+    def top_columns(a, value):
+        return leaf_columns(value, k) if a == 0 or send_whole else value[:, 2 * base_width :]
 
     top_rows = jnp.concatenate(
         [
-            in_order(leaf_columns(mine), leaf_columns(other))
-            for mine, other in zip(inverse_rows, inverse_others)
+            in_order(top_columns(a, mine), top_columns(a, other))
+            for a, (mine, other) in enumerate(zip(inverse_rows, inverse_others))
         ]
     )
 

time: 117 us -> 116 us (level)
  waiting for transfers between devices: 57.4 us -> 54.1 us
  other arithmetic: 8.07 us -> 10.5 us
  starting transfers between devices: 40.7 us -> 39.3 us
    ppermute x40, waiting for transfers between devices: 57.4 us -> 54.1 us  [exchange(): return lax.ppermute(value, ('leaf', 'blk'), pairs)]
    ppermute x40, starting transfers between devices: 40.7 us -> 39.3 us  [exchange(): return lax.ppermute(value, ('leaf', 'blk'), pairs)]
    select_n x6, other arithmetic: 2.58 us -> 3.92 us  [in_order(): first = jnp.where(core == 0, mine, other)]
    pallas_call x1 -> x2, Pallas kernels: 3.44 us -> 3.89 us  [the longest x1 3.49 us: leaf_partial(): pl.pallas_call(body, in_specs=vmem_specs(count) + [pl.BlockSpec(memory_sp...]
  transfers between devices with their start and end apart: 40 -> 40, of which waited for: 23 -> 21; matrix products, arithmetic and copies ran while one was open for 8% -> 10% of each run, Pallas kernels for 3% -> 3%
where the time goes in v2:
time: 116 us; the launch traced here: 115 us
  waiting for transfers between devices  54.1 us (47%)
  starting transfers between devices  39.3 us (34%)
  other arithmetic  10.5 us (9%)
  Pallas kernels  3.89 us (3%)
  local copies, waits for them, and re-layouts  3.21 us (3%)
  matrix products  2.91 us (3%)
  between operations  1.39 us (1%)
    ppermute x40, waiting for transfers between devices, exchange(): return lax.ppermute(value, ('leaf', 'blk'), pairs)  54.1 us
    ppermute x40, starting transfers between devices, exchange(): return lax.ppermute(value, ('leaf', 'blk'), pairs)  39.3 us
    select_n x6, other arithmetic, in_order(): first = jnp.where(core == 0, mine, other)  3.92 us
    pallas_call x1, Pallas kernels, leaf_partial(): pl.pallas_call(body, in_specs=vmem_specs(count) + [pl.BlockSpec(memory_sp...  3.49 us
    dot_general x6, matrix products, product(): return jnp.dot(matrix, vectors, preferred_element_type=jnp.float32)  2.91 us
    eq x4, other arithmetic, mix(): hit = (targets == t)[:, :, None, None]  2.34 us
  transfers between devices with their start and end apart: 40, of which 21 were waited for; matrix products, arithmetic and copies ran while one was open for 10% of the time, Pallas kernels for 3%

profile of v2, /device:TPU:0, one launch (start us, length us, event | category | flops | bytes accessed | tf_op | source)
XLA Modules:
  0.0 115.3 jit_solution(8695003335887727038)
XLA Ops:
  0.7 1.7 %constant_dynamic-slice_fusion.18 = (bf16[320,128]{1,0:T(8,128)(2,1)}, bf16[320,128]{1,0:T(8,128)(2,1)S(1)}) fusion(bf16[320,256]{1,0:T(8,128)(2,1)} %param.7, s32[]{:T(128)S(6)} %select_n.275, s32[]{:T(128)S(6)} %select_n.274), kind=kLoop, calls=%fused_computation.125 | loop fusion | bytes 327688 | tf_op jit(solution)/shard_map/dynamic_slice | solution.py:135
  2.9 3.7 %collective-permute-start.4 = (bf16[320,128]{1,0:T(8,128)(2,1)}, bf16[320,128]{1,0:T(8,128)(2,1)S(1)}, u32[]{:S(2)}, u32[]{:S(2)}) collective-permute-start(bf16[320,128]{1,0:T(8,128)(2,1)} %get-tuple-element.51), channel_id=1, source_target_pairs={{0,5},{1,4},{2,7},{3,6},{4,1},{5,0},{6,3},{7,2},{8,13},{9,12},{10,... | collective-permute-start | bytes 245768 | tf_op jit(solution)/shard_map/ppermute | solution.py:20
  9.3 1.5 %collective-permute-start.13 = (s32[2,2]{1,0:T(2,128)S(1)}, s32[2,2]{1,0:T(2,128)S(1)}, u32[]{:S(2)}, u32[]{:S(2)}) collective-permute-start(s32[2,2]{1,0:T(2,128)S(1)} %get-tuple-element.26), channel_id=1, source_target_pairs={{0,8},{1,9},{2,10},{3,11},{4,12},{5,13},{6,14},{7,15},{8,0},{9,1},... | collective-permute-start | bytes 56 | tf_op jit(solution)/shard_map/ppermute | solution.py:20
  13.5 1.5 %collective-permute-start.23 = (bf16[64,3072]{1,0:T(8,128)(2,1)}, bf16[64,3072]{1,0:T(8,128)(2,1)S(1)}, u32[]{:S(2)}, u32[]{:S(2)}) collective-permute-start(bf16[64,3072]{1,0:T(8,128)(2,1)} %param.11), channel_id=1, source_target_pairs={{0,8},{1,9},{2,10},{3,11},{4,12},{5,13},{6,14},{7,15},{8,0},{9,1},... | collective-permute-start | bytes 1179656 | tf_op jit(solution)/shard_map/ppermute | solution.py:20
  16.3 1.5 %collective-permute-start.25 = (bf16[64,3072]{1,0:T(8,128)(2,1)}, bf16[64,3072]{1,0:T(8,128)(2,1)S(1)}, u32[]{:S(2)}, u32[]{:S(2)}) collective-permute-start(bf16[64,3072]{1,0:T(8,128)(2,1)} %param.11), channel_id=1, source_target_pairs={{0,16},{1,17},{2,18},{3,19},{4,20},{5,21},{6,22},{7,23},{8,24},{9,... | collective-permute-start | bytes 1179656 | tf_op jit(solution)/shard_map/ppermute | solution.py:20
  17.9 1.8 %broadcast_select_fusion.1 = (bf16[128,1024]{1,0:T(8,128)(2,1)}, bf16[128,1024]{1,0:T(8,128)(2,1)}) fusion(bf16[128,1024]{1,0:T(8,128)(2,1)} %param.12, bf16[128,1024]{1,0:T(8,128)(2,1)S(1)} %collective-permute-done.29, pred[]{:T(512)S(6)} %eq.94), kind=kLoop, calls=%fused_computation.13 | loop fusion | flops 262144 | bytes 1048577 | tf_op jit(solution)/shard_map/jit(_where)/select_n | solution.py:138
  20.3 5.4 %collective-permute-done.23 = bf16[64,3072]{1,0:T(8,128)(2,1)S(1)} collective-permute-done((bf16[64,3072]{1,0:T(8,128)(2,1)}, bf16[64,3072]{1,0:T(8,128)(2,1)S(1)}, u32[]{:S(2)}, u32[]{:S(2)}) %collective-permute-start.23) | collective-permute-done | bytes 393248 | tf_op jit(solution)/shard_map/ppermute | solution.py:20
  25.7 10.6 %collective-permute-done.25 = bf16[64,3072]{1,0:T(8,128)(2,1)S(1)} collective-permute-done((bf16[64,3072]{1,0:T(8,128)(2,1)}, bf16[64,3072]{1,0:T(8,128)(2,1)S(1)}, u32[]{:S(2)}, u32[]{:S(2)}) %collective-permute-start.25) | collective-permute-done | bytes 393248 | tf_op jit(solution)/shard_map/ppermute | solution.py:20
  39.7 3.2 %collective-permute-start.5 = (bf16[320,128]{1,0:T(8,128)(2,1)S(1)}, bf16[320,128]{1,0:T(8,128)(2,1)S(1)}, u32[]{:S(2)}, u32[]{:S(2)}) collective-permute-start(bf16[320,128]{1,0:T(8,128)(2,1)S(1)} %get-tuple-element.52.refs_0_), channel_id=1, source_target_pairs={{0,6},{1,7},{2,4},{3,5},{4,2},{5,3},{6,0},{7,1},{8,14},{9,15},{10,... | collective-permute-start | bytes 245768 | tf_op jit(solution)/shard_map/ppermute | solution.py:20
  43.8 4.7 %collective-permute-done.3.refs_2_ = bf16[320,128]{1,0:T(8,128)(2,1)S(1)} collective-permute-done((bf16[320,128]{1,0:T(8,128)(2,1)S(1)}, bf16[320,128]{1,0:T(8,128)(2,1)S(1)}, u32[]{:S(2)}, u32[]{:S(2)}) %collective-permute-start.3) | collective-permute-done | bytes 81952 | tf_op jit(solution)/shard_map/ppermute | solution.py:20
  48.9 1.9 %collective-permute-start.17 = (bf16[128,2560]{1,0:T(8,128)(2,1)S(1)}, bf16[128,2560]{1,0:T(8,128)(2,1)}, u32[]{:S(2)}, u32[]{:S(2)}) collective-permute-start(bf16[128,2560]{1,0:T(8,128)(2,1)S(1)} %copy-done.3), channel_id=1, source_target_pairs={{0,1},{1,0},{2,3},{3,2},{4,5},{5,4},{6,7},{7,6},{8,9},{9,8},{10,11... | collective-permute-start | bytes 1966088 | tf_op jit(solution)/shard_map/ppermute | solution.py:20
  51.3 3.5 %leaf_partial.1 = (f32[2,320,128]{2,1,0:T(8,128)S(1)}, bf16[2,320,640]{2,1,0:T(8,128)(2,1)S(1)}) custom-call(bf16[320,128]{1,0:T(8,128)(2,1)S(1)} %get-tuple-element.52.refs_0_, bf16[320,128]{1,0:T(8,128)(2,1)S(1)} %collective-permute-done.2.refs_1_, bf16[320,128]{1,0:T(8,128)(2,1)S(1)} %collective-permute-done.3.refs_2_, ...), custom_call_target="tpu_custom_call" | custom-call | flops 419430400 | bytes 3276800 | tf_op jit(solution)/shard_map/leaf_partial/pallas_call | solution.py:62
  56.1 3.1 %collective-permute-start.15 = (bf16[640,128]{1,0:T(8,128)(2,1)S(1)}, bf16[640,128]{1,0:T(8,128)(2,1)S(1)}, u32[]{:S(2)}, u32[]{:S(2)}) collective-permute-start(bf16[640,128]{1,0:T(8,128)(2,1)S(1)} %get-tuple-element.11), channel_id=1, source_target_pairs={{0,4},{1,5},{2,6},{3,7},{4,0},{5,1},{6,2},{7,3},{8,12},{9,13},{10,... | collective-permute-start | bytes 491528 | tf_op jit(solution)/shard_map/ppermute | solution.py:20
  59.3 1.1 collective-permute-done.8
  61.0 3.3 %collective-permute-done.14 = bf16[640,128]{1,0:T(8,128)(2,1)S(1)} collective-permute-done((bf16[640,128]{1,0:T(8,128)(2,1)S(1)}, bf16[640,128]{1,0:T(8,128)(2,1)S(1)}, u32[]{:S(2)}, u32[]{:S(2)}) %collective-permute-start.14) | collective-permute-done | bytes 163872 | tf_op jit(solution)/shard_map/ppermute | solution.py:20
  64.3 9.8 %collective-permute-done.15 = bf16[640,128]{1,0:T(8,128)(2,1)S(1)} collective-permute-done((bf16[640,128]{1,0:T(8,128)(2,1)S(1)}, bf16[640,128]{1,0:T(8,128)(2,1)S(1)}, u32[]{:S(2)}, u32[]{:S(2)}) %collective-permute-start.15) | collective-permute-done | bytes 163872 | tf_op jit(solution)/shard_map/ppermute | solution.py:20
  74.3 1.4 %fusion.34 = f32[128,128]{0,1:T(8,128)S(1)} fusion(bf16[128,2560]{1,0:T(8,128)(2,1)} %collective-permute-done.17, bf16[2560,128]{1,0:T(8,128)(2,1)S(1)} %constant_dynamic-update-slice_fusion), kind=kOutput, calls=%fused_computation.150 | convolution fusion | flops 83886080 | bytes 1376256 | tf_op jit(solution)/shard_map/dot_general | solution.py:24
  76.1 1.0 collective-permute-start.18
  77.2 3.2 %collective-permute-done.18 = bf16[2,2,64,128]{3,2,1,0:T(8,128)(2,1)S(1)} collective-permute-done((bf16[2,2,64,128]{3,2,1,0:T(8,128)(2,1)S(1)}, bf16[2,2,64,128]{3,2,1,0:T(8,128)(2,1)S(1)}, u32[]{:S(2)}, u32[]{:S(2)}) %collective-permute-start.18) | collective-permute-done | bytes 65568 | tf_op jit(solution)/shard_map/ppermute | solution.py:20
  82.2 3.6 %collective-permute-start.21 = (bf16[2,128,128]{2,1,0:T(8,128)(2,1)S(1)}, bf16[2,128,128]{2,1,0:T(8,128)(2,1)S(1)}, u32[]{:S(2)}, u32[]{:S(2)}) collective-permute-start(bf16[2,128,128]{2,1,0:T(8,128)(2,1)S(1)} %pad_maximum_fusion.10), channel_id=1, source_target_pairs={{0,2},{1,3},{2,0},{3,1},{4,6},{5,7},{6,4},{7,5},{8,10},{9,11},{10,... | collective-permute-start | bytes 196616 | tf_op jit(solution)/shard_map/ppermute | solution.py:20
  86.0 1.8 %collective-permute-done.19 = bf16[2,128,128]{2,1,0:T(8,128)(2,1)S(1)} collective-permute-done((bf16[2,128,128]{2,1,0:T(8,128)(2,1)S(1)}, bf16[2,128,128]{2,1,0:T(8,128)(2,1)S(1)}, u32[]{:S(2)}, u32[]{:S(2)}) %collective-permute-start.19) | collective-permute-done | bytes 65568 | tf_op jit(solution)/shard_map/ppermute | solution.py:20
  89.3 2.0 %collective-permute-start.30 = (bf16[2,128,128]{2,1,0:T(8,128)(2,1)S(1)}, bf16[2,128,128]{2,1,0:T(8,128)(2,1)S(1)}, u32[]{:S(2)}, u32[]{:S(2)}) collective-permute-start(bf16[2,128,128]{2,1,0:T(8,128)(2,1)S(1)} %pad_maximum_fusion.11), channel_id=1, source_target_pairs={{0,6},{1,7},{2,4},{3,5},{4,2},{5,3},{6,0},{7,1},{8,14},{9,15},{10,... | collective-permute-start | bytes 196616 | tf_op jit(solution)/shard_map/ppermute | solution.py:20
  92.2 1.6 %collective-permute-start.32 = (bf16[2,128,128]{2,1,0:T(8,128)(2,1)S(1)}, bf16[2,128,128]{2,1,0:T(8,128)(2,1)S(1)}, u32[]{:S(2)}, u32[]{:S(2)}) collective-permute-start(bf16[2,128,128]{2,1,0:T(8,128)(2,1)S(1)} %pad_maximum_fusion.11), channel_id=1, source_target_pairs={{0,2},{1,3},{2,0},{3,1},{4,6},{5,7},{6,4},{7,5},{8,10},{9,11},{10,... | collective-permute-start | bytes 196616 | tf_op jit(solution)/shard_map/ppermute | solution.py:20
  93.9 2.4 %collective-permute-done.30 = bf16[2,128,128]{2,1,0:T(8,128)(2,1)S(1)} collective-permute-done((bf16[2,128,128]{2,1,0:T(8,128)(2,1)S(1)}, bf16[2,128,128]{2,1,0:T(8,128)(2,1)S(1)}, u32[]{:S(2)}, u32[]{:S(2)}) %collective-permute-start.30) | collective-permute-done | bytes 65568 | tf_op jit(solution)/shard_map/ppermute | solution.py:20
  96.2 1.2 %collective-permute-done.31 = bf16[2,128,128]{2,1,0:T(8,128)(2,1)S(1)} collective-permute-done((bf16[2,128,128]{2,1,0:T(8,128)(2,1)S(1)}, bf16[2,128,128]{2,1,0:T(8,128)(2,1)S(1)}, u32[]{:S(2)}, u32[]{:S(2)}) %collective-permute-start.31) | collective-permute-done | bytes 65568 | tf_op jit(solution)/shard_map/ppermute | solution.py:20
  97.9 1.6 %collective-permute-start.33 = (bf16[2,128,128]{2,1,0:T(8,128)(2,1)S(1)}, bf16[2,128,128]{2,1,0:T(8,128)(2,1)S(1)}, u32[]{:S(2)}, u32[]{:S(2)}) collective-permute-start(bf16[2,128,128]{2,1,0:T(8,128)(2,1)S(1)} %pad_maximum_fusion.12), channel_id=1, source_target_pairs={{0,6},{1,7},{2,4},{3,5},{4,2},{5,3},{6,0},{7,1},{8,14},{9,15},{10,... | collective-permute-start | bytes 196616 | tf_op jit(solution)/shard_map/ppermute | solution.py:20
  100.1 2.3 %collective-permute-start.35 = (bf16[2,128,128]{2,1,0:T(8,128)(2,1)S(1)}, bf16[2,128,128]{2,1,0:T(8,128)(2,1)S(1)}, u32[]{:S(2)}, u32[]{:S(2)}) collective-permute-start(bf16[2,128,128]{2,1,0:T(8,128)(2,1)S(1)} %pad_maximum_fusion.12), channel_id=1, source_target_pairs={{0,2},{1,3},{2,0},{3,1},{4,6},{5,7},{6,4},{7,5},{8,10},{9,11},{10,... | collective-permute-start | bytes 196616 | tf_op jit(solution)/shard_map/ppermute | solution.py:20
  102.4 1.6 %collective-permute-done.33 = bf16[2,128,128]{2,1,0:T(8,128)(2,1)S(1)} collective-permute-done((bf16[2,128,128]{2,1,0:T(8,128)(2,1)S(1)}, bf16[2,128,128]{2,1,0:T(8,128)(2,1)S(1)}, u32[]{:S(2)}, u32[]{:S(2)}) %collective-permute-start.33) | collective-permute-done | bytes 65568 | tf_op jit(solution)/shard_map/ppermute | solution.py:20
  104.1 1.4 %collective-permute-done.34 = bf16[2,128,128]{2,1,0:T(8,128)(2,1)S(1)} collective-permute-done((bf16[2,128,128]{2,1,0:T(8,128)(2,1)S(1)}, bf16[2,128,128]{2,1,0:T(8,128)(2,1)S(1)}, u32[]{:S(2)}, u32[]{:S(2)}) %collective-permute-start.34) | collective-permute-done | bytes 65568 | tf_op jit(solution)/shard_map/ppermute | solution.py:20
  106.0 1.0 collective-permute-start.36
  107.0 1.5 %collective-permute-start.37 = (bf16[128,128]{1,0:T(8,128)(2,1)S(1)}, bf16[128,128]{1,0:T(8,128)(2,1)S(1)}, u32[]{:S(2)}, u32[]{:S(2)}) collective-permute-start(bf16[128,128]{1,0:T(8,128)(2,1)S(1)} %get-tuple-element.55), channel_id=1, source_target_pairs={{0,16},{1,17},{2,18},{3,19},{4,20},{5,21},{6,22},{7,23},{8,24},{9,... | collective-permute-start | bytes 98312 | tf_op jit(solution)/shard_map/ppermute | solution.py:20
  110.9 2.4 %collective-permute-done.38 = bf16[128,128]{1,0:T(8,128)(2,1)S(1)} collective-permute-done((bf16[128,128]{1,0:T(8,128)(2,1)S(1)}, bf16[128,128]{1,0:T(8,128)(2,1)S(1)}, u32[]{:S(2)}, u32[]{:S(2)}) %collective-permute-start.38) | collective-permute-done | bytes 32800 | tf_op jit(solution)/shard_map/ppermute | solution.py:20
  (166 shorter events, 25.6 us)
Async XLA Ops:
  2.4 41.3 %collective-permute-start.2 = (bf16[320,128]{1,0:T(8,128)(2,1)}, bf16[320,128]{1,0:T(8,128)(2,1)S(1)}, u32[]{:S(2)}, u32[]{:S(2)}) collective-permute-start(bf16[320,128]{1,0:T(8,128)(2,1)} %get-tuple-element.51), channel_id=1, source_target_pairs={{0,1},{1,0},{2,3},{3,2},{4,5},{5,4},{6,7},{7,6},{8,9},{9,8},{10,11... | collective-permute-start | bytes 245768 | tf_op jit(solution)/shard_map/ppermute | solution.py:20
  2.9 45.6 %collective-permute-start.4 = (bf16[320,128]{1,0:T(8,128)(2,1)}, bf16[320,128]{1,0:T(8,128)(2,1)S(1)}, u32[]{:S(2)}, u32[]{:S(2)}) collective-permute-start(bf16[320,128]{1,0:T(8,128)(2,1)} %get-tuple-element.51), channel_id=1, source_target_pairs={{0,5},{1,4},{2,7},{3,6},{4,1},{5,0},{6,3},{7,2},{8,13},{9,12},{10,... | collective-permute-start | bytes 245768 | tf_op jit(solution)/shard_map/ppermute | solution.py:20
  6.6 6.9 %collective-permute-start.10 = (bf16[2,64,256]{2,1,0:T(8,128)(2,1)}, bf16[2,64,256]{2,1,0:T(8,128)(2,1)S(1)}, u32[]{:S(2)}, u32[]{:S(2)}) collective-permute-start(bf16[2,64,256]{2,1,0:T(8,128)(2,1)} %param.10), channel_id=1, source_target_pairs={{0,1},{1,0},{2,3},{3,2},{4,5},{5,4},{6,7},{7,6},{8,9},{9,8},{10,11... | collective-permute-start | bytes 196616 | tf_op jit(solution)/shard_map/ppermute | solution.py:20
  7.1 12.6 %collective-permute-start.9 = (bf16[64,3072]{1,0:T(8,128)(2,1)}, bf16[64,3072]{1,0:T(8,128)(2,1)S(1)}, u32[]{:S(2)}, u32[]{:S(2)}) collective-permute-start(bf16[64,3072]{1,0:T(8,128)(2,1)} %param.11), channel_id=1, source_target_pairs={{0,1},{1,0},{2,3},{3,2},{4,5},{5,4},{6,7},{7,6},{8,9},{9,8},{10,11... | collective-permute-start | bytes 1179656 | tf_op jit(solution)/shard_map/ppermute | solution.py:20
  13.5 12.2 %collective-permute-start.23 = (bf16[64,3072]{1,0:T(8,128)(2,1)}, bf16[64,3072]{1,0:T(8,128)(2,1)S(1)}, u32[]{:S(2)}, u32[]{:S(2)}) collective-permute-start(bf16[64,3072]{1,0:T(8,128)(2,1)} %param.11), channel_id=1, source_target_pairs={{0,8},{1,9},{2,10},{3,11},{4,12},{5,13},{6,14},{7,15},{8,0},{9,1},... | collective-permute-start | bytes 1179656 | tf_op jit(solution)/shard_map/ppermute | solution.py:20
  16.3 19.9 %collective-permute-start.25 = (bf16[64,3072]{1,0:T(8,128)(2,1)}, bf16[64,3072]{1,0:T(8,128)(2,1)S(1)}, u32[]{:S(2)}, u32[]{:S(2)}) collective-permute-start(bf16[64,3072]{1,0:T(8,128)(2,1)} %param.11), channel_id=1, source_target_pairs={{0,16},{1,17},{2,18},{3,19},{4,20},{5,21},{6,22},{7,23},{8,24},{9,... | collective-permute-start | bytes 1179656 | tf_op jit(solution)/shard_map/ppermute | solution.py:20
  19.7 17.3 %collective-permute-start.27 = (bf16[64,3072]{1,0:T(8,128)(2,1)S(1)}, bf16[64,3072]{1,0:T(8,128)(2,1)S(1)}, u32[]{:S(2)}, u32[]{:S(2)}) collective-permute-start(bf16[64,3072]{1,0:T(8,128)(2,1)S(1)} %copy-done.6), channel_id=1, source_target_pairs={{0,24},{1,25},{2,26},{3,27},{4,28},{5,29},{6,30},{7,31},{8,16},{9,... | collective-permute-start | bytes 1179656 | tf_op jit(solution)/shard_map/ppermute | solution.py:20
  25.7 25.7 %collective-permute-start.7 = (bf16[320,2560]{1,0:T(8,128)(2,1)S(1)}, bf16[320,2560]{1,0:T(8,128)(2,1)}, u32[]{:S(2)}, u32[]{:S(2)}) collective-permute-start(bf16[320,2560]{1,0:T(8,128)(2,1)S(1)} %copy-done), channel_id=1, source_target_pairs={{0,1},{1,0},{2,3},{3,2},{4,5},{5,4},{6,7},{7,6},{8,9},{9,8},{10,11... | collective-permute-start | bytes 4915208 | tf_op jit(solution)/shard_map/ppermute | solution.py:20
  38.8 9.7 %collective-permute-start.3 = (bf16[320,128]{1,0:T(8,128)(2,1)S(1)}, bf16[320,128]{1,0:T(8,128)(2,1)S(1)}, u32[]{:S(2)}, u32[]{:S(2)}) collective-permute-start(bf16[320,128]{1,0:T(8,128)(2,1)S(1)} %get-tuple-element.52.refs_0_), channel_id=1, source_target_pairs={{0,4},{1,5},{2,6},{3,7},{4,0},{5,1},{6,2},{7,3},{8,12},{9,13},{10,... | collective-permute-start | bytes 245768 | tf_op jit(solution)/shard_map/ppermute | solution.py:20
  39.7 9.2 %collective-permute-start.5 = (bf16[320,128]{1,0:T(8,128)(2,1)S(1)}, bf16[320,128]{1,0:T(8,128)(2,1)S(1)}, u32[]{:S(2)}, u32[]{:S(2)}) collective-permute-start(bf16[320,128]{1,0:T(8,128)(2,1)S(1)} %get-tuple-element.52.refs_0_), channel_id=1, source_target_pairs={{0,6},{1,7},{2,4},{3,5},{4,2},{5,3},{6,0},{7,1},{8,14},{9,15},{10,... | collective-permute-start | bytes 245768 | tf_op jit(solution)/shard_map/ppermute | solution.py:20
  43.7 7.1 %collective-permute-start.6 = (bf16[320,128]{1,0:T(8,128)(2,1)}, bf16[320,128]{1,0:T(8,128)(2,1)S(1)}, u32[]{:S(2)}, u32[]{:S(2)}) collective-permute-start(bf16[320,128]{1,0:T(8,128)(2,1)} %get-tuple-element.51), channel_id=1, source_target_pairs={{0,7},{1,6},{2,5},{3,4},{4,3},{5,2},{6,1},{7,0},{8,15},{9,14},{10,... | collective-permute-start | bytes 245768 | tf_op jit(solution)/shard_map/ppermute | solution.py:20
  48.5 6.3 %collective-permute-start = (bf16[320,128]{1,0:T(8,128)(2,1)S(1)}, bf16[320,128]{1,0:T(8,128)(2,1)S(1)}, u32[]{:S(2)}, u32[]{:S(2)}) collective-permute-start(bf16[320,128]{1,0:T(8,128)(2,1)S(1)} %get-tuple-element.52.refs_0_), channel_id=1, source_target_pairs={{0,2},{1,3},{2,0},{3,1},{4,6},{5,7},{6,4},{7,5},{8,10},{9,11},{10,... | collective-permute-start | bytes 245768 | tf_op jit(solution)/shard_map/ppermute | solution.py:20
  48.5 6.3 %collective-permute-start.1 = (bf16[320,128]{1,0:T(8,128)(2,1)}, bf16[320,128]{1,0:T(8,128)(2,1)S(1)}, u32[]{:S(2)}, u32[]{:S(2)}) collective-permute-start(bf16[320,128]{1,0:T(8,128)(2,1)} %get-tuple-element.51), channel_id=1, source_target_pairs={{0,3},{1,2},{2,1},{3,0},{4,7},{5,6},{6,5},{7,4},{8,11},{9,10},{10,... | collective-permute-start | bytes 245768 | tf_op jit(solution)/shard_map/ppermute | solution.py:20
  48.9 25.4 %collective-permute-start.17 = (bf16[128,2560]{1,0:T(8,128)(2,1)S(1)}, bf16[128,2560]{1,0:T(8,128)(2,1)}, u32[]{:S(2)}, u32[]{:S(2)}) collective-permute-start(bf16[128,2560]{1,0:T(8,128)(2,1)S(1)} %copy-done.3), channel_id=1, source_target_pairs={{0,1},{1,0},{2,3},{3,2},{4,5},{5,4},{6,7},{7,6},{8,9},{9,8},{10,11... | collective-permute-start | bytes 1966088 | tf_op jit(solution)/shard_map/ppermute | solution.py:20
  50.8 29.7 %collective-permute-start.11 = (bf16[128,128]{1,0:T(8,128)(2,1)}, bf16[128,128]{1,0:T(8,128)(2,1)S(1)}, u32[]{:S(2)}, u32[]{:S(2)}) collective-permute-start(bf16[128,128]{1,0:T(8,128)(2,1)} %fusion.21), channel_id=1, source_target_pairs={{0,8},{1,9},{2,10},{3,11},{4,12},{5,13},{6,14},{7,15},{8,0},{9,1},... | collective-permute-start | bytes 98312 | tf_op jit(solution)/shard_map/ppermute | solution.py:20
  55.3 9.0 %collective-permute-start.14 = (bf16[640,128]{1,0:T(8,128)(2,1)S(1)}, bf16[640,128]{1,0:T(8,128)(2,1)S(1)}, u32[]{:S(2)}, u32[]{:S(2)}) collective-permute-start(bf16[640,128]{1,0:T(8,128)(2,1)S(1)} %get-tuple-element.11), channel_id=1, source_target_pairs={{0,6},{1,7},{2,4},{3,5},{4,2},{5,3},{6,0},{7,1},{8,14},{9,15},{10,... | collective-permute-start | bytes 491528 | tf_op jit(solution)/shard_map/ppermute | solution.py:20
  56.1 18.0 %collective-permute-start.15 = (bf16[640,128]{1,0:T(8,128)(2,1)S(1)}, bf16[640,128]{1,0:T(8,128)(2,1)S(1)}, u32[]{:S(2)}, u32[]{:S(2)}) collective-permute-start(bf16[640,128]{1,0:T(8,128)(2,1)S(1)} %get-tuple-element.11), channel_id=1, source_target_pairs={{0,4},{1,5},{2,6},{3,7},{4,0},{5,1},{6,2},{7,3},{8,12},{9,13},{10,... | collective-permute-start | bytes 491528 | tf_op jit(solution)/shard_map/ppermute | solution.py:20
  60.4 13.7 %collective-permute-start.16 = (bf16[640,128]{1,0:T(8,128)(2,1)S(1)}, bf16[640,128]{1,0:T(8,128)(2,1)S(1)}, u32[]{:S(2)}, u32[]{:S(2)}) collective-permute-start(bf16[640,128]{1,0:T(8,128)(2,1)S(1)} %get-tuple-element.11), channel_id=1, source_target_pairs={{0,2},{1,3},{2,0},{3,1},{4,6},{5,7},{6,4},{7,5},{8,10},{9,11},{10,... | collective-permute-start | bytes 491528 | tf_op jit(solution)/shard_map/ppermute | solution.py:20
  76.1 4.3 %collective-permute-start.18 = (bf16[2,2,64,128]{3,2,1,0:T(8,128)(2,1)S(1)}, bf16[2,2,64,128]{3,2,1,0:T(8,128)(2,1)S(1)}, u32[]{:S(2)}, u32[]{:S(2)}) collective-permute-start(bf16[2,2,64,128]{3,2,1,0:T(8,128)(2,1)S(1)} %get-tuple-element.58), channel_id=1, source_target_pairs={{0,8},{1,9},{2,10},{3,11},{4,12},{5,13},{6,14},{7,15},{8,0},{9,1},... | collective-permute-start | bytes 196616 | tf_op jit(solution)/shard_map/ppermute | solution.py:20
  81.4 6.4 %collective-permute-start.19 = (bf16[2,128,128]{2,1,0:T(8,128)(2,1)S(1)}, bf16[2,128,128]{2,1,0:T(8,128)(2,1)S(1)}, u32[]{:S(2)}, u32[]{:S(2)}) collective-permute-start(bf16[2,128,128]{2,1,0:T(8,128)(2,1)S(1)} %pad_maximum_fusion.10), channel_id=1, source_target_pairs={{0,6},{1,7},{2,4},{3,5},{4,2},{5,3},{6,0},{7,1},{8,14},{9,15},{10,... | collective-permute-start | bytes 196616 | tf_op jit(solution)/shard_map/ppermute | solution.py:20
  82.2 6.6 %collective-permute-start.20 = (bf16[2,128,128]{2,1,0:T(8,128)(2,1)S(1)}, bf16[2,128,128]{2,1,0:T(8,128)(2,1)S(1)}, u32[]{:S(2)}, u32[]{:S(2)}) collective-permute-start(bf16[2,128,128]{2,1,0:T(8,128)(2,1)S(1)} %pad_maximum_fusion.10), channel_id=1, source_target_pairs={{0,4},{1,5},{2,6},{3,7},{4,0},{5,1},{6,2},{7,3},{8,12},{9,13},{10,... | collective-permute-start | bytes 196616 | tf_op jit(solution)/shard_map/ppermute | solution.py:20
  82.2 6.6 %collective-permute-start.21 = (bf16[2,128,128]{2,1,0:T(8,128)(2,1)S(1)}, bf16[2,128,128]{2,1,0:T(8,128)(2,1)S(1)}, u32[]{:S(2)}, u32[]{:S(2)}) collective-permute-start(bf16[2,128,128]{2,1,0:T(8,128)(2,1)S(1)} %pad_maximum_fusion.10), channel_id=1, source_target_pairs={{0,2},{1,3},{2,0},{3,1},{4,6},{5,7},{6,4},{7,5},{8,10},{9,11},{10,... | collective-permute-start | bytes 196616 | tf_op jit(solution)/shard_map/ppermute | solution.py:20
  89.3 6.9 %collective-permute-start.30 = (bf16[2,128,128]{2,1,0:T(8,128)(2,1)S(1)}, bf16[2,128,128]{2,1,0:T(8,128)(2,1)S(1)}, u32[]{:S(2)}, u32[]{:S(2)}) collective-permute-start(bf16[2,128,128]{2,1,0:T(8,128)(2,1)S(1)} %pad_maximum_fusion.11), channel_id=1, source_target_pairs={{0,6},{1,7},{2,4},{3,5},{4,2},{5,3},{6,0},{7,1},{8,14},{9,15},{10,... | collective-permute-start | bytes 196616 | tf_op jit(solution)/shard_map/ppermute | solution.py:20
  91.4 6.0 %collective-permute-start.31 = (bf16[2,128,128]{2,1,0:T(8,128)(2,1)S(1)}, bf16[2,128,128]{2,1,0:T(8,128)(2,1)S(1)}, u32[]{:S(2)}, u32[]{:S(2)}) collective-permute-start(bf16[2,128,128]{2,1,0:T(8,128)(2,1)S(1)} %pad_maximum_fusion.11), channel_id=1, source_target_pairs={{0,4},{1,5},{2,6},{3,7},{4,0},{5,1},{6,2},{7,3},{8,12},{9,13},{10,... | collective-permute-start | bytes 196616 | tf_op jit(solution)/shard_map/ppermute | solution.py:20
  92.2 5.3 %collective-permute-start.32 = (bf16[2,128,128]{2,1,0:T(8,128)(2,1)S(1)}, bf16[2,128,128]{2,1,0:T(8,128)(2,1)S(1)}, u32[]{:S(2)}, u32[]{:S(2)}) collective-permute-start(bf16[2,128,128]{2,1,0:T(8,128)(2,1)S(1)} %pad_maximum_fusion.11), channel_id=1, source_target_pairs={{0,2},{1,3},{2,0},{3,1},{4,6},{5,7},{6,4},{7,5},{8,10},{9,11},{10,... | collective-permute-start | bytes 196616 | tf_op jit(solution)/shard_map/ppermute | solution.py:20
  97.9 6.1 %collective-permute-start.33 = (bf16[2,128,128]{2,1,0:T(8,128)(2,1)S(1)}, bf16[2,128,128]{2,1,0:T(8,128)(2,1)S(1)}, u32[]{:S(2)}, u32[]{:S(2)}) collective-permute-start(bf16[2,128,128]{2,1,0:T(8,128)(2,1)S(1)} %pad_maximum_fusion.12), channel_id=1, source_target_pairs={{0,6},{1,7},{2,4},{3,5},{4,2},{5,3},{6,0},{7,1},{8,14},{9,15},{10,... | collective-permute-start | bytes 196616 | tf_op jit(solution)/shard_map/ppermute | solution.py:20
  99.5 5.9 %collective-permute-start.34 = (bf16[2,128,128]{2,1,0:T(8,128)(2,1)S(1)}, bf16[2,128,128]{2,1,0:T(8,128)(2,1)S(1)}, u32[]{:S(2)}, u32[]{:S(2)}) collective-permute-start(bf16[2,128,128]{2,1,0:T(8,128)(2,1)S(1)} %pad_maximum_fusion.12), channel_id=1, source_target_pairs={{0,4},{1,5},{2,6},{3,7},{4,0},{5,1},{6,2},{7,3},{8,12},{9,13},{10,... | collective-permute-start | bytes 196616 | tf_op jit(solution)/shard_map/ppermute | solution.py:20
  100.1 5.4 %collective-permute-start.35 = (bf16[2,128,128]{2,1,0:T(8,128)(2,1)S(1)}, bf16[2,128,128]{2,1,0:T(8,128)(2,1)S(1)}, u32[]{:S(2)}, u32[]{:S(2)}) collective-permute-start(bf16[2,128,128]{2,1,0:T(8,128)(2,1)S(1)} %pad_maximum_fusion.12), channel_id=1, source_target_pairs={{0,2},{1,3},{2,0},{3,1},{4,6},{5,7},{6,4},{7,5},{8,10},{9,11},{10,... | collective-permute-start | bytes 196616 | tf_op jit(solution)/shard_map/ppermute | solution.py:20
  106.0 4.0 %collective-permute-start.36 = (bf16[128,128]{1,0:T(8,128)(2,1)S(1)}, bf16[128,128]{1,0:T(8,128)(2,1)S(1)}, u32[]{:S(2)}, u32[]{:S(2)}) collective-permute-start(bf16[128,128]{1,0:T(8,128)(2,1)S(1)} %get-tuple-element.53), channel_id=1, source_target_pairs={{0,8},{1,9},{2,10},{3,11},{4,12},{5,13},{6,14},{7,15},{8,0},{9,1},... | collective-permute-start | bytes 98312 | tf_op jit(solution)/shard_map/ppermute | solution.py:20
  107.0 3.9 %collective-permute-start.37 = (bf16[128,128]{1,0:T(8,128)(2,1)S(1)}, bf16[128,128]{1,0:T(8,128)(2,1)S(1)}, u32[]{:S(2)}, u32[]{:S(2)}) collective-permute-start(bf16[128,128]{1,0:T(8,128)(2,1)S(1)} %get-tuple-element.55), channel_id=1, source_target_pairs={{0,16},{1,17},{2,18},{3,19},{4,20},{5,21},{6,22},{7,23},{8,24},{9,... | collective-permute-start | bytes 98312 | tf_op jit(solution)/shard_map/ppermute | solution.py:20
  108.5 4.8 %collective-permute-start.38 = (bf16[128,128]{1,0:T(8,128)(2,1)S(1)}, bf16[128,128]{1,0:T(8,128)(2,1)S(1)}, u32[]{:S(2)}, u32[]{:S(2)}) collective-permute-start(bf16[128,128]{1,0:T(8,128)(2,1)S(1)} %get-tuple-element.54), channel_id=1, source_target_pairs={{0,24},{1,25},{2,26},{3,27},{4,28},{5,29},{6,30},{7,31},{8,16},{9,... | collective-permute-start | bytes 98312 | tf_op jit(solution)/shard_map/ppermute | solution.py:20
  109.5 4.6 %collective-permute-start.22 = (bf16[64,128]{1,0:T(8,128)(2,1)S(1)}, bf16[64,128]{1,0:T(8,128)(2,1)S(1)}, u32[]{:S(2)}, u32[]{:S(2)}) collective-permute-start(bf16[64,128]{1,0:T(8,128)(2,1)S(1)} %constant_dynamic-slice_fusion.17), channel_id=1, source_target_pairs={{0,1},{1,0},{2,3},{3,2},{4,5},{5,4},{6,7},{7,6},{8,9},{9,8},{10,11... | collective-permute-start | bytes 49160 | tf_op jit(solution)/shard_map/ppermute | solution.py:20
  (28 other events, 203.7 us)

commit v3 on v2

--- a/solution.py
+++ b/solution.py
@@ -37,6 +37,8 @@
     count = len(masks)
     rows, half = pieces[0].shape
     total = near.shape[1]
+    block = 4 * rows
+    flip = total // block - 1
     dtype = near.dtype
 
     def body(*refs):
@@ -49,15 +51,15 @@
         ]
         for copy in copies:
             copy.start()
-        missing = pl.multiple_of((b // 2 ^ 1) * 2 * rows, 128)
-        rhs[pl.ds(missing, 2 * rows)] = jnp.zeros((2 * rows, half), dtype)
+        missing = pl.multiple_of((b // 4 ^ flip) * block, 128)
+        rhs[pl.ds(missing, block)] = jnp.zeros((block, half), dtype)
         for mask, piece_ref in zip(masks, piece_refs):
             where = pl.multiple_of((b ^ mask) * rows, 16)
             rhs[pl.ds(where, rows)] = piece_ref[...]
         for i, matrix in enumerate((near_vmem, far_vmem)):
             copies[i].wait()
             sum_ref[i] = jnp.dot(matrix[...], rhs[...], preferred_element_type=jnp.float32)
-            rest_ref[i] = matrix[:, pl.ds(missing, 2 * rows)]
+        rest_ref[...] = near_vmem[:, pl.ds(missing, block)]
 
     return pl.pallas_call(
         body,
@@ -65,7 +67,7 @@
         out_specs=vmem_specs(2),
         out_shape=[
             pltpu.VMEM((2, rows, half), jnp.float32),
-            pltpu.VMEM((2, rows, 2 * rows), dtype),
+            pltpu.VMEM((rows, block), dtype),
         ],
         scratch_shapes=[
             pltpu.VMEM((total, half), dtype),
@@ -84,37 +86,80 @@
     )
 
 
-def leaf_finish(same, cross, sums, rest):
-    rows, half = same.shape
-    dtype = same.dtype
-
-    def body(same_ref, cross_ref, sum_ref, rest_ref, all_ref, mine_ref, other_ref, rhs):
-        core = lax.axis_index("blk") % 2
-        low = pl.multiple_of(core * rows, 16)
-        high = pl.multiple_of((1 - core) * rows, 16)
-        rhs[pl.ds(low, rows)] = same_ref[...]
-        rhs[pl.ds(high, rows)] = cross_ref[...]
-        for i, (where, out_ref) in enumerate(((low, mine_ref), (high, other_ref))):
-            value = jnp.dot(rest_ref[i], rhs[...], preferred_element_type=jnp.float32)
+def leaf_finish(pieces, sums, rest, far):
+    count = len(pieces)
+    rows, half = pieces[0].shape
+    dtype = pieces[0].dtype
+    flip = far.shape[1] // (count * rows) - 1
+
+    def body(*refs):
+        piece_refs = refs[:count]
+        sum_ref, rest_ref, far_ref, all_ref, mine_ref, other_ref, rhs, far_vmem, sem = refs[count:]
+        b = lax.axis_index("blk")
+        where = pl.multiple_of((b // count ^ flip) * count * rows, 128)
+        copy = pltpu.make_async_copy(far_ref.at[:, pl.ds(where, count * rows)], far_vmem, sem)
+        copy.start()
+        for mask, piece_ref in enumerate(piece_refs):
+            where = pl.multiple_of((b % count ^ mask) * rows, 16)
+            rhs[pl.ds(where, rows)] = piece_ref[...]
+        for i, (matrix, out_ref) in enumerate(((rest_ref, mine_ref), (far_vmem, other_ref))):
+            if i == 1:
+                copy.wait()
+            value = jnp.dot(matrix[...], rhs[...], preferred_element_type=jnp.float32)
             value = (value + sum_ref[i]).astype(dtype)
             out_ref[...] = value
-            all_ref[pl.ds(where, rows)] = value
+            all_ref[pl.ds(pl.multiple_of((b % 2 ^ i) * rows, 16), rows)] = value
 
     return pl.pallas_call(
         body,
-        in_specs=vmem_specs(4),
+        in_specs=vmem_specs(count + 2) + [pl.BlockSpec(memory_space=pltpu.HBM)],
         out_specs=vmem_specs(3),
         out_shape=[
             pltpu.VMEM((2 * rows, half), dtype),
             pltpu.VMEM((rows, half), dtype),
             pltpu.VMEM((rows, half), dtype),
         ],
-        scratch_shapes=[pltpu.VMEM((2 * rows, half), dtype)],
+        scratch_shapes=[
+            pltpu.VMEM((count * rows, half), dtype),
+            pltpu.VMEM((rows, count * rows), dtype),
+            pltpu.SemaphoreType.DMA,
+        ],
         cost_estimate=pl.CostEstimate(
-            flops=8 * rows * rows * half, bytes_accessed=0, transcendentals=0
+            flops=4 * rows * count * rows * half, bytes_accessed=0, transcendentals=0
         ),
         name="leaf_finish",
-    )(on_chip(same), on_chip(cross), on_chip(sums), on_chip(rest))
+    )(
+        *[on_chip(value) for value in pieces],
+        on_chip(sums),
+        on_chip(rest),
+        pltpu.with_memory_space_constraint(far, pltpu.HBM),
+    )
+
+
+def column_halves(value):
+    rows, half = value.shape[0], value.shape[1] // 2
+
+    def body(value_ref, own_ref, other_ref, sems):
+        core = lax.axis_index("blk") % 2
+        copies = []
+        for i, out_ref in enumerate((own_ref, other_ref)):
+            where = pl.multiple_of((core ^ i) * half, 128)
+            copies.append(
+                pltpu.make_async_copy(value_ref.at[:, pl.ds(where, half)], out_ref, sems.at[i])
+            )
+        for copy in copies:
+            copy.start()
+        for copy in copies:
+            copy.wait()
+
+    return pl.pallas_call(
+        body,
+        in_specs=[pl.BlockSpec(memory_space=pltpu.HBM)],
+        out_specs=vmem_specs(2),
+        out_shape=[pltpu.VMEM((rows, half), value.dtype)] * 2,
+        scratch_shapes=[pltpu.SemaphoreType.DMA((2,))],
+        name="column_halves",
+    )(value)
 
 
 def on_device(leaf_rhs, leaf_inverse, leaf_lower, sep_rhs, sep_inverse, sep_lower, slot_map):
@@ -153,16 +198,12 @@
         )
         return jnp.concatenate([near, far], axis=1)
 
-    own_half = columns_of(leaf_rhs, core)
-    other_half = columns_of(leaf_rhs, 1 - core)
+    inverse_other = exchange(leaf_inverse, 0, 1)
+    own_half, other_half = column_halves(leaf_rhs)
     arrived = {0: own_half}
-    for mask in list(range(blks - 1, 3, -1)) + [1, 3, 2]:
+    far = list(range(blks - 4, blks))
+    for mask in far[::-1] + [m for m in range(blks - 5, 1, -1)] + [1]:
         arrived[mask] = exchange(own_half if mask % 2 == 0 else other_half, 0, mask)
-    inverse_other = exchange(leaf_inverse, 0, 1)
-    slot_other = exchange(slot_map, 0, 1)
-    sep_rhs_other = exchange(sep_rhs, 0, 1)
-    lower_other = exchange(leaf_lower, 0, 1)
-    sep_lower_other = exchange(sep_lower, 0, 1)
     inverse_rows = [sep_inverse]
     for a in range(1, leaves):
         value = sep_inverse
@@ -170,10 +211,14 @@
             value = jnp.concatenate([value[:, : 2 * base_width], leaf_columns(value, k ^ a)], 1)
         inverse_rows.append(exchange(value, a, 0))
 
-    same, cross = arrived.pop(2), arrived.pop(3)
+    last = [arrived.pop(mask) for mask in far]
     sums, beside = leaf_partial(arrived, leaf_inverse, inverse_other)
-    s_all, s_mine, s_other = leaf_finish(same, cross, sums, beside)
+    s_all, s_mine, s_other = leaf_finish(last, sums, beside, inverse_other)
     got = [(m, exchange(s_all, 0, m)) for m in range(blks - 2, 0, -2)]
+    slot_other = exchange(slot_map, 0, 1)
+    sep_rhs_other = exchange(sep_rhs, 0, 1)
+    lower_other = exchange(leaf_lower, 0, 1)
+    sep_lower_other = exchange(sep_lower, 0, 1)
     s_full = put(jnp.zeros((blks * rows, half), dtype), s_all, z)
     for m, value in got:
         s_full = put(s_full, value, z ^ (m // 2))
@@ -289,7 +334,7 @@
     partial = product(top_rows, contributions).reshape(leaves, 2 * pivots, half)
     rounded = partial.astype(dtype)
     total = partial[0]
-    for a in range(1, leaves):
+    for a in range(leaves - 1, 0, -1):
         total = total + exchange(rounded[a], a, 0).astype(jnp.float32)
     solutions.append(total.astype(dtype))
 

time: 116 us -> 116 us (level)
  waiting for transfers between devices: 54.1 us -> 49 us
  Pallas kernels: 3.89 us -> 6.66 us
  local copies, waits for them, and re-layouts: 3.21 us -> 4.54 us
    ppermute x40, waiting for transfers between devices: 54.1 us -> 49 us  [exchange(): return lax.ppermute(value, ('leaf', 'blk'), pairs)]
    pallas_call x1 -> x2, Pallas kernels: 0.39 us -> 3.18 us  [the longest x1 2.08 us: leaf_finish(): pl.pallas_call(body, in_specs=vmem_specs(count + 2) + [pl.BlockSpec(memor...]
    unnamed x40 -> x44, local copies, waits for them, and re-layouts: 0.09 us -> 2.26 us
    dynamic_slice x1 -> x0, local copies, waits for them, and re-layouts: 1.71 us -> none  [columns_of(): return lax.dynamic_slice_in_dim(value, which * half, half, value.ndim - 1)]
  transfers between devices with their start and end apart: 40 -> 40, of which waited for: 21 -> 19; matrix products, arithmetic and copies ran while one was open for 10% -> 12% of each run, Pallas kernels for 3% -> 5%
where the time goes in v3:
time: 116 us; the launch traced here: 115 us
  waiting for transfers between devices  49 us (42%)
  starting transfers between devices  40.1 us (35%)
  other arithmetic  10.7 us (9%)
  Pallas kernels  6.66 us (6%)
  local copies, waits for them, and re-layouts  4.54 us (4%)
  matrix products  2.91 us (3%)
  between operations  1.4 us (1%)
    ppermute x40, waiting for transfers between devices, exchange(): return lax.ppermute(value, ('leaf', 'blk'), pairs)  49 us
    ppermute x40, starting transfers between devices, exchange(): return lax.ppermute(value, ('leaf', 'blk'), pairs)  40.1 us
    select_n x6, other arithmetic, in_order(): first = jnp.where(core == 0, mine, other)  4.82 us
    pallas_call x1, Pallas kernels, leaf_partial(): pl.pallas_call(body, in_specs=vmem_specs(count) + [pl.BlockSpec(memory_sp...  3.48 us
    dot_general x6, matrix products, product(): return jnp.dot(matrix, vectors, preferred_element_type=jnp.float32)  2.91 us
    eq x4, other arithmetic, mix(): hit = (targets == t)[:, :, None, None]  2.36 us
  transfers between devices with their start and end apart: 40, of which 19 were waited for; matrix products, arithmetic and copies ran while one was open for 12% of the time, Pallas kernels for 5%

profile of v3, /device:TPU:0, one launch (start us, length us, event | category | flops | bytes accessed | tf_op | source)
XLA Modules:
  0.0 115.3 jit_solution(12025768300397803626)
XLA Ops:
  2.3 2.7 %collective-permute-start.6 = (bf16[320,128]{1,0:T(8,128)(2,1)S(1)}, bf16[320,128]{1,0:T(8,128)(2,1)S(1)}, u32[]{:S(2)}, u32[]{:S(2)}) collective-permute-start(bf16[320,128]{1,0:T(8,128)(2,1)S(1)} %get-tuple-element.10), channel_id=1, source_target_pairs={{0,3},{1,2},{2,1},{3,0},{4,7},{5,6},{6,5},{7,4},{8,11},{9,10},{10,... | collective-permute-start | bytes 245768 | tf_op jit(solution)/shard_map/ppermute | solution.py:20
  7.7 1.5 %collective-permute-start.13 = (s32[2,2]{1,0:T(2,128)S(1)}, s32[2,2]{1,0:T(2,128)S(1)}, u32[]{:S(2)}, u32[]{:S(2)}) collective-permute-start(s32[2,2]{1,0:T(2,128)S(1)} %get-tuple-element.30), channel_id=1, source_target_pairs={{0,8},{1,9},{2,10},{3,11},{4,12},{5,13},{6,14},{7,15},{8,0},{9,1},... | collective-permute-start | bytes 56 | tf_op jit(solution)/shard_map/ppermute | solution.py:20
  11.9 1.5 %collective-permute-start.23 = (bf16[64,3072]{1,0:T(8,128)(2,1)}, bf16[64,3072]{1,0:T(8,128)(2,1)S(1)}, u32[]{:S(2)}, u32[]{:S(2)}) collective-permute-start(bf16[64,3072]{1,0:T(8,128)(2,1)} %param.11), channel_id=1, source_target_pairs={{0,8},{1,9},{2,10},{3,11},{4,12},{5,13},{6,14},{7,15},{8,0},{9,1},... | collective-permute-start | bytes 1179656 | tf_op jit(solution)/shard_map/ppermute | solution.py:20
  14.8 1.5 %collective-permute-start.25 = (bf16[64,3072]{1,0:T(8,128)(2,1)}, bf16[64,3072]{1,0:T(8,128)(2,1)S(1)}, u32[]{:S(2)}, u32[]{:S(2)}) collective-permute-start(bf16[64,3072]{1,0:T(8,128)(2,1)} %param.11), channel_id=1, source_target_pairs={{0,16},{1,17},{2,18},{3,19},{4,20},{5,21},{6,22},{7,23},{8,24},{9,... | collective-permute-start | bytes 1179656 | tf_op jit(solution)/shard_map/ppermute | solution.py:20
  16.3 1.8 %broadcast_select_fusion.1 = (bf16[128,1024]{1,0:T(8,128)(2,1)}, bf16[128,1024]{1,0:T(8,128)(2,1)}) fusion(bf16[128,1024]{1,0:T(8,128)(2,1)} %param.12, bf16[128,1024]{1,0:T(8,128)(2,1)S(1)} %collective-permute-done.29, pred[]{:T(512)S(6)} %eq.94), kind=kLoop, calls=%fused_computation.13 | loop fusion | flops 262144 | bytes 1048577 | tf_op jit(solution)/shard_map/jit(_where)/select_n | solution.py:183
  19.6 4.5 %collective-permute-done.23 = bf16[64,3072]{1,0:T(8,128)(2,1)S(1)} collective-permute-done((bf16[64,3072]{1,0:T(8,128)(2,1)}, bf16[64,3072]{1,0:T(8,128)(2,1)S(1)}, u32[]{:S(2)}, u32[]{:S(2)}) %collective-permute-start.23) | collective-permute-done | bytes 393248 | tf_op jit(solution)/shard_map/ppermute | solution.py:20
  24.1 10.6 %collective-permute-done.25 = bf16[64,3072]{1,0:T(8,128)(2,1)S(1)} collective-permute-done((bf16[64,3072]{1,0:T(8,128)(2,1)}, bf16[64,3072]{1,0:T(8,128)(2,1)S(1)}, u32[]{:S(2)}, u32[]{:S(2)}) %collective-permute-start.25) | collective-permute-done | bytes 393248 | tf_op jit(solution)/shard_map/ppermute | solution.py:20
  34.7 1.6 %broadcast_select_fusion.5 = (bf16[64,1024]{1,0:T(8,128)(2,1)S(1)}, bf16[64,1024]{1,0:T(8,128)(2,1)}) fusion(pred[]{:T(512)S(6)} %eq.94, bf16[64,3072]{1,0:T(8,128)(2,1)} %collective-permute-done.9, bf16[64,3072]{1,0:T(8,128)(2,1)S(1)} %copy-done.7), kind=kLoop, calls=%fused_computation.50 | loop fusion | flops 131072 | bytes 524289 | tf_op jit(solution)/shard_map/jit(_where)/select_n | solution.py:183
  38.7 2.7 %collective-permute-start = (bf16[320,128]{1,0:T(8,128)(2,1)S(1)}, bf16[320,128]{1,0:T(8,128)(2,1)S(1)}, u32[]{:S(2)}, u32[]{:S(2)}) collective-permute-start(bf16[320,128]{1,0:T(8,128)(2,1)S(1)} %get-tuple-element.9.refs_0_), channel_id=1, source_target_pairs={{0,4},{1,5},{2,6},{3,7},{4,0},{5,1},{6,2},{7,3},{8,12},{9,13},{10,... | collective-permute-start | bytes 245768 | tf_op jit(solution)/shard_map/ppermute | solution.py:20
  42.2 2.4 %collective-permute-done.5.refs_2_ = bf16[320,128]{1,0:T(8,128)(2,1)S(1)} collective-permute-done((bf16[320,128]{1,0:T(8,128)(2,1)S(1)}, bf16[320,128]{1,0:T(8,128)(2,1)S(1)}, u32[]{:S(2)}, u32[]{:S(2)}) %collective-permute-start.5) | collective-permute-done | bytes 81952 | tf_op jit(solution)/shard_map/ppermute | solution.py:20
  48.2 2.6 %collective-permute-start.17 = (bf16[128,2560]{1,0:T(8,128)(2,1)S(1)}, bf16[128,2560]{1,0:T(8,128)(2,1)}, u32[]{:S(2)}, u32[]{:S(2)}) collective-permute-start(bf16[128,2560]{1,0:T(8,128)(2,1)S(1)} %copy-done.4), channel_id=1, source_target_pairs={{0,1},{1,0},{2,3},{3,2},{4,5},{5,4},{6,7},{7,6},{8,9},{9,8},{10,11... | collective-permute-start | bytes 1966088 | tf_op jit(solution)/shard_map/ppermute | solution.py:20
  50.8 3.5 %leaf_partial.1 = (f32[2,320,128]{2,1,0:T(8,128)S(1)}, bf16[320,1280]{1,0:T(8,128)(2,1)S(1)}) custom-call(bf16[320,128]{1,0:T(8,128)(2,1)S(1)} %get-tuple-element.9.refs_0_, bf16[320,128]{1,0:T(8,128)(2,1)S(1)} %collective-permute-done.4.refs_1_, bf16[320,128]{1,0:T(8,128)(2,1)S(1)} %collective-permute-done.5.refs_2_, ...), custom_call_target="tpu_custom_call" | custom-call | flops 419430400 | bytes 3276800 | tf_op jit(solution)/shard_map/leaf_partial/pallas_call | solution.py:64
  54.9 2.1 %leaf_finish.1 = (bf16[640,128]{1,0:T(8,128)(2,1)S(1)}, bf16[320,128]{1,0:T(8,128)(2,1)S(1)}, bf16[320,128]{1,0:T(8,128)(2,1)S(1)}) custom-call(bf16[320,128]{1,0:T(8,128)(2,1)S(1)} %collective-permute-done.refs_0_, bf16[320,128]{1,0:T(8,128)(2,1)S(1)} %collective-permute-done.1.refs_1_, bf16[320,128]{1,0:T(8,128)(2,1)S(1)} %collective-permute-done.2.refs_2_, ...), custom_call_target="tpu_custom_call" | custom-call | flops 209715200 | tf_op jit(solution)/shard_map/leaf_finish/pallas_call | solution.py:113
  57.0 1.4 %collective-permute-start.14 = (bf16[640,128]{1,0:T(8,128)(2,1)S(1)}, bf16[640,128]{1,0:T(8,128)(2,1)S(1)}, u32[]{:S(2)}, u32[]{:S(2)}) collective-permute-start(bf16[640,128]{1,0:T(8,128)(2,1)S(1)} %get-tuple-element.15), channel_id=1, source_target_pairs={{0,6},{1,7},{2,4},{3,5},{4,2},{5,3},{6,0},{7,1},{8,14},{9,15},{10,... | collective-permute-start | bytes 491528 | tf_op jit(solution)/shard_map/ppermute | solution.py:20
  58.5 2.9 %collective-permute-start.15 = (bf16[640,128]{1,0:T(8,128)(2,1)S(1)}, bf16[640,128]{1,0:T(8,128)(2,1)S(1)}, u32[]{:S(2)}, u32[]{:S(2)}) collective-permute-start(bf16[640,128]{1,0:T(8,128)(2,1)S(1)} %get-tuple-element.15), channel_id=1, source_target_pairs={{0,4},{1,5},{2,6},{3,7},{4,0},{5,1},{6,2},{7,3},{8,12},{9,13},{10,... | collective-permute-start | bytes 491528 | tf_op jit(solution)/shard_map/ppermute | solution.py:20
  62.9 2.3 %collective-permute-done.14 = bf16[640,128]{1,0:T(8,128)(2,1)S(1)} collective-permute-done((bf16[640,128]{1,0:T(8,128)(2,1)S(1)}, bf16[640,128]{1,0:T(8,128)(2,1)S(1)}, u32[]{:S(2)}, u32[]{:S(2)}) %collective-permute-start.14) | collective-permute-done | bytes 163872 | tf_op jit(solution)/shard_map/ppermute | solution.py:20
  65.2 10.0 %collective-permute-done.15 = bf16[640,128]{1,0:T(8,128)(2,1)S(1)} collective-permute-done((bf16[640,128]{1,0:T(8,128)(2,1)S(1)}, bf16[640,128]{1,0:T(8,128)(2,1)S(1)}, u32[]{:S(2)}, u32[]{:S(2)}) %collective-permute-start.15) | collective-permute-done | bytes 163872 | tf_op jit(solution)/shard_map/ppermute | solution.py:20
  75.4 1.4 %fusion.34 = f32[128,128]{0,1:T(8,128)S(1)} fusion(bf16[128,2560]{1,0:T(8,128)(2,1)} %collective-permute-done.17, bf16[2560,128]{1,0:T(8,128)(2,1)S(1)} %constant_dynamic-update-slice_fusion), kind=kOutput, calls=%fused_computation.148 | convolution fusion | flops 83886080 | bytes 1376256 | tf_op jit(solution)/shard_map/dot_general | solution.py:24
  77.2 1.4 %collective-permute-start.18 = (bf16[2,2,64,128]{3,2,1,0:T(8,128)(2,1)S(1)}, bf16[2,2,64,128]{3,2,1,0:T(8,128)(2,1)S(1)}, u32[]{:S(2)}, u32[]{:S(2)}) collective-permute-start(bf16[2,2,64,128]{3,2,1,0:T(8,128)(2,1)S(1)} %get-tuple-element.60), channel_id=1, source_target_pairs={{0,8},{1,9},{2,10},{3,11},{4,12},{5,13},{6,14},{7,15},{8,0},{9,1},... | collective-permute-start | bytes 196616 | tf_op jit(solution)/shard_map/ppermute | solution.py:20
  78.8 2.8 %collective-permute-done.18 = bf16[2,2,64,128]{3,2,1,0:T(8,128)(2,1)S(1)} collective-permute-done((bf16[2,2,64,128]{3,2,1,0:T(8,128)(2,1)S(1)}, bf16[2,2,64,128]{3,2,1,0:T(8,128)(2,1)S(1)}, u32[]{:S(2)}, u32[]{:S(2)}) %collective-permute-start.18) | collective-permute-done | bytes 65568 | tf_op jit(solution)/shard_map/ppermute | solution.py:20
  81.8 1.9 %collective-permute-start.19 = (bf16[2,128,128]{2,1,0:T(8,128)(2,1)S(1)}, bf16[2,128,128]{2,1,0:T(8,128)(2,1)S(1)}, u32[]{:S(2)}, u32[]{:S(2)}) collective-permute-start(bf16[2,128,128]{2,1,0:T(8,128)(2,1)S(1)} %pad_maximum_fusion.10), channel_id=1, source_target_pairs={{0,6},{1,7},{2,4},{3,5},{4,2},{5,3},{6,0},{7,1},{8,14},{9,15},{10,... | collective-permute-start | bytes 196616 | tf_op jit(solution)/shard_map/ppermute | solution.py:20
  83.7 2.5 %collective-permute-start.21 = (bf16[2,128,128]{2,1,0:T(8,128)(2,1)S(1)}, bf16[2,128,128]{2,1,0:T(8,128)(2,1)S(1)}, u32[]{:S(2)}, u32[]{:S(2)}) collective-permute-start(bf16[2,128,128]{2,1,0:T(8,128)(2,1)S(1)} %pad_maximum_fusion.10), channel_id=1, source_target_pairs={{0,2},{1,3},{2,0},{3,1},{4,6},{5,7},{6,4},{7,5},{8,10},{9,11},{10,... | collective-permute-start | bytes 196616 | tf_op jit(solution)/shard_map/ppermute | solution.py:20
  86.4 2.0 %collective-permute-done.19 = bf16[2,128,128]{2,1,0:T(8,128)(2,1)S(1)} collective-permute-done((bf16[2,128,128]{2,1,0:T(8,128)(2,1)S(1)}, bf16[2,128,128]{2,1,0:T(8,128)(2,1)S(1)}, u32[]{:S(2)}, u32[]{:S(2)}) %collective-permute-start.19) | collective-permute-done | bytes 65568 | tf_op jit(solution)/shard_map/ppermute | solution.py:20
  90.4 2.0 %collective-permute-start.30 = (bf16[2,128,128]{2,1,0:T(8,128)(2,1)S(1)}, bf16[2,128,128]{2,1,0:T(8,128)(2,1)S(1)}, u32[]{:S(2)}, u32[]{:S(2)}) collective-permute-start(bf16[2,128,128]{2,1,0:T(8,128)(2,1)S(1)} %pad_maximum_fusion.11), channel_id=1, source_target_pairs={{0,6},{1,7},{2,4},{3,5},{4,2},{5,3},{6,0},{7,1},{8,14},{9,15},{10,... | collective-permute-start | bytes 196616 | tf_op jit(solution)/shard_map/ppermute | solution.py:20
  92.6 2.3 %collective-permute-start.32 = (bf16[2,128,128]{2,1,0:T(8,128)(2,1)S(1)}, bf16[2,128,128]{2,1,0:T(8,128)(2,1)S(1)}, u32[]{:S(2)}, u32[]{:S(2)}) collective-permute-start(bf16[2,128,128]{2,1,0:T(8,128)(2,1)S(1)} %pad_maximum_fusion.11), channel_id=1, source_target_pairs={{0,2},{1,3},{2,0},{3,1},{4,6},{5,7},{6,4},{7,5},{8,10},{9,11},{10,... | collective-permute-start | bytes 196616 | tf_op jit(solution)/shard_map/ppermute | solution.py:20
  94.9 1.6 %collective-permute-done.30 = bf16[2,128,128]{2,1,0:T(8,128)(2,1)S(1)} collective-permute-done((bf16[2,128,128]{2,1,0:T(8,128)(2,1)S(1)}, bf16[2,128,128]{2,1,0:T(8,128)(2,1)S(1)}, u32[]{:S(2)}, u32[]{:S(2)}) %collective-permute-start.30) | collective-permute-done | bytes 65568 | tf_op jit(solution)/shard_map/ppermute | solution.py:20
  96.5 1.5 %collective-permute-done.31 = bf16[2,128,128]{2,1,0:T(8,128)(2,1)S(1)} collective-permute-done((bf16[2,128,128]{2,1,0:T(8,128)(2,1)S(1)}, bf16[2,128,128]{2,1,0:T(8,128)(2,1)S(1)}, u32[]{:S(2)}, u32[]{:S(2)}) %collective-permute-start.31) | collective-permute-done | bytes 65568 | tf_op jit(solution)/shard_map/ppermute | solution.py:20
  98.5 2.0 %collective-permute-start.33 = (bf16[2,128,128]{2,1,0:T(8,128)(2,1)S(1)}, bf16[2,128,128]{2,1,0:T(8,128)(2,1)S(1)}, u32[]{:S(2)}, u32[]{:S(2)}) collective-permute-start(bf16[2,128,128]{2,1,0:T(8,128)(2,1)S(1)} %pad_maximum_fusion.12), channel_id=1, source_target_pairs={{0,6},{1,7},{2,4},{3,5},{4,2},{5,3},{6,0},{7,1},{8,14},{9,15},{10,... | collective-permute-start | bytes 196616 | tf_op jit(solution)/shard_map/ppermute | solution.py:20
  101.1 1.9 %collective-permute-start.35 = (bf16[2,128,128]{2,1,0:T(8,128)(2,1)S(1)}, bf16[2,128,128]{2,1,0:T(8,128)(2,1)S(1)}, u32[]{:S(2)}, u32[]{:S(2)}) collective-permute-start(bf16[2,128,128]{2,1,0:T(8,128)(2,1)S(1)} %pad_maximum_fusion.12), channel_id=1, source_target_pairs={{0,2},{1,3},{2,0},{3,1},{4,6},{5,7},{6,4},{7,5},{8,10},{9,11},{10,... | collective-permute-start | bytes 196616 | tf_op jit(solution)/shard_map/ppermute | solution.py:20
  103.0 1.6 %collective-permute-done.33 = bf16[2,128,128]{2,1,0:T(8,128)(2,1)S(1)} collective-permute-done((bf16[2,128,128]{2,1,0:T(8,128)(2,1)S(1)}, bf16[2,128,128]{2,1,0:T(8,128)(2,1)S(1)}, u32[]{:S(2)}, u32[]{:S(2)}) %collective-permute-start.33) | collective-permute-done | bytes 65568 | tf_op jit(solution)/shard_map/ppermute | solution.py:20
  104.6 1.4 %collective-permute-done.34 = bf16[2,128,128]{2,1,0:T(8,128)(2,1)S(1)} collective-permute-done((bf16[2,128,128]{2,1,0:T(8,128)(2,1)S(1)}, bf16[2,128,128]{2,1,0:T(8,128)(2,1)S(1)}, u32[]{:S(2)}, u32[]{:S(2)}) %collective-permute-start.34) | collective-permute-done | bytes 65568 | tf_op jit(solution)/shard_map/ppermute | solution.py:20
  106.6 2.4 %collective-permute-start.36 = (bf16[128,128]{1,0:T(8,128)(2,1)S(1)}, bf16[128,128]{1,0:T(8,128)(2,1)S(1)}, u32[]{:S(2)}, u32[]{:S(2)}) collective-permute-start(bf16[128,128]{1,0:T(8,128)(2,1)S(1)} %get-tuple-element.55), channel_id=1, source_target_pairs={{0,24},{1,25},{2,26},{3,27},{4,28},{5,29},{6,30},{7,31},{8,16},{9,... | collective-permute-start | bytes 98312 | tf_op jit(solution)/shard_map/ppermute | solution.py:20
  (170 shorter events, 29.7 us)
Async XLA Ops:
  1.8 40.4 %collective-permute-start.4 = (bf16[320,128]{1,0:T(8,128)(2,1)S(1)}, bf16[320,128]{1,0:T(8,128)(2,1)S(1)}, u32[]{:S(2)}, u32[]{:S(2)}) collective-permute-start(bf16[320,128]{1,0:T(8,128)(2,1)S(1)} %get-tuple-element.10), channel_id=1, source_target_pairs={{0,1},{1,0},{2,3},{3,2},{4,5},{5,4},{6,7},{7,6},{8,9},{9,8},{10,11... | collective-permute-start | bytes 245768 | tf_op jit(solution)/shard_map/ppermute | solution.py:20
  2.3 43.3 %collective-permute-start.6 = (bf16[320,128]{1,0:T(8,128)(2,1)S(1)}, bf16[320,128]{1,0:T(8,128)(2,1)S(1)}, u32[]{:S(2)}, u32[]{:S(2)}) collective-permute-start(bf16[320,128]{1,0:T(8,128)(2,1)S(1)} %get-tuple-element.10), channel_id=1, source_target_pairs={{0,3},{1,2},{2,1},{3,0},{4,7},{5,6},{6,5},{7,4},{8,11},{9,10},{10,... | collective-permute-start | bytes 245768 | tf_op jit(solution)/shard_map/ppermute | solution.py:20
  5.1 6.9 %collective-permute-start.10 = (bf16[2,64,256]{2,1,0:T(8,128)(2,1)}, bf16[2,64,256]{2,1,0:T(8,128)(2,1)S(1)}, u32[]{:S(2)}, u32[]{:S(2)}) collective-permute-start(bf16[2,64,256]{2,1,0:T(8,128)(2,1)} %param.10), channel_id=1, source_target_pairs={{0,1},{1,0},{2,3},{3,2},{4,5},{5,4},{6,7},{7,6},{8,9},{9,8},{10,11... | collective-permute-start | bytes 196616 | tf_op jit(solution)/shard_map/ppermute | solution.py:20
  5.5 12.6 %collective-permute-start.9 = (bf16[64,3072]{1,0:T(8,128)(2,1)}, bf16[64,3072]{1,0:T(8,128)(2,1)}, u32[]{:S(2)}, u32[]{:S(2)}) collective-permute-start(bf16[64,3072]{1,0:T(8,128)(2,1)} %param.11), channel_id=1, source_target_pairs={{0,1},{1,0},{2,3},{3,2},{4,5},{5,4},{6,7},{7,6},{8,9},{9,8},{10,11... | collective-permute-start | bytes 1179656 | tf_op jit(solution)/shard_map/ppermute | solution.py:20
  11.9 12.2 %collective-permute-start.23 = (bf16[64,3072]{1,0:T(8,128)(2,1)}, bf16[64,3072]{1,0:T(8,128)(2,1)S(1)}, u32[]{:S(2)}, u32[]{:S(2)}) collective-permute-start(bf16[64,3072]{1,0:T(8,128)(2,1)} %param.11), channel_id=1, source_target_pairs={{0,8},{1,9},{2,10},{3,11},{4,12},{5,13},{6,14},{7,15},{8,0},{9,1},... | collective-permute-start | bytes 1179656 | tf_op jit(solution)/shard_map/ppermute | solution.py:20
  14.8 19.9 %collective-permute-start.25 = (bf16[64,3072]{1,0:T(8,128)(2,1)}, bf16[64,3072]{1,0:T(8,128)(2,1)S(1)}, u32[]{:S(2)}, u32[]{:S(2)}) collective-permute-start(bf16[64,3072]{1,0:T(8,128)(2,1)} %param.11), channel_id=1, source_target_pairs={{0,16},{1,17},{2,18},{3,19},{4,20},{5,21},{6,22},{7,23},{8,24},{9,... | collective-permute-start | bytes 1179656 | tf_op jit(solution)/shard_map/ppermute | solution.py:20
  18.1 18.2 %collective-permute-start.27 = (bf16[64,3072]{1,0:T(8,128)(2,1)S(1)}, bf16[64,3072]{1,0:T(8,128)(2,1)S(1)}, u32[]{:S(2)}, u32[]{:S(2)}) collective-permute-start(bf16[64,3072]{1,0:T(8,128)(2,1)S(1)} %copy-done.7), channel_id=1, source_target_pairs={{0,24},{1,25},{2,26},{3,27},{4,28},{5,29},{6,30},{7,31},{8,16},{9,... | collective-permute-start | bytes 1179656 | tf_op jit(solution)/shard_map/ppermute | solution.py:20
  24.1 21.9 %collective-permute-start.7 = (bf16[320,2560]{1,0:T(8,128)(2,1)S(1)}, bf16[320,2560]{1,0:T(8,128)(2,1)S(1)}, u32[]{:S(2)}, u32[]{:S(2)}) collective-permute-start(bf16[320,2560]{1,0:T(8,128)(2,1)S(1)} %copy-done.1), channel_id=1, source_target_pairs={{0,1},{1,0},{2,3},{3,2},{4,5},{5,4},{6,7},{7,6},{8,9},{9,8},{10,11... | collective-permute-start | bytes 4915208 | tf_op jit(solution)/shard_map/ppermute | solution.py:20
  38.2 6.5 %collective-permute-start.5 = (bf16[320,128]{1,0:T(8,128)(2,1)S(1)}, bf16[320,128]{1,0:T(8,128)(2,1)S(1)}, u32[]{:S(2)}, u32[]{:S(2)}) collective-permute-start(bf16[320,128]{1,0:T(8,128)(2,1)S(1)} %get-tuple-element.9.refs_0_), channel_id=1, source_target_pairs={{0,2},{1,3},{2,0},{3,1},{4,6},{5,7},{6,4},{7,5},{8,10},{9,11},{10,... | collective-permute-start | bytes 245768 | tf_op jit(solution)/shard_map/ppermute | solution.py:20
  38.7 15.6 %collective-permute-start = (bf16[320,128]{1,0:T(8,128)(2,1)S(1)}, bf16[320,128]{1,0:T(8,128)(2,1)S(1)}, u32[]{:S(2)}, u32[]{:S(2)}) collective-permute-start(bf16[320,128]{1,0:T(8,128)(2,1)S(1)} %get-tuple-element.9.refs_0_), channel_id=1, source_target_pairs={{0,4},{1,5},{2,6},{3,7},{4,0},{5,1},{6,2},{7,3},{8,12},{9,13},{10,... | collective-permute-start | bytes 245768 | tf_op jit(solution)/shard_map/ppermute | solution.py:20
  42.2 12.8 %collective-permute-start.1 = (bf16[320,128]{1,0:T(8,128)(2,1)S(1)}, bf16[320,128]{1,0:T(8,128)(2,1)S(1)}, u32[]{:S(2)}, u32[]{:S(2)}) collective-permute-start(bf16[320,128]{1,0:T(8,128)(2,1)S(1)} %get-tuple-element.10), channel_id=1, source_target_pairs={{0,5},{1,4},{2,7},{3,6},{4,1},{5,0},{6,3},{7,2},{8,13},{9,12},{10,... | collective-permute-start | bytes 245768 | tf_op jit(solution)/shard_map/ppermute | solution.py:20
  44.6 10.3 %collective-permute-start.2 = (bf16[320,128]{1,0:T(8,128)(2,1)S(1)}, bf16[320,128]{1,0:T(8,128)(2,1)S(1)}, u32[]{:S(2)}, u32[]{:S(2)}) collective-permute-start(bf16[320,128]{1,0:T(8,128)(2,1)S(1)} %get-tuple-element.9.refs_0_), channel_id=1, source_target_pairs={{0,6},{1,7},{2,4},{3,5},{4,2},{5,3},{6,0},{7,1},{8,14},{9,15},{10,... | collective-permute-start | bytes 245768 | tf_op jit(solution)/shard_map/ppermute | solution.py:20
  45.6 9.3 %collective-permute-start.3 = (bf16[320,128]{1,0:T(8,128)(2,1)S(1)}, bf16[320,128]{1,0:T(8,128)(2,1)S(1)}, u32[]{:S(2)}, u32[]{:S(2)}) collective-permute-start(bf16[320,128]{1,0:T(8,128)(2,1)S(1)} %get-tuple-element.10), channel_id=1, source_target_pairs={{0,7},{1,6},{2,5},{3,4},{4,3},{5,2},{6,1},{7,0},{8,15},{9,14},{10,... | collective-permute-start | bytes 245768 | tf_op jit(solution)/shard_map/ppermute | solution.py:20
  48.2 27.2 %collective-permute-start.17 = (bf16[128,2560]{1,0:T(8,128)(2,1)S(1)}, bf16[128,2560]{1,0:T(8,128)(2,1)}, u32[]{:S(2)}, u32[]{:S(2)}) collective-permute-start(bf16[128,2560]{1,0:T(8,128)(2,1)S(1)} %copy-done.4), channel_id=1, source_target_pairs={{0,1},{1,0},{2,3},{3,2},{4,5},{5,4},{6,7},{7,6},{8,9},{9,8},{10,11... | collective-permute-start | bytes 1966088 | tf_op jit(solution)/shard_map/ppermute | solution.py:20
  54.3 27.4 %collective-permute-start.11 = (bf16[128,128]{1,0:T(8,128)(2,1)S(1)}, bf16[128,128]{1,0:T(8,128)(2,1)S(1)}, u32[]{:S(2)}, u32[]{:S(2)}) collective-permute-start(bf16[128,128]{1,0:T(8,128)(2,1)S(1)} %copy-done.11), channel_id=1, source_target_pairs={{0,8},{1,9},{2,10},{3,11},{4,12},{5,13},{6,14},{7,15},{8,0},{9,1},... | collective-permute-start | bytes 98312 | tf_op jit(solution)/shard_map/ppermute | solution.py:20
  57.0 8.2 %collective-permute-start.14 = (bf16[640,128]{1,0:T(8,128)(2,1)S(1)}, bf16[640,128]{1,0:T(8,128)(2,1)S(1)}, u32[]{:S(2)}, u32[]{:S(2)}) collective-permute-start(bf16[640,128]{1,0:T(8,128)(2,1)S(1)} %get-tuple-element.15), channel_id=1, source_target_pairs={{0,6},{1,7},{2,4},{3,5},{4,2},{5,3},{6,0},{7,1},{8,14},{9,15},{10,... | collective-permute-start | bytes 491528 | tf_op jit(solution)/shard_map/ppermute | solution.py:20
  58.5 16.8 %collective-permute-start.15 = (bf16[640,128]{1,0:T(8,128)(2,1)S(1)}, bf16[640,128]{1,0:T(8,128)(2,1)S(1)}, u32[]{:S(2)}, u32[]{:S(2)}) collective-permute-start(bf16[640,128]{1,0:T(8,128)(2,1)S(1)} %get-tuple-element.15), channel_id=1, source_target_pairs={{0,4},{1,5},{2,6},{3,7},{4,0},{5,1},{6,2},{7,3},{8,12},{9,13},{10,... | collective-permute-start | bytes 491528 | tf_op jit(solution)/shard_map/ppermute | solution.py:20
  62.6 12.7 %collective-permute-start.16 = (bf16[640,128]{1,0:T(8,128)(2,1)S(1)}, bf16[640,128]{1,0:T(8,128)(2,1)S(1)}, u32[]{:S(2)}, u32[]{:S(2)}) collective-permute-start(bf16[640,128]{1,0:T(8,128)(2,1)S(1)} %get-tuple-element.15), channel_id=1, source_target_pairs={{0,2},{1,3},{2,0},{3,1},{4,6},{5,7},{6,4},{7,5},{8,10},{9,11},{10,... | collective-permute-start | bytes 491528 | tf_op jit(solution)/shard_map/ppermute | solution.py:20
  77.2 4.3 %collective-permute-start.18 = (bf16[2,2,64,128]{3,2,1,0:T(8,128)(2,1)S(1)}, bf16[2,2,64,128]{3,2,1,0:T(8,128)(2,1)S(1)}, u32[]{:S(2)}, u32[]{:S(2)}) collective-permute-start(bf16[2,2,64,128]{3,2,1,0:T(8,128)(2,1)S(1)} %get-tuple-element.60), channel_id=1, source_target_pairs={{0,8},{1,9},{2,10},{3,11},{4,12},{5,13},{6,14},{7,15},{8,0},{9,1},... | collective-permute-start | bytes 196616 | tf_op jit(solution)/shard_map/ppermute | solution.py:20
  81.8 6.6 %collective-permute-start.19 = (bf16[2,128,128]{2,1,0:T(8,128)(2,1)S(1)}, bf16[2,128,128]{2,1,0:T(8,128)(2,1)S(1)}, u32[]{:S(2)}, u32[]{:S(2)}) collective-permute-start(bf16[2,128,128]{2,1,0:T(8,128)(2,1)S(1)} %pad_maximum_fusion.10), channel_id=1, source_target_pairs={{0,6},{1,7},{2,4},{3,5},{4,2},{5,3},{6,0},{7,1},{8,14},{9,15},{10,... | collective-permute-start | bytes 196616 | tf_op jit(solution)/shard_map/ppermute | solution.py:20
  83.7 6.1 %collective-permute-start.20 = (bf16[2,128,128]{2,1,0:T(8,128)(2,1)S(1)}, bf16[2,128,128]{2,1,0:T(8,128)(2,1)S(1)}, u32[]{:S(2)}, u32[]{:S(2)}) collective-permute-start(bf16[2,128,128]{2,1,0:T(8,128)(2,1)S(1)} %pad_maximum_fusion.10), channel_id=1, source_target_pairs={{0,4},{1,5},{2,6},{3,7},{4,0},{5,1},{6,2},{7,3},{8,12},{9,13},{10,... | collective-permute-start | bytes 196616 | tf_op jit(solution)/shard_map/ppermute | solution.py:20
  83.7 6.1 %collective-permute-start.21 = (bf16[2,128,128]{2,1,0:T(8,128)(2,1)S(1)}, bf16[2,128,128]{2,1,0:T(8,128)(2,1)S(1)}, u32[]{:S(2)}, u32[]{:S(2)}) collective-permute-start(bf16[2,128,128]{2,1,0:T(8,128)(2,1)S(1)} %pad_maximum_fusion.10), channel_id=1, source_target_pairs={{0,2},{1,3},{2,0},{3,1},{4,6},{5,7},{6,4},{7,5},{8,10},{9,11},{10,... | collective-permute-start | bytes 196616 | tf_op jit(solution)/shard_map/ppermute | solution.py:20
  90.4 6.1 %collective-permute-start.30 = (bf16[2,128,128]{2,1,0:T(8,128)(2,1)S(1)}, bf16[2,128,128]{2,1,0:T(8,128)(2,1)S(1)}, u32[]{:S(2)}, u32[]{:S(2)}) collective-permute-start(bf16[2,128,128]{2,1,0:T(8,128)(2,1)S(1)} %pad_maximum_fusion.11), channel_id=1, source_target_pairs={{0,6},{1,7},{2,4},{3,5},{4,2},{5,3},{6,0},{7,1},{8,14},{9,15},{10,... | collective-permute-start | bytes 196616 | tf_op jit(solution)/shard_map/ppermute | solution.py:20
  92.4 5.6 %collective-permute-start.31 = (bf16[2,128,128]{2,1,0:T(8,128)(2,1)S(1)}, bf16[2,128,128]{2,1,0:T(8,128)(2,1)S(1)}, u32[]{:S(2)}, u32[]{:S(2)}) collective-permute-start(bf16[2,128,128]{2,1,0:T(8,128)(2,1)S(1)} %pad_maximum_fusion.11), channel_id=1, source_target_pairs={{0,4},{1,5},{2,6},{3,7},{4,0},{5,1},{6,2},{7,3},{8,12},{9,13},{10,... | collective-permute-start | bytes 196616 | tf_op jit(solution)/shard_map/ppermute | solution.py:20
  92.6 5.4 %collective-permute-start.32 = (bf16[2,128,128]{2,1,0:T(8,128)(2,1)S(1)}, bf16[2,128,128]{2,1,0:T(8,128)(2,1)S(1)}, u32[]{:S(2)}, u32[]{:S(2)}) collective-permute-start(bf16[2,128,128]{2,1,0:T(8,128)(2,1)S(1)} %pad_maximum_fusion.11), channel_id=1, source_target_pairs={{0,2},{1,3},{2,0},{3,1},{4,6},{5,7},{6,4},{7,5},{8,10},{9,11},{10,... | collective-permute-start | bytes 196616 | tf_op jit(solution)/shard_map/ppermute | solution.py:20
  98.5 6.1 %collective-permute-start.33 = (bf16[2,128,128]{2,1,0:T(8,128)(2,1)S(1)}, bf16[2,128,128]{2,1,0:T(8,128)(2,1)S(1)}, u32[]{:S(2)}, u32[]{:S(2)}) collective-permute-start(bf16[2,128,128]{2,1,0:T(8,128)(2,1)S(1)} %pad_maximum_fusion.12), channel_id=1, source_target_pairs={{0,6},{1,7},{2,4},{3,5},{4,2},{5,3},{6,0},{7,1},{8,14},{9,15},{10,... | collective-permute-start | bytes 196616 | tf_op jit(solution)/shard_map/ppermute | solution.py:20
  100.5 5.5 %collective-permute-start.34 = (bf16[2,128,128]{2,1,0:T(8,128)(2,1)S(1)}, bf16[2,128,128]{2,1,0:T(8,128)(2,1)S(1)}, u32[]{:S(2)}, u32[]{:S(2)}) collective-permute-start(bf16[2,128,128]{2,1,0:T(8,128)(2,1)S(1)} %pad_maximum_fusion.12), channel_id=1, source_target_pairs={{0,4},{1,5},{2,6},{3,7},{4,0},{5,1},{6,2},{7,3},{8,12},{9,13},{10,... | collective-permute-start | bytes 196616 | tf_op jit(solution)/shard_map/ppermute | solution.py:20
  101.1 5.0 %collective-permute-start.35 = (bf16[2,128,128]{2,1,0:T(8,128)(2,1)S(1)}, bf16[2,128,128]{2,1,0:T(8,128)(2,1)S(1)}, u32[]{:S(2)}, u32[]{:S(2)}) collective-permute-start(bf16[2,128,128]{2,1,0:T(8,128)(2,1)S(1)} %pad_maximum_fusion.12), channel_id=1, source_target_pairs={{0,2},{1,3},{2,0},{3,1},{4,6},{5,7},{6,4},{7,5},{8,10},{9,11},{10,... | collective-permute-start | bytes 196616 | tf_op jit(solution)/shard_map/ppermute | solution.py:20
  106.6 4.9 %collective-permute-start.36 = (bf16[128,128]{1,0:T(8,128)(2,1)S(1)}, bf16[128,128]{1,0:T(8,128)(2,1)S(1)}, u32[]{:S(2)}, u32[]{:S(2)}) collective-permute-start(bf16[128,128]{1,0:T(8,128)(2,1)S(1)} %get-tuple-element.55), channel_id=1, source_target_pairs={{0,24},{1,25},{2,26},{3,27},{4,28},{5,29},{6,30},{7,31},{8,16},{9,... | collective-permute-start | bytes 98312 | tf_op jit(solution)/shard_map/ppermute | solution.py:20
  108.9 3.9 %collective-permute-start.37 = (bf16[128,128]{1,0:T(8,128)(2,1)S(1)}, bf16[128,128]{1,0:T(8,128)(2,1)S(1)}, u32[]{:S(2)}, u32[]{:S(2)}) collective-permute-start(bf16[128,128]{1,0:T(8,128)(2,1)S(1)} %get-tuple-element.57), channel_id=1, source_target_pairs={{0,16},{1,17},{2,18},{3,19},{4,20},{5,21},{6,22},{7,23},{8,24},{9,... | collective-permute-start | bytes 98312 | tf_op jit(solution)/shard_map/ppermute | solution.py:20
  109.5 3.9 %collective-permute-start.38 = (bf16[128,128]{1,0:T(8,128)(2,1)S(1)}, bf16[128,128]{1,0:T(8,128)(2,1)S(1)}, u32[]{:S(2)}, u32[]{:S(2)}) collective-permute-start(bf16[128,128]{1,0:T(8,128)(2,1)S(1)} %get-tuple-element.56), channel_id=1, source_target_pairs={{0,8},{1,9},{2,10},{3,11},{4,12},{5,13},{6,14},{7,15},{8,0},{9,1},... | collective-permute-start | bytes 98312 | tf_op jit(solution)/shard_map/ppermute | solution.py:20
  110.1 4.0 %collective-permute-start.22 = (bf16[64,128]{1,0:T(8,128)(2,1)S(1)}, bf16[64,128]{1,0:T(8,128)(2,1)S(1)}, u32[]{:S(2)}, u32[]{:S(2)}) collective-permute-start(bf16[64,128]{1,0:T(8,128)(2,1)S(1)} %constant_dynamic-slice_fusion.17), channel_id=1, source_target_pairs={{0,1},{1,0},{2,3},{3,2},{4,5},{5,4},{6,7},{7,6},{8,9},{9,8},{10,11... | collective-permute-start | bytes 49160 | tf_op jit(solution)/shard_map/ppermute | solution.py:20
  (30 other events, 207.0 us)

commit v4 on v3

--- a/solution.py
+++ b/solution.py
@@ -32,18 +32,24 @@
     return [pl.BlockSpec(memory_space=pltpu.VMEM)] * count
 
 
+def split_masks(blks):
+    last = [2, 3, blks - 2, blks - 1]
+    return [mask for mask in range(blks) if mask not in last], last
+
+
 def leaf_partial(pieces, near, far):
     masks = sorted(pieces)
     count = len(masks)
     rows, half = pieces[0].shape
     total = near.shape[1]
-    block = 4 * rows
-    flip = total // block - 1
+    chips = total // (2 * rows)
     dtype = near.dtype
 
     def body(*refs):
         piece_refs = refs[:count]
-        near_ref, far_ref, sum_ref, rest_ref, rhs, near_vmem, far_vmem, sems = refs[count:]
+        near_ref, far_ref, sum_ref = refs[count : count + 3]
+        rests = refs[count + 3 : count + 5]
+        rhs, near_vmem, far_vmem, sems = refs[count + 5 :]
         b = lax.axis_index("blk")
         copies = [
             pltpu.make_async_copy(source, target, sems.at[i])
@@ -51,23 +57,29 @@
         ]
         for copy in copies:
             copy.start()
-        missing = pl.multiple_of((b // 4 ^ flip) * block, 128)
-        rhs[pl.ds(missing, block)] = jnp.zeros((block, half), dtype)
+        missing = [
+            pl.multiple_of((b // 2 ^ flip) * 2 * rows, 128) for flip in (1, chips - 1)
+        ]
+        for where in missing:
+            rhs[pl.ds(where, 2 * rows)] = jnp.zeros((2 * rows, half), dtype)
         for mask, piece_ref in zip(masks, piece_refs):
             where = pl.multiple_of((b ^ mask) * rows, 16)
             rhs[pl.ds(where, rows)] = piece_ref[...]
         for i, matrix in enumerate((near_vmem, far_vmem)):
             copies[i].wait()
             sum_ref[i] = jnp.dot(matrix[...], rhs[...], preferred_element_type=jnp.float32)
-        rest_ref[...] = near_vmem[:, pl.ds(missing, block)]
+            for j, where in enumerate(missing):
+                columns = pl.ds(j * 2 * rows, 2 * rows)
+                rests[i][:, columns] = matrix[:, pl.ds(where, 2 * rows)]
 
     return pl.pallas_call(
         body,
         in_specs=vmem_specs(count) + [pl.BlockSpec(memory_space=pltpu.HBM)] * 2,
-        out_specs=vmem_specs(2),
+        out_specs=vmem_specs(3),
         out_shape=[
             pltpu.VMEM((2, rows, half), jnp.float32),
-            pltpu.VMEM((rows, block), dtype),
+            pltpu.VMEM((rows, 4 * rows), dtype),
+            pltpu.VMEM((rows, 4 * rows), dtype),
         ],
         scratch_shapes=[
             pltpu.VMEM((total, half), dtype),
@@ -86,54 +98,41 @@
     )
 
 
-def leaf_finish(pieces, sums, rest, far):
+def leaf_finish(pieces, sums, rests):
     count = len(pieces)
     rows, half = pieces[0].shape
     dtype = pieces[0].dtype
-    flip = far.shape[1] // (count * rows) - 1
 
     def body(*refs):
         piece_refs = refs[:count]
-        sum_ref, rest_ref, far_ref, all_ref, mine_ref, other_ref, rhs, far_vmem, sem = refs[count:]
-        b = lax.axis_index("blk")
-        where = pl.multiple_of((b // count ^ flip) * count * rows, 128)
-        copy = pltpu.make_async_copy(far_ref.at[:, pl.ds(where, count * rows)], far_vmem, sem)
-        copy.start()
-        for mask, piece_ref in enumerate(piece_refs):
-            where = pl.multiple_of((b % count ^ mask) * rows, 16)
+        sum_ref = refs[count]
+        rest_refs = refs[count + 1 : count + 3]
+        all_ref, mine_ref, other_ref, rhs = refs[count + 3 :]
+        core = lax.axis_index("blk") % 2
+        for i, piece_ref in enumerate(piece_refs):
+            where = pl.multiple_of((i // 2 * 2 + (core ^ i % 2)) * rows, 16)
             rhs[pl.ds(where, rows)] = piece_ref[...]
-        for i, (matrix, out_ref) in enumerate(((rest_ref, mine_ref), (far_vmem, other_ref))):
-            if i == 1:
-                copy.wait()
-            value = jnp.dot(matrix[...], rhs[...], preferred_element_type=jnp.float32)
+        for i, out_ref in enumerate((mine_ref, other_ref)):
+            value = jnp.dot(rest_refs[i][...], rhs[...], preferred_element_type=jnp.float32)
             value = (value + sum_ref[i]).astype(dtype)
             out_ref[...] = value
-            all_ref[pl.ds(pl.multiple_of((b % 2 ^ i) * rows, 16), rows)] = value
+            all_ref[pl.ds(pl.multiple_of((core ^ i) * rows, 16), rows)] = value
 
     return pl.pallas_call(
         body,
-        in_specs=vmem_specs(count + 2) + [pl.BlockSpec(memory_space=pltpu.HBM)],
+        in_specs=vmem_specs(count + 3),
         out_specs=vmem_specs(3),
         out_shape=[
             pltpu.VMEM((2 * rows, half), dtype),
             pltpu.VMEM((rows, half), dtype),
             pltpu.VMEM((rows, half), dtype),
         ],
-        scratch_shapes=[
-            pltpu.VMEM((count * rows, half), dtype),
-            pltpu.VMEM((rows, count * rows), dtype),
-            pltpu.SemaphoreType.DMA,
-        ],
+        scratch_shapes=[pltpu.VMEM((count * rows, half), dtype)],
         cost_estimate=pl.CostEstimate(
             flops=4 * rows * count * rows * half, bytes_accessed=0, transcendentals=0
         ),
         name="leaf_finish",
-    )(
-        *[on_chip(value) for value in pieces],
-        on_chip(sums),
-        on_chip(rest),
-        pltpu.with_memory_space_constraint(far, pltpu.HBM),
-    )
+    )(*[on_chip(value) for value in pieces], on_chip(sums), *[on_chip(value) for value in rests])
 
 
 def column_halves(value):
@@ -201,9 +200,10 @@
     inverse_other = exchange(leaf_inverse, 0, 1)
     own_half, other_half = column_halves(leaf_rhs)
     arrived = {0: own_half}
-    far = list(range(blks - 4, blks))
-    for mask in far[::-1] + [m for m in range(blks - 5, 1, -1)] + [1]:
+    soon, last = split_masks(blks)
+    for mask in soon[:0:-1] + last[::-1]:
         arrived[mask] = exchange(own_half if mask % 2 == 0 else other_half, 0, mask)
+
     inverse_rows = [sep_inverse]
     for a in range(1, leaves):
         value = sep_inverse
@@ -211,10 +211,11 @@
             value = jnp.concatenate([value[:, : 2 * base_width], leaf_columns(value, k ^ a)], 1)
         inverse_rows.append(exchange(value, a, 0))
 
-    last = [arrived.pop(mask) for mask in far]
-    sums, beside = leaf_partial(arrived, leaf_inverse, inverse_other)
-    s_all, s_mine, s_other = leaf_finish(last, sums, beside, inverse_other)
-    got = [(m, exchange(s_all, 0, m)) for m in range(blks - 2, 0, -2)]
+    pieces = [arrived.pop(mask) for mask in last]
+    sums, *beside = leaf_partial(arrived, leaf_inverse, inverse_other)
+    s_all, s_mine, s_other = leaf_finish(pieces, sums, beside)
+    zorder = [m for m in range(blks - 4, 2, -2)] + [blks - 2, 2]
+    got = [(m, exchange(s_all, 0, m)) for m in zorder]
     slot_other = exchange(slot_map, 0, 1)
     sep_rhs_other = exchange(sep_rhs, 0, 1)
     lower_other = exchange(leaf_lower, 0, 1)

time: 116 us -> 114 us (0.983)
  other arithmetic: 10.7 us -> 6.41 us
  waiting for transfers between devices: 49 us -> 53.1 us
  Pallas kernels: 6.66 us -> 5.26 us
    ppermute x40, waiting for transfers between devices: 49 us -> 53.1 us  [exchange(): return lax.ppermute(value, ('leaf', 'blk'), pairs)]
    eq x4, other arithmetic: 2.36 us -> 0.04 us  [mix(): hit = (targets == t)[:, :, None, None]]
    pallas_call x1, Pallas kernels: 2.08 us -> 0.63 us  [leaf_finish(): pl.pallas_call(body, in_specs=vmem_specs(count + 3), out_specs=vmem_specs...]
    select_n x6, other arithmetic: 4.82 us -> 3.48 us  [in_order(): first = jnp.where(core == 0, mine, other)]
  transfers between devices with their start and end apart: 40 -> 40, of which waited for: 19 -> 21; matrix products, arithmetic and copies ran while one was open for 12% -> 9% of each run, Pallas kernels for 5% -> 4%
where the time goes in v4:
time: 114 us; the launch traced here: 113 us
  waiting for transfers between devices  53.1 us (47%)
  starting transfers between devices  39.7 us (35%)
  other arithmetic  6.41 us (6%)
  Pallas kernels  5.26 us (5%)
  matrix products  3.98 us (3%)
  local copies, waits for them, and re-layouts  3.58 us (3%)
  between operations  1.26 us (1%)
    ppermute x40, waiting for transfers between devices, exchange(): return lax.ppermute(value, ('leaf', 'blk'), pairs)  53.1 us
    ppermute x40, starting transfers between devices, exchange(): return lax.ppermute(value, ('leaf', 'blk'), pairs)  39.7 us
    dot_general x6, matrix products, product(): return jnp.dot(matrix, vectors, preferred_element_type=jnp.float32)  3.98 us
    pallas_call x1, Pallas kernels, leaf_partial(): pl.pallas_call(body, in_specs=vmem_specs(count) + [pl.BlockSpec(memory_sp...  3.56 us
    select_n x6, other arithmetic, in_order(): first = jnp.where(core == 0, mine, other)  3.48 us
  transfers between devices with their start and end apart: 40, of which 21 were waited for; matrix products, arithmetic and copies ran while one was open for 9% of the time, Pallas kernels for 4%

profile of v4, /device:TPU:0, one launch (start us, length us, event | category | flops | bytes accessed | tf_op | source)
XLA Modules:
  0.0 113.4 jit_solution(210760440942072269)
XLA Ops:
  2.3 3.7 %collective-permute-start.6 = (bf16[320,128]{1,0:T(8,128)(2,1)S(1)}, bf16[320,128]{1,0:T(8,128)(2,1)S(1)}, u32[]{:S(2)}, u32[]{:S(2)}) collective-permute-start(bf16[320,128]{1,0:T(8,128)(2,1)S(1)} %get-tuple-element.11), channel_id=1, source_target_pairs={{0,5},{1,4},{2,7},{3,6},{4,1},{5,0},{6,3},{7,2},{8,13},{9,12},{10,... | collective-permute-start | bytes 245768 | tf_op jit(solution)/shard_map/ppermute | solution.py:20
  8.2 1.6 %collective-permute-start.13 = (s32[2,2]{1,0:T(2,128)S(1)}, s32[2,2]{1,0:T(2,128)S(1)}, u32[]{:S(2)}, u32[]{:S(2)}) collective-permute-start(s32[2,2]{1,0:T(2,128)S(1)} %get-tuple-element.32), channel_id=1, source_target_pairs={{0,8},{1,9},{2,10},{3,11},{4,12},{5,13},{6,14},{7,15},{8,0},{9,1},... | collective-permute-start | bytes 56 | tf_op jit(solution)/shard_map/ppermute | solution.py:20
  9.7 2.1 %collective-permute-done.13 = s32[2,2]{1,0:T(2,128)S(1)} collective-permute-done((s32[2,2]{1,0:T(2,128)S(1)}, s32[2,2]{1,0:T(2,128)S(1)}, u32[]{:S(2)}, u32[]{:S(2)}) %collective-permute-start.13) | collective-permute-done | bytes 48 | tf_op jit(solution)/shard_map/ppermute | solution.py:20
  11.8 1.6 %collective-permute-start.23 = (bf16[64,3072]{1,0:T(8,128)(2,1)}, bf16[64,3072]{1,0:T(8,128)(2,1)S(1)}, u32[]{:S(2)}, u32[]{:S(2)}) collective-permute-start(bf16[64,3072]{1,0:T(8,128)(2,1)} %param.11), channel_id=1, source_target_pairs={{0,8},{1,9},{2,10},{3,11},{4,12},{5,13},{6,14},{7,15},{8,0},{9,1},... | collective-permute-start | bytes 1179656 | tf_op jit(solution)/shard_map/ppermute | solution.py:20
  14.2 1.6 %collective-permute-start.25 = (bf16[64,3072]{1,0:T(8,128)(2,1)}, bf16[64,3072]{1,0:T(8,128)(2,1)S(1)}, u32[]{:S(2)}, u32[]{:S(2)}) collective-permute-start(bf16[64,3072]{1,0:T(8,128)(2,1)} %param.11), channel_id=1, source_target_pairs={{0,16},{1,17},{2,18},{3,19},{4,20},{5,21},{6,22},{7,23},{8,24},{9,... | collective-permute-start | bytes 1179656 | tf_op jit(solution)/shard_map/ppermute | solution.py:20
  15.8 1.8 %broadcast_select_fusion.1 = (bf16[128,1024]{1,0:T(8,128)(2,1)}, bf16[128,1024]{1,0:T(8,128)(2,1)}) fusion(bf16[128,1024]{1,0:T(8,128)(2,1)} %param.12, bf16[128,1024]{1,0:T(8,128)(2,1)S(1)} %collective-permute-done.29, pred[]{:T(512)S(6)} %eq.94), kind=kLoop, calls=%fused_computation.13 | loop fusion | flops 262144 | bytes 1048577 | tf_op jit(solution)/shard_map/jit(_where)/select_n | solution.py:182
  18.4 5.7 %collective-permute-done.23 = bf16[64,3072]{1,0:T(8,128)(2,1)S(1)} collective-permute-done((bf16[64,3072]{1,0:T(8,128)(2,1)}, bf16[64,3072]{1,0:T(8,128)(2,1)S(1)}, u32[]{:S(2)}, u32[]{:S(2)}) %collective-permute-start.23) | collective-permute-done | bytes 393248 | tf_op jit(solution)/shard_map/ppermute | solution.py:20
  24.1 10.0 %collective-permute-done.25 = bf16[64,3072]{1,0:T(8,128)(2,1)S(1)} collective-permute-done((bf16[64,3072]{1,0:T(8,128)(2,1)}, bf16[64,3072]{1,0:T(8,128)(2,1)S(1)}, u32[]{:S(2)}, u32[]{:S(2)}) %collective-permute-start.25) | collective-permute-done | bytes 393248 | tf_op jit(solution)/shard_map/ppermute | solution.py:20
  37.6 1.6 %collective-permute-start = (bf16[320,128]{1,0:T(8,128)(2,1)S(1)}, bf16[320,128]{1,0:T(8,128)(2,1)S(1)}, u32[]{:S(2)}, u32[]{:S(2)}) collective-permute-start(bf16[320,128]{1,0:T(8,128)(2,1)S(1)} %get-tuple-element.10.refs_0_), channel_id=1, source_target_pairs={{0,2},{1,3},{2,0},{3,1},{4,6},{5,7},{6,4},{7,5},{8,10},{9,11},{10,... | collective-permute-start | bytes 245768 | tf_op jit(solution)/shard_map/ppermute | solution.py:20
  39.5 5.1 %collective-permute-done.5.refs_2_ = bf16[320,128]{1,0:T(8,128)(2,1)S(1)} collective-permute-done((bf16[320,128]{1,0:T(8,128)(2,1)S(1)}, bf16[320,128]{1,0:T(8,128)(2,1)S(1)}, u32[]{:S(2)}, u32[]{:S(2)}) %collective-permute-start.5) | collective-permute-done | bytes 81952 | tf_op jit(solution)/shard_map/ppermute | solution.py:20
  48.9 1.8 %collective-permute-start.17 = (bf16[128,2560]{1,0:T(8,128)(2,1)}, bf16[128,2560]{1,0:T(8,128)(2,1)}, u32[]{:S(2)}, u32[]{:S(2)}) collective-permute-start(bf16[128,2560]{1,0:T(8,128)(2,1)} %param.9), channel_id=1, source_target_pairs={{0,1},{1,0},{2,3},{3,2},{4,5},{5,4},{6,7},{7,6},{8,9},{9,8},{10,11... | collective-permute-start | bytes 1966088 | tf_op jit(solution)/shard_map/ppermute | solution.py:20
  50.7 3.6 %leaf_partial.1 = (f32[2,320,128]{2,1,0:T(8,128)S(1)}, bf16[320,1280]{1,0:T(8,128)(2,1)S(1)}, bf16[320,1280]{1,0:T(8,128)(2,1)S(1)}) custom-call(bf16[320,128]{1,0:T(8,128)(2,1)S(1)} %get-tuple-element.10.refs_0_, bf16[320,128]{1,0:T(8,128)(2,1)S(1)} %collective-permute-done.4.refs_1_, bf16[320,128]{1,0:T(8,128)(2,1)S(1)} %collective-permute-done.5.refs_2_, ...), custom_call_target="tpu_custom_call" | custom-call | flops 419430400 | bytes 3276800 | tf_op jit(solution)/shard_map/leaf_partial/pallas_call | solution.py:75
  58.3 2.2 %collective-permute-start.16 = (bf16[640,128]{1,0:T(8,128)(2,1)S(1)}, bf16[640,128]{1,0:T(8,128)(2,1)S(1)}, u32[]{:S(2)}, u32[]{:S(2)}) collective-permute-start(bf16[640,128]{1,0:T(8,128)(2,1)S(1)} %get-tuple-element.17), channel_id=1, source_target_pairs={{0,2},{1,3},{2,0},{3,1},{4,6},{5,7},{6,4},{7,5},{8,10},{9,11},{10,... | collective-permute-start | bytes 491528 | tf_op jit(solution)/shard_map/ppermute | solution.py:20
  60.5 7.7 %collective-permute-done.14 = bf16[640,128]{1,0:T(8,128)(2,1)S(1)} collective-permute-done((bf16[640,128]{1,0:T(8,128)(2,1)S(1)}, bf16[640,128]{1,0:T(8,128)(2,1)S(1)}, u32[]{:S(2)}, u32[]{:S(2)}) %collective-permute-start.14) | collective-permute-done | bytes 163872 | tf_op jit(solution)/shard_map/ppermute | solution.py:20
  68.2 3.0 %collective-permute-done.16 = bf16[640,128]{1,0:T(8,128)(2,1)S(1)} collective-permute-done((bf16[640,128]{1,0:T(8,128)(2,1)S(1)}, bf16[640,128]{1,0:T(8,128)(2,1)S(1)}, u32[]{:S(2)}, u32[]{:S(2)}) %collective-permute-start.16) | collective-permute-done | bytes 163872 | tf_op jit(solution)/shard_map/ppermute | solution.py:20
  71.3 1.4 %fusion.34 = f32[128,128]{0,1:T(8,128)S(1)} fusion(bf16[128,2560]{1,0:T(8,128)(2,1)} %collective-permute-done.17, bf16[2560,128]{1,0:T(8,128)(2,1)S(1)} %constant_dynamic-update-slice_fusion), kind=kOutput, calls=%fused_computation.148 | convolution fusion | flops 83886080 | bytes 1376256 | tf_op jit(solution)/shard_map/dot_general | solution.py:24
  72.7 1.4 %select_bitcast_fusion.1 = (f32[128,128]{1,0:T(8,128)S(1)}, f32[128,128]{1,0:T(8,128)S(1)}) fusion(f32[128,128]{0,1:T(8,128)S(1)} %fusion.34, pred[]{:T(512)S(6)} %eq.94, bf16[128,2560]{1,0:T(8,128)(2,1)} %param.9, bf16[2560,128]{1,0:T(8,128)(2,1)S(1)} %constant_dynamic-update-slice_fusion), kind=kOutput, calls=%fused_computation.87 | convolution fusion | flops 83918848 | bytes 1507329 | tf_op jit(solution)/shard_map/dot_general | solution.py:24
  74.2 1.4 %collective-permute-start.18 = (bf16[2,2,64,128]{3,2,1,0:T(8,128)(2,1)S(1)}, bf16[2,2,64,128]{3,2,1,0:T(8,128)(2,1)S(1)}, u32[]{:S(2)}, u32[]{:S(2)}) collective-permute-start(bf16[2,2,64,128]{3,2,1,0:T(8,128)(2,1)S(1)} %get-tuple-element.62), channel_id=1, source_target_pairs={{0,8},{1,9},{2,10},{3,11},{4,12},{5,13},{6,14},{7,15},{8,0},{9,1},... | collective-permute-start | bytes 196616 | tf_op jit(solution)/shard_map/ppermute | solution.py:20
  75.7 2.8 %collective-permute-done.18 = bf16[2,2,64,128]{3,2,1,0:T(8,128)(2,1)S(1)} collective-permute-done((bf16[2,2,64,128]{3,2,1,0:T(8,128)(2,1)S(1)}, bf16[2,2,64,128]{3,2,1,0:T(8,128)(2,1)S(1)}, u32[]{:S(2)}, u32[]{:S(2)}) %collective-permute-start.18) | collective-permute-done | bytes 65568 | tf_op jit(solution)/shard_map/ppermute | solution.py:20
  78.7 2.5 %collective-permute-start.19 = (bf16[2,128,128]{2,1,0:T(8,128)(2,1)S(1)}, bf16[2,128,128]{2,1,0:T(8,128)(2,1)S(1)}, u32[]{:S(2)}, u32[]{:S(2)}) collective-permute-start(bf16[2,128,128]{2,1,0:T(8,128)(2,1)S(1)} %pad_maximum_fusion.10), channel_id=1, source_target_pairs={{0,6},{1,7},{2,4},{3,5},{4,2},{5,3},{6,0},{7,1},{8,14},{9,15},{10,... | collective-permute-start | bytes 196616 | tf_op jit(solution)/shard_map/ppermute | solution.py:20
  81.1 2.0 %collective-permute-start.21 = (bf16[2,128,128]{2,1,0:T(8,128)(2,1)S(1)}, bf16[2,128,128]{2,1,0:T(8,128)(2,1)S(1)}, u32[]{:S(2)}, u32[]{:S(2)}) collective-permute-start(bf16[2,128,128]{2,1,0:T(8,128)(2,1)S(1)} %pad_maximum_fusion.10), channel_id=1, source_target_pairs={{0,2},{1,3},{2,0},{3,1},{4,6},{5,7},{6,4},{7,5},{8,10},{9,11},{10,... | collective-permute-start | bytes 196616 | tf_op jit(solution)/shard_map/ppermute | solution.py:20
  83.3 2.2 %collective-permute-done.19 = bf16[2,128,128]{2,1,0:T(8,128)(2,1)S(1)} collective-permute-done((bf16[2,128,128]{2,1,0:T(8,128)(2,1)S(1)}, bf16[2,128,128]{2,1,0:T(8,128)(2,1)S(1)}, u32[]{:S(2)}, u32[]{:S(2)}) %collective-permute-start.19) | collective-permute-done | bytes 65568 | tf_op jit(solution)/shard_map/ppermute | solution.py:20
  87.4 2.2 %collective-permute-start.30 = (bf16[2,128,128]{2,1,0:T(8,128)(2,1)S(1)}, bf16[2,128,128]{2,1,0:T(8,128)(2,1)S(1)}, u32[]{:S(2)}, u32[]{:S(2)}) collective-permute-start(bf16[2,128,128]{2,1,0:T(8,128)(2,1)S(1)} %pad_maximum_fusion.11), channel_id=1, source_target_pairs={{0,6},{1,7},{2,4},{3,5},{4,2},{5,3},{6,0},{7,1},{8,14},{9,15},{10,... | collective-permute-start | bytes 196616 | tf_op jit(solution)/shard_map/ppermute | solution.py:20
  89.6 2.3 %collective-permute-start.32 = (bf16[2,128,128]{2,1,0:T(8,128)(2,1)S(1)}, bf16[2,128,128]{2,1,0:T(8,128)(2,1)S(1)}, u32[]{:S(2)}, u32[]{:S(2)}) collective-permute-start(bf16[2,128,128]{2,1,0:T(8,128)(2,1)S(1)} %pad_maximum_fusion.11), channel_id=1, source_target_pairs={{0,2},{1,3},{2,0},{3,1},{4,6},{5,7},{6,4},{7,5},{8,10},{9,11},{10,... | collective-permute-start | bytes 196616 | tf_op jit(solution)/shard_map/ppermute | solution.py:20
  92.0 2.1 %collective-permute-done.30 = bf16[2,128,128]{2,1,0:T(8,128)(2,1)S(1)} collective-permute-done((bf16[2,128,128]{2,1,0:T(8,128)(2,1)S(1)}, bf16[2,128,128]{2,1,0:T(8,128)(2,1)S(1)}, u32[]{:S(2)}, u32[]{:S(2)}) %collective-permute-start.30) | collective-permute-done | bytes 65568 | tf_op jit(solution)/shard_map/ppermute | solution.py:20
  94.1 1.4 %collective-permute-done.31 = bf16[2,128,128]{2,1,0:T(8,128)(2,1)S(1)} collective-permute-done((bf16[2,128,128]{2,1,0:T(8,128)(2,1)S(1)}, bf16[2,128,128]{2,1,0:T(8,128)(2,1)S(1)}, u32[]{:S(2)}, u32[]{:S(2)}) %collective-permute-start.31) | collective-permute-done | bytes 65568 | tf_op jit(solution)/shard_map/ppermute | solution.py:20
  96.0 2.5 %collective-permute-start.33 = (bf16[2,128,128]{2,1,0:T(8,128)(2,1)S(1)}, bf16[2,128,128]{2,1,0:T(8,128)(2,1)S(1)}, u32[]{:S(2)}, u32[]{:S(2)}) collective-permute-start(bf16[2,128,128]{2,1,0:T(8,128)(2,1)S(1)} %pad_maximum_fusion.12), channel_id=1, source_target_pairs={{0,6},{1,7},{2,4},{3,5},{4,2},{5,3},{6,0},{7,1},{8,14},{9,15},{10,... | collective-permute-start | bytes 196616 | tf_op jit(solution)/shard_map/ppermute | solution.py:20
  98.5 1.9 %collective-permute-start.35 = (bf16[2,128,128]{2,1,0:T(8,128)(2,1)S(1)}, bf16[2,128,128]{2,1,0:T(8,128)(2,1)S(1)}, u32[]{:S(2)}, u32[]{:S(2)}) collective-permute-start(bf16[2,128,128]{2,1,0:T(8,128)(2,1)S(1)} %pad_maximum_fusion.12), channel_id=1, source_target_pairs={{0,2},{1,3},{2,0},{3,1},{4,6},{5,7},{6,4},{7,5},{8,10},{9,11},{10,... | collective-permute-start | bytes 196616 | tf_op jit(solution)/shard_map/ppermute | solution.py:20
  100.5 1.7 %collective-permute-done.33 = bf16[2,128,128]{2,1,0:T(8,128)(2,1)S(1)} collective-permute-done((bf16[2,128,128]{2,1,0:T(8,128)(2,1)S(1)}, bf16[2,128,128]{2,1,0:T(8,128)(2,1)S(1)}, u32[]{:S(2)}, u32[]{:S(2)}) %collective-permute-start.33) | collective-permute-done | bytes 65568 | tf_op jit(solution)/shard_map/ppermute | solution.py:20
  102.3 1.8 %collective-permute-done.34 = bf16[2,128,128]{2,1,0:T(8,128)(2,1)S(1)} collective-permute-done((bf16[2,128,128]{2,1,0:T(8,128)(2,1)S(1)}, bf16[2,128,128]{2,1,0:T(8,128)(2,1)S(1)}, u32[]{:S(2)}, u32[]{:S(2)}) %collective-permute-start.34) | collective-permute-done | bytes 65568 | tf_op jit(solution)/shard_map/ppermute | solution.py:20
  104.6 2.3 %collective-permute-start.36 = (bf16[128,128]{1,0:T(8,128)(2,1)S(1)}, bf16[128,128]{1,0:T(8,128)(2,1)S(1)}, u32[]{:S(2)}, u32[]{:S(2)}) collective-permute-start(bf16[128,128]{1,0:T(8,128)(2,1)S(1)} %get-tuple-element.57), channel_id=1, source_target_pairs={{0,24},{1,25},{2,26},{3,27},{4,28},{5,29},{6,30},{7,31},{8,16},{9,... | collective-permute-start | bytes 98312 | tf_op jit(solution)/shard_map/ppermute | solution.py:20
  109.5 1.4 %collective-permute-done.37 = bf16[128,128]{1,0:T(8,128)(2,1)S(1)} collective-permute-done((bf16[128,128]{1,0:T(8,128)(2,1)S(1)}, bf16[128,128]{1,0:T(8,128)(2,1)S(1)}, u32[]{:S(2)}, u32[]{:S(2)}) %collective-permute-start.37) | collective-permute-done | bytes 32800 | tf_op jit(solution)/shard_map/ppermute | solution.py:20
  (142 shorter events, 25.8 us)
Async XLA Ops:
  1.7 37.5 %collective-permute-start.4 = (bf16[320,128]{1,0:T(8,128)(2,1)S(1)}, bf16[320,128]{1,0:T(8,128)(2,1)S(1)}, u32[]{:S(2)}, u32[]{:S(2)}) collective-permute-start(bf16[320,128]{1,0:T(8,128)(2,1)S(1)} %get-tuple-element.11), channel_id=1, source_target_pairs={{0,1},{1,0},{2,3},{3,2},{4,5},{5,4},{6,7},{7,6},{8,9},{9,8},{10,11... | collective-permute-start | bytes 245768 | tf_op jit(solution)/shard_map/ppermute | solution.py:20
  2.3 43.5 %collective-permute-start.6 = (bf16[320,128]{1,0:T(8,128)(2,1)S(1)}, bf16[320,128]{1,0:T(8,128)(2,1)S(1)}, u32[]{:S(2)}, u32[]{:S(2)}) collective-permute-start(bf16[320,128]{1,0:T(8,128)(2,1)S(1)} %get-tuple-element.11), channel_id=1, source_target_pairs={{0,5},{1,4},{2,7},{3,6},{4,1},{5,0},{6,3},{7,2},{8,13},{9,12},{10,... | collective-permute-start | bytes 245768 | tf_op jit(solution)/shard_map/ppermute | solution.py:20
  6.0 5.8 %collective-permute-start.10 = (bf16[2,64,256]{2,1,0:T(8,128)(2,1)}, bf16[2,64,256]{2,1,0:T(8,128)(2,1)S(1)}, u32[]{:S(2)}, u32[]{:S(2)}) collective-permute-start(bf16[2,64,256]{2,1,0:T(8,128)(2,1)} %param.10), channel_id=1, source_target_pairs={{0,1},{1,0},{2,3},{3,2},{4,5},{5,4},{6,7},{7,6},{8,9},{9,8},{10,11... | collective-permute-start | bytes 196616 | tf_op jit(solution)/shard_map/ppermute | solution.py:20
  6.5 11.1 %collective-permute-start.9 = (bf16[64,3072]{1,0:T(8,128)(2,1)}, bf16[64,3072]{1,0:T(8,128)(2,1)S(1)}, u32[]{:S(2)}, u32[]{:S(2)}) collective-permute-start(bf16[64,3072]{1,0:T(8,128)(2,1)} %param.11), channel_id=1, source_target_pairs={{0,1},{1,0},{2,3},{3,2},{4,5},{5,4},{6,7},{7,6},{8,9},{9,8},{10,11... | collective-permute-start | bytes 1179656 | tf_op jit(solution)/shard_map/ppermute | solution.py:20
  11.8 12.3 %collective-permute-start.23 = (bf16[64,3072]{1,0:T(8,128)(2,1)}, bf16[64,3072]{1,0:T(8,128)(2,1)S(1)}, u32[]{:S(2)}, u32[]{:S(2)}) collective-permute-start(bf16[64,3072]{1,0:T(8,128)(2,1)} %param.11), channel_id=1, source_target_pairs={{0,8},{1,9},{2,10},{3,11},{4,12},{5,13},{6,14},{7,15},{8,0},{9,1},... | collective-permute-start | bytes 1179656 | tf_op jit(solution)/shard_map/ppermute | solution.py:20
  14.2 19.9 %collective-permute-start.25 = (bf16[64,3072]{1,0:T(8,128)(2,1)}, bf16[64,3072]{1,0:T(8,128)(2,1)S(1)}, u32[]{:S(2)}, u32[]{:S(2)}) collective-permute-start(bf16[64,3072]{1,0:T(8,128)(2,1)} %param.11), channel_id=1, source_target_pairs={{0,16},{1,17},{2,18},{3,19},{4,20},{5,21},{6,22},{7,23},{8,24},{9,... | collective-permute-start | bytes 1179656 | tf_op jit(solution)/shard_map/ppermute | solution.py:20
  17.6 17.5 %collective-permute-start.27 = (bf16[64,3072]{1,0:T(8,128)(2,1)}, bf16[64,3072]{1,0:T(8,128)(2,1)S(1)}, u32[]{:S(2)}, u32[]{:S(2)}) collective-permute-start(bf16[64,3072]{1,0:T(8,128)(2,1)} %param.11), channel_id=1, source_target_pairs={{0,24},{1,25},{2,26},{3,27},{4,28},{5,29},{6,30},{7,31},{8,16},{9,... | collective-permute-start | bytes 1179656 | tf_op jit(solution)/shard_map/ppermute | solution.py:20
  24.1 22.6 %collective-permute-start.7 = (bf16[320,2560]{1,0:T(8,128)(2,1)S(1)}, bf16[320,2560]{1,0:T(8,128)(2,1)S(1)}, u32[]{:S(2)}, u32[]{:S(2)}) collective-permute-start(bf16[320,2560]{1,0:T(8,128)(2,1)S(1)} %copy-done), channel_id=1, source_target_pairs={{0,1},{1,0},{2,3},{3,2},{4,5},{5,4},{6,7},{7,6},{8,9},{9,8},{10,11... | collective-permute-start | bytes 4915208 | tf_op jit(solution)/shard_map/ppermute | solution.py:20
  37.0 7.5 %collective-permute-start.5 = (bf16[320,128]{1,0:T(8,128)(2,1)S(1)}, bf16[320,128]{1,0:T(8,128)(2,1)S(1)}, u32[]{:S(2)}, u32[]{:S(2)}) collective-permute-start(bf16[320,128]{1,0:T(8,128)(2,1)S(1)} %get-tuple-element.10.refs_0_), channel_id=1, source_target_pairs={{0,4},{1,5},{2,6},{3,7},{4,0},{5,1},{6,2},{7,3},{8,12},{9,13},{10,... | collective-permute-start | bytes 245768 | tf_op jit(solution)/shard_map/ppermute | solution.py:20
  37.6 16.7 %collective-permute-start = (bf16[320,128]{1,0:T(8,128)(2,1)S(1)}, bf16[320,128]{1,0:T(8,128)(2,1)S(1)}, u32[]{:S(2)}, u32[]{:S(2)}) collective-permute-start(bf16[320,128]{1,0:T(8,128)(2,1)S(1)} %get-tuple-element.10.refs_0_), channel_id=1, source_target_pairs={{0,2},{1,3},{2,0},{3,1},{4,6},{5,7},{6,4},{7,5},{8,10},{9,11},{10,... | collective-permute-start | bytes 245768 | tf_op jit(solution)/shard_map/ppermute | solution.py:20
  39.3 15.8 %collective-permute-start.1 = (bf16[320,128]{1,0:T(8,128)(2,1)S(1)}, bf16[320,128]{1,0:T(8,128)(2,1)S(1)}, u32[]{:S(2)}, u32[]{:S(2)}) collective-permute-start(bf16[320,128]{1,0:T(8,128)(2,1)S(1)} %get-tuple-element.11), channel_id=1, source_target_pairs={{0,3},{1,2},{2,1},{3,0},{4,7},{5,6},{6,5},{7,4},{8,11},{9,10},{10,... | collective-permute-start | bytes 245768 | tf_op jit(solution)/shard_map/ppermute | solution.py:20
  44.5 10.5 %collective-permute-start.2 = (bf16[320,128]{1,0:T(8,128)(2,1)S(1)}, bf16[320,128]{1,0:T(8,128)(2,1)S(1)}, u32[]{:S(2)}, u32[]{:S(2)}) collective-permute-start(bf16[320,128]{1,0:T(8,128)(2,1)S(1)} %get-tuple-element.10.refs_0_), channel_id=1, source_target_pairs={{0,6},{1,7},{2,4},{3,5},{4,2},{5,3},{6,0},{7,1},{8,14},{9,15},{10,... | collective-permute-start | bytes 245768 | tf_op jit(solution)/shard_map/ppermute | solution.py:20
  45.7 9.3 %collective-permute-start.3 = (bf16[320,128]{1,0:T(8,128)(2,1)S(1)}, bf16[320,128]{1,0:T(8,128)(2,1)S(1)}, u32[]{:S(2)}, u32[]{:S(2)}) collective-permute-start(bf16[320,128]{1,0:T(8,128)(2,1)S(1)} %get-tuple-element.11), channel_id=1, source_target_pairs={{0,7},{1,6},{2,5},{3,4},{4,3},{5,2},{6,1},{7,0},{8,15},{9,14},{10,... | collective-permute-start | bytes 245768 | tf_op jit(solution)/shard_map/ppermute | solution.py:20
  48.9 22.4 %collective-permute-start.17 = (bf16[128,2560]{1,0:T(8,128)(2,1)}, bf16[128,2560]{1,0:T(8,128)(2,1)}, u32[]{:S(2)}, u32[]{:S(2)}) collective-permute-start(bf16[128,2560]{1,0:T(8,128)(2,1)} %param.9), channel_id=1, source_target_pairs={{0,1},{1,0},{2,3},{3,2},{4,5},{5,4},{6,7},{7,6},{8,9},{9,8},{10,11... | collective-permute-start | bytes 1966088 | tf_op jit(solution)/shard_map/ppermute | solution.py:20
  54.3 24.3 %collective-permute-start.11 = (bf16[128,128]{1,0:T(8,128)(2,1)S(1)}, bf16[128,128]{1,0:T(8,128)(2,1)S(1)}, u32[]{:S(2)}, u32[]{:S(2)}) collective-permute-start(bf16[128,128]{1,0:T(8,128)(2,1)S(1)} %fusion.21), channel_id=1, source_target_pairs={{0,8},{1,9},{2,10},{3,11},{4,12},{5,13},{6,14},{7,15},{8,0},{9,1},... | collective-permute-start | bytes 98312 | tf_op jit(solution)/shard_map/ppermute | solution.py:20
  55.7 12.5 %collective-permute-start.14 = (bf16[640,128]{1,0:T(8,128)(2,1)S(1)}, bf16[640,128]{1,0:T(8,128)(2,1)S(1)}, u32[]{:S(2)}, u32[]{:S(2)}) collective-permute-start(bf16[640,128]{1,0:T(8,128)(2,1)S(1)} %get-tuple-element.17), channel_id=1, source_target_pairs={{0,4},{1,5},{2,6},{3,7},{4,0},{5,1},{6,2},{7,3},{8,12},{9,13},{10,... | collective-permute-start | bytes 491528 | tf_op jit(solution)/shard_map/ppermute | solution.py:20
  55.8 12.5 %collective-permute-start.15 = (bf16[640,128]{1,0:T(8,128)(2,1)S(1)}, bf16[640,128]{1,0:T(8,128)(2,1)S(1)}, u32[]{:S(2)}, u32[]{:S(2)}) collective-permute-start(bf16[640,128]{1,0:T(8,128)(2,1)S(1)} %get-tuple-element.17), channel_id=1, source_target_pairs={{0,6},{1,7},{2,4},{3,5},{4,2},{5,3},{6,0},{7,1},{8,14},{9,15},{10,... | collective-permute-start | bytes 491528 | tf_op jit(solution)/shard_map/ppermute | solution.py:20
  58.3 13.0 %collective-permute-start.16 = (bf16[640,128]{1,0:T(8,128)(2,1)S(1)}, bf16[640,128]{1,0:T(8,128)(2,1)S(1)}, u32[]{:S(2)}, u32[]{:S(2)}) collective-permute-start(bf16[640,128]{1,0:T(8,128)(2,1)S(1)} %get-tuple-element.17), channel_id=1, source_target_pairs={{0,2},{1,3},{2,0},{3,1},{4,6},{5,7},{6,4},{7,5},{8,10},{9,11},{10,... | collective-permute-start | bytes 491528 | tf_op jit(solution)/shard_map/ppermute | solution.py:20
  74.2 4.3 %collective-permute-start.18 = (bf16[2,2,64,128]{3,2,1,0:T(8,128)(2,1)S(1)}, bf16[2,2,64,128]{3,2,1,0:T(8,128)(2,1)S(1)}, u32[]{:S(2)}, u32[]{:S(2)}) collective-permute-start(bf16[2,2,64,128]{3,2,1,0:T(8,128)(2,1)S(1)} %get-tuple-element.62), channel_id=1, source_target_pairs={{0,8},{1,9},{2,10},{3,11},{4,12},{5,13},{6,14},{7,15},{8,0},{9,1},... | collective-permute-start | bytes 196616 | tf_op jit(solution)/shard_map/ppermute | solution.py:20
  78.7 6.8 %collective-permute-start.19 = (bf16[2,128,128]{2,1,0:T(8,128)(2,1)S(1)}, bf16[2,128,128]{2,1,0:T(8,128)(2,1)S(1)}, u32[]{:S(2)}, u32[]{:S(2)}) collective-permute-start(bf16[2,128,128]{2,1,0:T(8,128)(2,1)S(1)} %pad_maximum_fusion.10), channel_id=1, source_target_pairs={{0,6},{1,7},{2,4},{3,5},{4,2},{5,3},{6,0},{7,1},{8,14},{9,15},{10,... | collective-permute-start | bytes 196616 | tf_op jit(solution)/shard_map/ppermute | solution.py:20
  81.1 5.8 %collective-permute-start.20 = (bf16[2,128,128]{2,1,0:T(8,128)(2,1)S(1)}, bf16[2,128,128]{2,1,0:T(8,128)(2,1)S(1)}, u32[]{:S(2)}, u32[]{:S(2)}) collective-permute-start(bf16[2,128,128]{2,1,0:T(8,128)(2,1)S(1)} %pad_maximum_fusion.10), channel_id=1, source_target_pairs={{0,4},{1,5},{2,6},{3,7},{4,0},{5,1},{6,2},{7,3},{8,12},{9,13},{10,... | collective-permute-start | bytes 196616 | tf_op jit(solution)/shard_map/ppermute | solution.py:20
  81.1 5.8 %collective-permute-start.21 = (bf16[2,128,128]{2,1,0:T(8,128)(2,1)S(1)}, bf16[2,128,128]{2,1,0:T(8,128)(2,1)S(1)}, u32[]{:S(2)}, u32[]{:S(2)}) collective-permute-start(bf16[2,128,128]{2,1,0:T(8,128)(2,1)S(1)} %pad_maximum_fusion.10), channel_id=1, source_target_pairs={{0,2},{1,3},{2,0},{3,1},{4,6},{5,7},{6,4},{7,5},{8,10},{9,11},{10,... | collective-permute-start | bytes 196616 | tf_op jit(solution)/shard_map/ppermute | solution.py:20
  87.4 6.7 %collective-permute-start.30 = (bf16[2,128,128]{2,1,0:T(8,128)(2,1)S(1)}, bf16[2,128,128]{2,1,0:T(8,128)(2,1)S(1)}, u32[]{:S(2)}, u32[]{:S(2)}) collective-permute-start(bf16[2,128,128]{2,1,0:T(8,128)(2,1)S(1)} %pad_maximum_fusion.11), channel_id=1, source_target_pairs={{0,6},{1,7},{2,4},{3,5},{4,2},{5,3},{6,0},{7,1},{8,14},{9,15},{10,... | collective-permute-start | bytes 196616 | tf_op jit(solution)/shard_map/ppermute | solution.py:20
  89.6 5.9 %collective-permute-start.31 = (bf16[2,128,128]{2,1,0:T(8,128)(2,1)S(1)}, bf16[2,128,128]{2,1,0:T(8,128)(2,1)S(1)}, u32[]{:S(2)}, u32[]{:S(2)}) collective-permute-start(bf16[2,128,128]{2,1,0:T(8,128)(2,1)S(1)} %pad_maximum_fusion.11), channel_id=1, source_target_pairs={{0,4},{1,5},{2,6},{3,7},{4,0},{5,1},{6,2},{7,3},{8,12},{9,13},{10,... | collective-permute-start | bytes 196616 | tf_op jit(solution)/shard_map/ppermute | solution.py:20
  89.6 5.9 %collective-permute-start.32 = (bf16[2,128,128]{2,1,0:T(8,128)(2,1)S(1)}, bf16[2,128,128]{2,1,0:T(8,128)(2,1)S(1)}, u32[]{:S(2)}, u32[]{:S(2)}) collective-permute-start(bf16[2,128,128]{2,1,0:T(8,128)(2,1)S(1)} %pad_maximum_fusion.11), channel_id=1, source_target_pairs={{0,2},{1,3},{2,0},{3,1},{4,6},{5,7},{6,4},{7,5},{8,10},{9,11},{10,... | collective-permute-start | bytes 196616 | tf_op jit(solution)/shard_map/ppermute | solution.py:20
  96.0 6.2 %collective-permute-start.33 = (bf16[2,128,128]{2,1,0:T(8,128)(2,1)S(1)}, bf16[2,128,128]{2,1,0:T(8,128)(2,1)S(1)}, u32[]{:S(2)}, u32[]{:S(2)}) collective-permute-start(bf16[2,128,128]{2,1,0:T(8,128)(2,1)S(1)} %pad_maximum_fusion.12), channel_id=1, source_target_pairs={{0,6},{1,7},{2,4},{3,5},{4,2},{5,3},{6,0},{7,1},{8,14},{9,15},{10,... | collective-permute-start | bytes 196616 | tf_op jit(solution)/shard_map/ppermute | solution.py:20
  98.5 5.6 %collective-permute-start.34 = (bf16[2,128,128]{2,1,0:T(8,128)(2,1)S(1)}, bf16[2,128,128]{2,1,0:T(8,128)(2,1)S(1)}, u32[]{:S(2)}, u32[]{:S(2)}) collective-permute-start(bf16[2,128,128]{2,1,0:T(8,128)(2,1)S(1)} %pad_maximum_fusion.12), channel_id=1, source_target_pairs={{0,4},{1,5},{2,6},{3,7},{4,0},{5,1},{6,2},{7,3},{8,12},{9,13},{10,... | collective-permute-start | bytes 196616 | tf_op jit(solution)/shard_map/ppermute | solution.py:20
  98.5 5.6 %collective-permute-start.35 = (bf16[2,128,128]{2,1,0:T(8,128)(2,1)S(1)}, bf16[2,128,128]{2,1,0:T(8,128)(2,1)S(1)}, u32[]{:S(2)}, u32[]{:S(2)}) collective-permute-start(bf16[2,128,128]{2,1,0:T(8,128)(2,1)S(1)} %pad_maximum_fusion.12), channel_id=1, source_target_pairs={{0,2},{1,3},{2,0},{3,1},{4,6},{5,7},{6,4},{7,5},{8,10},{9,11},{10,... | collective-permute-start | bytes 196616 | tf_op jit(solution)/shard_map/ppermute | solution.py:20
  104.6 4.9 %collective-permute-start.36 = (bf16[128,128]{1,0:T(8,128)(2,1)S(1)}, bf16[128,128]{1,0:T(8,128)(2,1)S(1)}, u32[]{:S(2)}, u32[]{:S(2)}) collective-permute-start(bf16[128,128]{1,0:T(8,128)(2,1)S(1)} %get-tuple-element.57), channel_id=1, source_target_pairs={{0,24},{1,25},{2,26},{3,27},{4,28},{5,29},{6,30},{7,31},{8,16},{9,... | collective-permute-start | bytes 98312 | tf_op jit(solution)/shard_map/ppermute | solution.py:20
  106.9 3.9 %collective-permute-start.37 = (bf16[128,128]{1,0:T(8,128)(2,1)S(1)}, bf16[128,128]{1,0:T(8,128)(2,1)S(1)}, u32[]{:S(2)}, u32[]{:S(2)}) collective-permute-start(bf16[128,128]{1,0:T(8,128)(2,1)S(1)} %get-tuple-element.59), channel_id=1, source_target_pairs={{0,16},{1,17},{2,18},{3,19},{4,20},{5,21},{6,22},{7,23},{8,24},{9,... | collective-permute-start | bytes 98312 | tf_op jit(solution)/shard_map/ppermute | solution.py:20
  107.5 3.9 %collective-permute-start.38 = (bf16[128,128]{1,0:T(8,128)(2,1)S(1)}, bf16[128,128]{1,0:T(8,128)(2,1)S(1)}, u32[]{:S(2)}, u32[]{:S(2)}) collective-permute-start(bf16[128,128]{1,0:T(8,128)(2,1)S(1)} %get-tuple-element.58), channel_id=1, source_target_pairs={{0,8},{1,9},{2,10},{3,11},{4,12},{5,13},{6,14},{7,15},{8,0},{9,1},... | collective-permute-start | bytes 98312 | tf_op jit(solution)/shard_map/ppermute | solution.py:20
  108.2 4.0 %collective-permute-start.22 = (bf16[64,128]{1,0:T(8,128)(2,1)S(1)}, bf16[64,128]{1,0:T(8,128)(2,1)S(1)}, u32[]{:S(2)}, u32[]{:S(2)}) collective-permute-start(bf16[64,128]{1,0:T(8,128)(2,1)S(1)} %constant_dynamic-slice_fusion.17), channel_id=1, source_target_pairs={{0,1},{1,0},{2,3},{3,2},{4,5},{5,4},{6,7},{7,6},{8,9},{9,8},{10,11... | collective-permute-start | bytes 49160 | tf_op jit(solution)/shard_map/ppermute | solution.py:20
  (16 other events, 94.7 us)

commit v5 on v4

--- a/solution.py
+++ b/solution.py
@@ -235,8 +235,12 @@
     low_chip = in_order(sep_lower, sep_lower_other)
     inv_chip = in_order(sep_inverse[:, :top_offset], inverse_others[0][:, :top_offset])
     if paired:
-        inv_theirs = in_order(
-            inverse_rows[1][:, : 2 * base_width], inverse_others[1][:, : 2 * base_width]
+        inv_own, inv_theirs = [
+            in_order(mine[:, : 2 * base_width], other[:, : 2 * base_width])
+            for mine, other in zip(inverse_rows[:2], inverse_others[:2])
+        ]
+        inv_pair = jnp.concatenate(
+            [jnp.where(k % 2 == 1, inv_theirs, inv_own), jnp.where(k % 2 == 1, inv_own, inv_theirs)]
         )
 
     def top_columns(a, value):
@@ -318,9 +322,9 @@
             their_pivot = (their_sep.astype(jnp.float32) + their_own + their_sent).astype(dtype)
             pivots_all = gather_z(by_leaf(pivot, their_pivot))
             pivots_all = jnp.swapaxes(pivots_all, 0, 1).reshape(-1, half)
-            solved = product(inverse_here, pivots_all).astype(dtype)
-            their_solved = product(inv_theirs, pivots_all).astype(dtype)
-            solved_all = gather_z(by_leaf(solved, their_solved))
+            both = product(inv_pair, pivots_all).astype(dtype)
+            solved = lax.dynamic_slice_in_dim(both, k % 2 * 2 * pivots, 2 * pivots, 0)
+            solved_all = gather_z(both.reshape(2, 2 * pivots, half))
             solved_all = jnp.swapaxes(solved_all, 0, 1).reshape(-1, half)
         else:
             solved = product(inverse_here, gather_node(pivot, height)).astype(dtype)

time: 114 us -> 106 us (0.930)
  waiting for transfers between devices: 53.1 us -> 34.1 us
  other arithmetic: 6.41 us -> 11.1 us
  starting transfers between devices: 39.7 us -> 44.3 us
  local copies, waits for them, and re-layouts: 3.58 us -> 5.45 us
    ppermute x40, waiting for transfers between devices: 53.1 us -> 34.1 us  [exchange(): return lax.ppermute(value, ('leaf', 'blk'), pairs)]
    ppermute x40, starting transfers between devices: 39.7 us -> 44.3 us  [exchange(): return lax.ppermute(value, ('leaf', 'blk'), pairs)]
    eq x4, other arithmetic: 0.04 us -> 2.34 us  [mix(): hit = (targets == t)[:, :, None, None]]
    dynamic_slice x8, local copies, waits for them, and re-layouts: 0.95 us -> 2.72 us  [leaf_columns(): lax.dynamic_slice_in_dim(value, top_offset + leaf * base_width, base_widt...]
    select_n x6 -> x7, other arithmetic: 3.48 us -> 4.38 us  [in_order(): first = jnp.where(core == 0, mine, other)]
    dot_general x6 -> x5, matrix products: 3.98 us -> 3.85 us  [product(): return jnp.dot(matrix, vectors, preferred_element_type=jnp.float32)]
  transfers between devices with their start and end apart: 40 -> 40, of which waited for: 21 -> 18; matrix products, arithmetic and copies ran while one was open for 9% -> 16% of each run, Pallas kernels for 4% -> 5%
where the time goes in v5:
time: 106 us; the launch traced here: 105 us
  starting transfers between devices  44.3 us (42%)
  waiting for transfers between devices  34.1 us (32%)
  other arithmetic  11.1 us (10%)
  local copies, waits for them, and re-layouts  5.45 us (5%)
  Pallas kernels  5.13 us (5%)
  matrix products  3.85 us (4%)
  between operations  1.48 us (1%)
    ppermute x40, starting transfers between devices, exchange(): return lax.ppermute(value, ('leaf', 'blk'), pairs)  44.3 us
    ppermute x40, waiting for transfers between devices, exchange(): return lax.ppermute(value, ('leaf', 'blk'), pairs)  34.1 us
    select_n x7, other arithmetic, in_order(): first = jnp.where(core == 0, mine, other)  4.38 us
    dot_general x5, matrix products, product(): return jnp.dot(matrix, vectors, preferred_element_type=jnp.float32)  3.85 us
    pallas_call x1, Pallas kernels, leaf_partial(): pl.pallas_call(body, in_specs=vmem_specs(count) + [pl.BlockSpec(memory_sp...  3.56 us
    dynamic_slice x8, local copies, waits for them, and re-layouts, leaf_columns(): lax.dynamic_slice_in_dim(value, top_offset + leaf * base_width, base_widt...  2.72 us
    eq x4, other arithmetic, mix(): hit = (targets == t)[:, :, None, None]  2.34 us
    unnamed x42, local copies, waits for them, and re-layouts  2.25 us
  transfers between devices with their start and end apart: 40, of which 18 were waited for; matrix products, arithmetic and copies ran while one was open for 16% of the time, Pallas kernels for 5%

profile of v5, /device:TPU:0, one launch (start us, length us, event | category | flops | bytes accessed | tf_op | source)
XLA Modules:
  0.0 105.4 jit_solution(1256452224375672293)
XLA Ops:
  0.6 3.0 %collective-permute-start.9 = (bf16[64,3072]{1,0:T(8,128)(2,1)}, bf16[64,3072]{1,0:T(8,128)(2,1)}, u32[]{:S(2)}, u32[]{:S(2)}) collective-permute-start(bf16[64,3072]{1,0:T(8,128)(2,1)} %param.11), channel_id=1, source_target_pairs={{0,8},{1,9},{2,10},{3,11},{4,12},{5,13},{6,14},{7,15},{8,0},{9,1},... | collective-permute-start | bytes 1179656 | tf_op jit(solution)/shard_map/ppermute | solution.py:20
  3.7 1.5 %collective-permute-start.25 = (bf16[64,3072]{1,0:T(8,128)(2,1)}, bf16[64,3072]{1,0:T(8,128)(2,1)}, u32[]{:S(2)}, u32[]{:S(2)}) collective-permute-start(bf16[64,3072]{1,0:T(8,128)(2,1)} %param.11), channel_id=1, source_target_pairs={{0,16},{1,17},{2,18},{3,19},{4,20},{5,21},{6,22},{7,23},{8,24},{9,... | collective-permute-start | bytes 1179656 | tf_op jit(solution)/shard_map/ppermute | solution.py:20
  10.6 2.5 %collective-permute-done.15 = s32[2,2]{1,0:T(2,128)S(1)} collective-permute-done((s32[2,2]{1,0:T(2,128)S(1)}, s32[2,2]{1,0:T(2,128)S(1)}, u32[]{:S(2)}, u32[]{:S(2)}) %collective-permute-start.15) | collective-permute-done | bytes 48 | tf_op jit(solution)/shard_map/ppermute | solution.py:20
  13.7 2.7 %collective-permute-start.27 = (bf16[64,3072]{1,0:T(8,128)(2,1)}, bf16[64,3072]{1,0:T(8,128)(2,1)S(1)}, u32[]{:S(2)}, u32[]{:S(2)}) collective-permute-start(bf16[64,3072]{1,0:T(8,128)(2,1)} %param.11), channel_id=1, source_target_pairs={{0,24},{1,25},{2,26},{3,27},{4,28},{5,29},{6,30},{7,31},{8,16},{9,... | collective-permute-start | bytes 1179656 | tf_op jit(solution)/shard_map/ppermute | solution.py:20
  18.1 1.8 %broadcast_select_fusion.1 = (bf16[128,1024]{1,0:T(8,128)(2,1)}, bf16[128,1024]{1,0:T(8,128)(2,1)}) fusion(bf16[128,1024]{1,0:T(8,128)(2,1)} %param.12, bf16[128,1024]{1,0:T(8,128)(2,1)S(1)} %collective-permute-done.29, pred[]{:T(512)S(6)} %eq.99), kind=kLoop, calls=%fused_computation.11 | loop fusion | flops 262144 | bytes 1048577 | tf_op jit(solution)/shard_map/jit(_where)/select_n | solution.py:182
  22.4 2.5 %collective-permute-start.6 = (bf16[320,128]{1,0:T(8,128)(2,1)S(1)}, bf16[320,128]{1,0:T(8,128)(2,1)S(1)}, u32[]{:S(2)}, u32[]{:S(2)}) collective-permute-start(bf16[320,128]{1,0:T(8,128)(2,1)S(1)} %get-tuple-element.11), channel_id=1, source_target_pairs={{0,5},{1,4},{2,7},{3,6},{4,1},{5,0},{6,3},{7,2},{8,13},{9,12},{10,... | collective-permute-start | bytes 245768 | tf_op jit(solution)/shard_map/ppermute | solution.py:20
  28.4 2.8 %collective-permute-start.5 = (bf16[320,128]{1,0:T(8,128)(2,1)S(1)}, bf16[320,128]{1,0:T(8,128)(2,1)S(1)}, u32[]{:S(2)}, u32[]{:S(2)}) collective-permute-start(bf16[320,128]{1,0:T(8,128)(2,1)S(1)} %get-tuple-element.10.refs_0_), channel_id=1, source_target_pairs={{0,4},{1,5},{2,6},{3,7},{4,0},{5,1},{6,2},{7,3},{8,12},{9,13},{10,... | collective-permute-start | bytes 245768 | tf_op jit(solution)/shard_map/ppermute | solution.py:20
  31.2 1.6 %collective-permute-start = (bf16[320,128]{1,0:T(8,128)(2,1)S(1)}, bf16[320,128]{1,0:T(8,128)(2,1)S(1)}, u32[]{:S(2)}, u32[]{:S(2)}) collective-permute-start(bf16[320,128]{1,0:T(8,128)(2,1)S(1)} %get-tuple-element.10.refs_0_), channel_id=1, source_target_pairs={{0,2},{1,3},{2,0},{3,1},{4,6},{5,7},{6,4},{7,5},{8,10},{9,11},{10,... | collective-permute-start | bytes 245768 | tf_op jit(solution)/shard_map/ppermute | solution.py:20
  35.5 3.8 %collective-permute-start.2 = (bf16[320,128]{1,0:T(8,128)(2,1)S(1)}, bf16[320,128]{1,0:T(8,128)(2,1)S(1)}, u32[]{:S(2)}, u32[]{:S(2)}) collective-permute-start(bf16[320,128]{1,0:T(8,128)(2,1)S(1)} %get-tuple-element.10.refs_0_), channel_id=1, source_target_pairs={{0,6},{1,7},{2,4},{3,5},{4,2},{5,3},{6,0},{7,1},{8,14},{9,15},{10,... | collective-permute-start | bytes 245768 | tf_op jit(solution)/shard_map/ppermute | solution.py:20
  41.7 3.6 %leaf_partial.1 = (f32[2,320,128]{2,1,0:T(8,128)S(1)}, bf16[320,1280]{1,0:T(8,128)(2,1)S(1)}, bf16[320,1280]{1,0:T(8,128)(2,1)S(1)}) custom-call(bf16[320,128]{1,0:T(8,128)(2,1)S(1)} %get-tuple-element.10.refs_0_, bf16[320,128]{1,0:T(8,128)(2,1)S(1)} %collective-permute-done.4.refs_1_, bf16[320,128]{1,0:T(8,128)(2,1)S(1)} %collective-permute-done.5.refs_2_, ...), custom_call_target="tpu_custom_call" | custom-call | flops 419430400 | bytes 3276800 | tf_op jit(solution)/shard_map/leaf_partial/pallas_call | solution.py:75
  45.2 1.7 %collective-permute-start.13 = (bf16[128,128]{1,0:T(8,128)(2,1)S(1)}, bf16[128,128]{1,0:T(8,128)(2,1)S(1)}, u32[]{:S(2)}, u32[]{:S(2)}) collective-permute-start(bf16[128,128]{1,0:T(8,128)(2,1)S(1)} %copy-done.10), channel_id=1, source_target_pairs={{0,8},{1,9},{2,10},{3,11},{4,12},{5,13},{6,14},{7,15},{8,0},{9,1},... | collective-permute-start | bytes 98312 | tf_op jit(solution)/shard_map/ppermute | solution.py:20
  47.6 3.7 %collective-permute-start.17 = (bf16[640,128]{1,0:T(8,128)(2,1)S(1)}, bf16[640,128]{1,0:T(8,128)(2,1)S(1)}, u32[]{:S(2)}, u32[]{:S(2)}) collective-permute-start(bf16[640,128]{1,0:T(8,128)(2,1)S(1)} %get-tuple-element.17), channel_id=1, source_target_pairs={{0,6},{1,7},{2,4},{3,5},{4,2},{5,3},{6,0},{7,1},{8,14},{9,15},{10,... | collective-permute-start | bytes 491528 | tf_op jit(solution)/shard_map/ppermute | solution.py:20
  53.8 8.7 %collective-permute-done.16 = bf16[640,128]{1,0:T(8,128)(2,1)S(1)} collective-permute-done((bf16[640,128]{1,0:T(8,128)(2,1)S(1)}, bf16[640,128]{1,0:T(8,128)(2,1)S(1)}, u32[]{:S(2)}, u32[]{:S(2)}) %collective-permute-start.16) | collective-permute-done | bytes 163872 | tf_op jit(solution)/shard_map/ppermute | solution.py:20
  62.6 2.0 %collective-permute-done.18 = bf16[640,128]{1,0:T(8,128)(2,1)S(1)} collective-permute-done((bf16[640,128]{1,0:T(8,128)(2,1)S(1)}, bf16[640,128]{1,0:T(8,128)(2,1)S(1)}, u32[]{:S(2)}, u32[]{:S(2)}) %collective-permute-start.18) | collective-permute-done | bytes 163872 | tf_op jit(solution)/shard_map/ppermute | solution.py:20
  64.7 1.4 %fusion.28 = f32[128,128]{0,1:T(8,128)S(1)} fusion(bf16[128,2560]{1,0:T(8,128)(2,1)} %collective-permute-done.19, bf16[2560,128]{1,0:T(8,128)(2,1)S(1)} %constant_dynamic-update-slice_fusion.1), kind=kOutput, calls=%fused_computation.144 | convolution fusion | flops 83886080 | bytes 1376256 | tf_op jit(solution)/shard_map/dot_general | solution.py:24
  66.1 1.4 %select_bitcast_fusion.1 = (f32[128,128]{1,0:T(8,128)S(1)}, f32[128,128]{1,0:T(8,128)S(1)}) fusion(f32[128,128]{0,1:T(8,128)S(1)} %fusion.28, pred[]{:T(512)S(6)} %eq.99, bf16[128,2560]{1,0:T(8,128)(2,1)} %param.9, bf16[2560,128]{1,0:T(8,128)(2,1)S(1)} %constant_dynamic-update-slice_fusion.1), kind=kOutput, calls=%fused_computation.85 | convolution fusion | flops 83918848 | bytes 1507329 | tf_op jit(solution)/shard_map/dot_general | solution.py:24
  68.3 3.6 %collective-permute-done.20 = bf16[2,2,64,128]{3,2,1,0:T(8,128)(2,1)S(1)} collective-permute-done((bf16[2,2,64,128]{3,2,1,0:T(8,128)(2,1)S(1)}, bf16[2,2,64,128]{3,2,1,0:T(8,128)(2,1)S(1)}, u32[]{:S(2)}, u32[]{:S(2)}) %collective-permute-start.20) | collective-permute-done | bytes 65568 | tf_op jit(solution)/shard_map/ppermute | solution.py:20
  72.2 1.8 %collective-permute-start.21 = (bf16[2,128,128]{2,1,0:T(8,128)(2,1)S(1)}, bf16[2,128,128]{2,1,0:T(8,128)(2,1)S(1)}, u32[]{:S(2)}, u32[]{:S(2)}) collective-permute-start(bf16[2,128,128]{2,1,0:T(8,128)(2,1)S(1)} %pad_maximum_fusion.12), channel_id=1, source_target_pairs={{0,6},{1,7},{2,4},{3,5},{4,2},{5,3},{6,0},{7,1},{8,14},{9,15},{10,... | collective-permute-start | bytes 196616 | tf_op jit(solution)/shard_map/ppermute | solution.py:20
  74.9 1.7 %collective-permute-start.23 = (bf16[2,128,128]{2,1,0:T(8,128)(2,1)S(1)}, bf16[2,128,128]{2,1,0:T(8,128)(2,1)S(1)}, u32[]{:S(2)}, u32[]{:S(2)}) collective-permute-start(bf16[2,128,128]{2,1,0:T(8,128)(2,1)S(1)} %pad_maximum_fusion.12), channel_id=1, source_target_pairs={{0,2},{1,3},{2,0},{3,1},{4,6},{5,7},{6,4},{7,5},{8,10},{9,11},{10,... | collective-permute-start | bytes 196616 | tf_op jit(solution)/shard_map/ppermute | solution.py:20
  76.7 2.0 %collective-permute-done.21 = bf16[2,128,128]{2,1,0:T(8,128)(2,1)S(1)} collective-permute-done((bf16[2,128,128]{2,1,0:T(8,128)(2,1)S(1)}, bf16[2,128,128]{2,1,0:T(8,128)(2,1)S(1)}, u32[]{:S(2)}, u32[]{:S(2)}) %collective-permute-start.21) | collective-permute-done | bytes 65568 | tf_op jit(solution)/shard_map/ppermute | solution.py:20
  78.7 1.4 %collective-permute-done.22 = bf16[2,128,128]{2,1,0:T(8,128)(2,1)S(1)} collective-permute-done((bf16[2,128,128]{2,1,0:T(8,128)(2,1)S(1)}, bf16[2,128,128]{2,1,0:T(8,128)(2,1)S(1)}, u32[]{:S(2)}, u32[]{:S(2)}) %collective-permute-start.22) | collective-permute-done | bytes 65568 | tf_op jit(solution)/shard_map/ppermute | solution.py:20
  80.5 2.1 %collective-permute-start.30 = (bf16[2,128,128]{2,1,0:T(8,128)(2,1)S(1)}, bf16[2,128,128]{2,1,0:T(8,128)(2,1)S(1)}, u32[]{:S(2)}, u32[]{:S(2)}) collective-permute-start(bf16[2,128,128]{2,1,0:T(8,128)(2,1)S(1)} %bitcast.126), channel_id=1, source_target_pairs={{0,6},{1,7},{2,4},{3,5},{4,2},{5,3},{6,0},{7,1},{8,14},{9,15},{10,... | collective-permute-start | bytes 196616 | tf_op jit(solution)/shard_map/ppermute | solution.py:20
  82.8 2.2 %collective-permute-start.32 = (bf16[2,128,128]{2,1,0:T(8,128)(2,1)S(1)}, bf16[2,128,128]{2,1,0:T(8,128)(2,1)S(1)}, u32[]{:S(2)}, u32[]{:S(2)}) collective-permute-start(bf16[2,128,128]{2,1,0:T(8,128)(2,1)S(1)} %bitcast.128), channel_id=1, source_target_pairs={{0,2},{1,3},{2,0},{3,1},{4,6},{5,7},{6,4},{7,5},{8,10},{9,11},{10,... | collective-permute-start | bytes 196616 | tf_op jit(solution)/shard_map/ppermute | solution.py:20
  85.1 1.7 %collective-permute-done.30 = bf16[2,128,128]{2,1,0:T(8,128)(2,1)S(1)} collective-permute-done((bf16[2,128,128]{2,1,0:T(8,128)(2,1)S(1)}, bf16[2,128,128]{2,1,0:T(8,128)(2,1)S(1)}, u32[]{:S(2)}, u32[]{:S(2)}) %collective-permute-start.30) | collective-permute-done | bytes 65568 | tf_op jit(solution)/shard_map/ppermute | solution.py:20
  86.8 1.5 %collective-permute-done.31 = bf16[2,128,128]{2,1,0:T(8,128)(2,1)S(1)} collective-permute-done((bf16[2,128,128]{2,1,0:T(8,128)(2,1)S(1)}, bf16[2,128,128]{2,1,0:T(8,128)(2,1)S(1)}, u32[]{:S(2)}, u32[]{:S(2)}) %collective-permute-start.31) | collective-permute-done | bytes 65568 | tf_op jit(solution)/shard_map/ppermute | solution.py:20
  88.8 2.6 %collective-permute-start.33 = (bf16[2,128,128]{2,1,0:T(8,128)(2,1)S(1)}, bf16[2,128,128]{2,1,0:T(8,128)(2,1)S(1)}, u32[]{:S(2)}, u32[]{:S(2)}) collective-permute-start(bf16[2,128,128]{2,1,0:T(8,128)(2,1)S(1)} %pad_maximum_fusion.13), channel_id=1, source_target_pairs={{0,6},{1,7},{2,4},{3,5},{4,2},{5,3},{6,0},{7,1},{8,14},{9,15},{10,... | collective-permute-start | bytes 196616 | tf_op jit(solution)/shard_map/ppermute | solution.py:20
  91.4 1.9 %collective-permute-start.35 = (bf16[2,128,128]{2,1,0:T(8,128)(2,1)S(1)}, bf16[2,128,128]{2,1,0:T(8,128)(2,1)S(1)}, u32[]{:S(2)}, u32[]{:S(2)}) collective-permute-start(bf16[2,128,128]{2,1,0:T(8,128)(2,1)S(1)} %pad_maximum_fusion.13), channel_id=1, source_target_pairs={{0,2},{1,3},{2,0},{3,1},{4,6},{5,7},{6,4},{7,5},{8,10},{9,11},{10,... | collective-permute-start | bytes 196616 | tf_op jit(solution)/shard_map/ppermute | solution.py:20
  93.4 1.8 %collective-permute-done.33 = bf16[2,128,128]{2,1,0:T(8,128)(2,1)S(1)} collective-permute-done((bf16[2,128,128]{2,1,0:T(8,128)(2,1)S(1)}, bf16[2,128,128]{2,1,0:T(8,128)(2,1)S(1)}, u32[]{:S(2)}, u32[]{:S(2)}) %collective-permute-start.33) | collective-permute-done | bytes 65568 | tf_op jit(solution)/shard_map/ppermute | solution.py:20
  95.2 1.8 %collective-permute-done.34 = bf16[2,128,128]{2,1,0:T(8,128)(2,1)S(1)} collective-permute-done((bf16[2,128,128]{2,1,0:T(8,128)(2,1)S(1)}, bf16[2,128,128]{2,1,0:T(8,128)(2,1)S(1)}, u32[]{:S(2)}, u32[]{:S(2)}) %collective-permute-start.34) | collective-permute-done | bytes 65568 | tf_op jit(solution)/shard_map/ppermute | solution.py:20
  97.4 1.6 %collective-permute-start.36 = (bf16[128,128]{1,0:T(8,128)(2,1)S(1)}, bf16[128,128]{1,0:T(8,128)(2,1)S(1)}, u32[]{:S(2)}, u32[]{:S(2)}) collective-permute-start(bf16[128,128]{1,0:T(8,128)(2,1)S(1)} %get-tuple-element.59), channel_id=1, source_target_pairs={{0,24},{1,25},{2,26},{3,27},{4,28},{5,29},{6,30},{7,31},{8,16},{9,... | collective-permute-start | bytes 98312 | tf_op jit(solution)/shard_map/ppermute | solution.py:20
  99.5 1.5 %collective-permute-start.38 = (bf16[128,128]{1,0:T(8,128)(2,1)S(1)}, bf16[128,128]{1,0:T(8,128)(2,1)S(1)}, u32[]{:S(2)}, u32[]{:S(2)}) collective-permute-start(bf16[128,128]{1,0:T(8,128)(2,1)S(1)} %get-tuple-element.60), channel_id=1, source_target_pairs={{0,8},{1,9},{2,10},{3,11},{4,12},{5,13},{6,14},{7,15},{8,0},{9,1},... | collective-permute-start | bytes 98312 | tf_op jit(solution)/shard_map/ppermute | solution.py:20
  101.0 1.3 %collective-permute-done.36 = bf16[128,128]{1,0:T(8,128)(2,1)S(1)} collective-permute-done((bf16[128,128]{1,0:T(8,128)(2,1)S(1)}, bf16[128,128]{1,0:T(8,128)(2,1)S(1)}, u32[]{:S(2)}, u32[]{:S(2)}) %collective-permute-start.36) | collective-permute-done | bytes 32800 | tf_op jit(solution)/shard_map/ppermute | solution.py:20
  (167 shorter events, 28.8 us)
Async XLA Ops:
  0.6 20.5 %collective-permute-start.9 = (bf16[64,3072]{1,0:T(8,128)(2,1)}, bf16[64,3072]{1,0:T(8,128)(2,1)}, u32[]{:S(2)}, u32[]{:S(2)}) collective-permute-start(bf16[64,3072]{1,0:T(8,128)(2,1)} %param.11), channel_id=1, source_target_pairs={{0,8},{1,9},{2,10},{3,11},{4,12},{5,13},{6,14},{7,15},{8,0},{9,1},... | collective-permute-start | bytes 1179656 | tf_op jit(solution)/shard_map/ppermute | solution.py:20
  3.7 16.2 %collective-permute-start.11 = (bf16[64,3072]{1,0:T(8,128)(2,1)}, bf16[64,3072]{1,0:T(8,128)(2,1)S(1)}, u32[]{:S(2)}, u32[]{:S(2)}) collective-permute-start(bf16[64,3072]{1,0:T(8,128)(2,1)} %param.11), channel_id=1, source_target_pairs={{0,1},{1,0},{2,3},{3,2},{4,5},{5,4},{6,7},{7,6},{8,9},{9,8},{10,11... | collective-permute-start | bytes 1179656 | tf_op jit(solution)/shard_map/ppermute | solution.py:20
  3.7 18.7 %collective-permute-start.25 = (bf16[64,3072]{1,0:T(8,128)(2,1)}, bf16[64,3072]{1,0:T(8,128)(2,1)}, u32[]{:S(2)}, u32[]{:S(2)}) collective-permute-start(bf16[64,3072]{1,0:T(8,128)(2,1)} %param.11), channel_id=1, source_target_pairs={{0,16},{1,17},{2,18},{3,19},{4,20},{5,21},{6,22},{7,23},{8,24},{9,... | collective-permute-start | bytes 1179656 | tf_op jit(solution)/shard_map/ppermute | solution.py:20
  5.4 8.3 %collective-permute-start.12 = (bf16[2,64,256]{2,1,0:T(8,128)(2,1)}, bf16[2,64,256]{2,1,0:T(8,128)(2,1)S(1)}, u32[]{:S(2)}, u32[]{:S(2)}) collective-permute-start(bf16[2,64,256]{2,1,0:T(8,128)(2,1)} %param.10), channel_id=1, source_target_pairs={{0,1},{1,0},{2,3},{3,2},{4,5},{5,4},{6,7},{7,6},{8,9},{9,8},{10,11... | collective-permute-start | bytes 196616 | tf_op jit(solution)/shard_map/ppermute | solution.py:20
  13.1 4.7 %collective-permute-start.29 = (bf16[128,1024]{1,0:T(8,128)(2,1)}, bf16[128,1024]{1,0:T(8,128)(2,1)S(1)}, u32[]{:S(2)}, u32[]{:S(2)}) collective-permute-start(bf16[128,1024]{1,0:T(8,128)(2,1)} %param.12), channel_id=1, source_target_pairs={{0,1},{1,0},{2,3},{3,2},{4,5},{5,4},{6,7},{7,6},{8,9},{9,8},{10,11... | collective-permute-start | bytes 786440 | tf_op jit(solution)/shard_map/ppermute | solution.py:20
  13.7 12.7 %collective-permute-start.27 = (bf16[64,3072]{1,0:T(8,128)(2,1)}, bf16[64,3072]{1,0:T(8,128)(2,1)S(1)}, u32[]{:S(2)}, u32[]{:S(2)}) collective-permute-start(bf16[64,3072]{1,0:T(8,128)(2,1)} %param.11), channel_id=1, source_target_pairs={{0,24},{1,25},{2,26},{3,27},{4,28},{5,29},{6,30},{7,31},{8,16},{9,... | collective-permute-start | bytes 1179656 | tf_op jit(solution)/shard_map/ppermute | solution.py:20
  17.8 17.0 %collective-permute-start.4 = (bf16[320,128]{1,0:T(8,128)(2,1)S(1)}, bf16[320,128]{1,0:T(8,128)(2,1)S(1)}, u32[]{:S(2)}, u32[]{:S(2)}) collective-permute-start(bf16[320,128]{1,0:T(8,128)(2,1)S(1)} %get-tuple-element.11), channel_id=1, source_target_pairs={{0,1},{1,0},{2,3},{3,2},{4,5},{5,4},{6,7},{7,6},{8,9},{9,8},{10,11... | collective-permute-start | bytes 245768 | tf_op jit(solution)/shard_map/ppermute | solution.py:20
  19.9 19.5 %collective-permute-start.7 = (bf16[320,2560]{1,0:T(8,128)(2,1)S(1)}, bf16[320,2560]{1,0:T(8,128)(2,1)S(1)}, u32[]{:S(2)}, u32[]{:S(2)}) collective-permute-start(bf16[320,2560]{1,0:T(8,128)(2,1)S(1)} %copy-done), channel_id=1, source_target_pairs={{0,1},{1,0},{2,3},{3,2},{4,5},{5,4},{6,7},{7,6},{8,9},{9,8},{10,11... | collective-permute-start | bytes 4915208 | tf_op jit(solution)/shard_map/ppermute | solution.py:20
  21.2 5.3 %collective-permute-start.10 = (bf16[64,3072]{1,0:T(8,128)(2,1)}, bf16[64,3072]{1,0:T(8,128)(2,1)S(1)}, u32[]{:S(2)}, u32[]{:S(2)}) collective-permute-start(bf16[64,3072]{1,0:T(8,128)(2,1)} %collective-permute-done.9), channel_id=1, source_target_pairs={{0,1},{1,0},{2,3},{3,2},{4,5},{5,4},{6,7},{7,6},{8,9},{9,8},{10,11... | collective-permute-start | bytes 1179656 | tf_op jit(solution)/shard_map/ppermute | solution.py:20
  22.4 16.9 %collective-permute-start.6 = (bf16[320,128]{1,0:T(8,128)(2,1)S(1)}, bf16[320,128]{1,0:T(8,128)(2,1)S(1)}, u32[]{:S(2)}, u32[]{:S(2)}) collective-permute-start(bf16[320,128]{1,0:T(8,128)(2,1)S(1)} %get-tuple-element.11), channel_id=1, source_target_pairs={{0,5},{1,4},{2,7},{3,6},{4,1},{5,0},{6,3},{7,2},{8,13},{9,12},{10,... | collective-permute-start | bytes 245768 | tf_op jit(solution)/shard_map/ppermute | solution.py:20
  26.4 4.8 %collective-permute-start.28 = (bf16[64,3072]{1,0:T(8,128)(2,1)S(1)}, bf16[64,3072]{1,0:T(8,128)(2,1)S(1)}, u32[]{:S(2)}, u32[]{:S(2)}) collective-permute-start(bf16[64,3072]{1,0:T(8,128)(2,1)S(1)} %collective-permute-done.27), channel_id=1, source_target_pairs={{0,1},{1,0},{2,3},{3,2},{4,5},{5,4},{6,7},{7,6},{8,9},{9,8},{10,11... | collective-permute-start | bytes 1179656 | tf_op jit(solution)/shard_map/ppermute | solution.py:20
  28.4 7.1 %collective-permute-start.5 = (bf16[320,128]{1,0:T(8,128)(2,1)S(1)}, bf16[320,128]{1,0:T(8,128)(2,1)S(1)}, u32[]{:S(2)}, u32[]{:S(2)}) collective-permute-start(bf16[320,128]{1,0:T(8,128)(2,1)S(1)} %get-tuple-element.10.refs_0_), channel_id=1, source_target_pairs={{0,4},{1,5},{2,6},{3,7},{4,0},{5,1},{6,2},{7,3},{8,12},{9,13},{10,... | collective-permute-start | bytes 245768 | tf_op jit(solution)/shard_map/ppermute | solution.py:20
  31.2 14.0 %collective-permute-start = (bf16[320,128]{1,0:T(8,128)(2,1)S(1)}, bf16[320,128]{1,0:T(8,128)(2,1)S(1)}, u32[]{:S(2)}, u32[]{:S(2)}) collective-permute-start(bf16[320,128]{1,0:T(8,128)(2,1)S(1)} %get-tuple-element.10.refs_0_), channel_id=1, source_target_pairs={{0,2},{1,3},{2,0},{3,1},{4,6},{5,7},{6,4},{7,5},{8,10},{9,11},{10,... | collective-permute-start | bytes 245768 | tf_op jit(solution)/shard_map/ppermute | solution.py:20
  34.8 12.1 %collective-permute-start.1 = (bf16[320,128]{1,0:T(8,128)(2,1)S(1)}, bf16[320,128]{1,0:T(8,128)(2,1)S(1)}, u32[]{:S(2)}, u32[]{:S(2)}) collective-permute-start(bf16[320,128]{1,0:T(8,128)(2,1)S(1)} %get-tuple-element.11), channel_id=1, source_target_pairs={{0,3},{1,2},{2,1},{3,0},{4,7},{5,6},{6,5},{7,4},{8,11},{9,10},{10,... | collective-permute-start | bytes 245768 | tf_op jit(solution)/shard_map/ppermute | solution.py:20
  35.5 11.4 %collective-permute-start.2 = (bf16[320,128]{1,0:T(8,128)(2,1)S(1)}, bf16[320,128]{1,0:T(8,128)(2,1)S(1)}, u32[]{:S(2)}, u32[]{:S(2)}) collective-permute-start(bf16[320,128]{1,0:T(8,128)(2,1)S(1)} %get-tuple-element.10.refs_0_), channel_id=1, source_target_pairs={{0,6},{1,7},{2,4},{3,5},{4,2},{5,3},{6,0},{7,1},{8,14},{9,15},{10,... | collective-permute-start | bytes 245768 | tf_op jit(solution)/shard_map/ppermute | solution.py:20
  39.3 7.6 %collective-permute-start.3 = (bf16[320,128]{1,0:T(8,128)(2,1)S(1)}, bf16[320,128]{1,0:T(8,128)(2,1)S(1)}, u32[]{:S(2)}, u32[]{:S(2)}) collective-permute-start(bf16[320,128]{1,0:T(8,128)(2,1)S(1)} %get-tuple-element.11), channel_id=1, source_target_pairs={{0,7},{1,6},{2,5},{3,4},{4,3},{5,2},{6,1},{7,0},{8,15},{9,14},{10,... | collective-permute-start | bytes 245768 | tf_op jit(solution)/shard_map/ppermute | solution.py:20
  41.5 23.2 %collective-permute-start.19 = (bf16[128,2560]{1,0:T(8,128)(2,1)}, bf16[128,2560]{1,0:T(8,128)(2,1)}, u32[]{:S(2)}, u32[]{:S(2)}) collective-permute-start(bf16[128,2560]{1,0:T(8,128)(2,1)} %param.9), channel_id=1, source_target_pairs={{0,1},{1,0},{2,3},{3,2},{4,5},{5,4},{6,7},{7,6},{8,9},{9,8},{10,11... | collective-permute-start | bytes 1966088 | tf_op jit(solution)/shard_map/ppermute | solution.py:20
  45.2 26.8 %collective-permute-start.13 = (bf16[128,128]{1,0:T(8,128)(2,1)S(1)}, bf16[128,128]{1,0:T(8,128)(2,1)S(1)}, u32[]{:S(2)}, u32[]{:S(2)}) collective-permute-start(bf16[128,128]{1,0:T(8,128)(2,1)S(1)} %copy-done.10), channel_id=1, source_target_pairs={{0,8},{1,9},{2,10},{3,11},{4,12},{5,13},{6,14},{7,15},{8,0},{9,1},... | collective-permute-start | bytes 98312 | tf_op jit(solution)/shard_map/ppermute | solution.py:20
  47.6 15.0 %collective-permute-start.16 = (bf16[640,128]{1,0:T(8,128)(2,1)S(1)}, bf16[640,128]{1,0:T(8,128)(2,1)S(1)}, u32[]{:S(2)}, u32[]{:S(2)}) collective-permute-start(bf16[640,128]{1,0:T(8,128)(2,1)S(1)} %get-tuple-element.17), channel_id=1, source_target_pairs={{0,4},{1,5},{2,6},{3,7},{4,0},{5,1},{6,2},{7,3},{8,12},{9,13},{10,... | collective-permute-start | bytes 491528 | tf_op jit(solution)/shard_map/ppermute | solution.py:20
  47.6 15.0 %collective-permute-start.17 = (bf16[640,128]{1,0:T(8,128)(2,1)S(1)}, bf16[640,128]{1,0:T(8,128)(2,1)S(1)}, u32[]{:S(2)}, u32[]{:S(2)}) collective-permute-start(bf16[640,128]{1,0:T(8,128)(2,1)S(1)} %get-tuple-element.17), channel_id=1, source_target_pairs={{0,6},{1,7},{2,4},{3,5},{4,2},{5,3},{6,0},{7,1},{8,14},{9,15},{10,... | collective-permute-start | bytes 491528 | tf_op jit(solution)/shard_map/ppermute | solution.py:20
  52.7 11.9 %collective-permute-start.18 = (bf16[640,128]{1,0:T(8,128)(2,1)S(1)}, bf16[640,128]{1,0:T(8,128)(2,1)S(1)}, u32[]{:S(2)}, u32[]{:S(2)}) collective-permute-start(bf16[640,128]{1,0:T(8,128)(2,1)S(1)} %get-tuple-element.17), channel_id=1, source_target_pairs={{0,2},{1,3},{2,0},{3,1},{4,6},{5,7},{6,4},{7,5},{8,10},{9,11},{10,... | collective-permute-start | bytes 491528 | tf_op jit(solution)/shard_map/ppermute | solution.py:20
  72.2 6.5 %collective-permute-start.21 = (bf16[2,128,128]{2,1,0:T(8,128)(2,1)S(1)}, bf16[2,128,128]{2,1,0:T(8,128)(2,1)S(1)}, u32[]{:S(2)}, u32[]{:S(2)}) collective-permute-start(bf16[2,128,128]{2,1,0:T(8,128)(2,1)S(1)} %pad_maximum_fusion.12), channel_id=1, source_target_pairs={{0,6},{1,7},{2,4},{3,5},{4,2},{5,3},{6,0},{7,1},{8,14},{9,15},{10,... | collective-permute-start | bytes 196616 | tf_op jit(solution)/shard_map/ppermute | solution.py:20
  73.9 6.2 %collective-permute-start.22 = (bf16[2,128,128]{2,1,0:T(8,128)(2,1)S(1)}, bf16[2,128,128]{2,1,0:T(8,128)(2,1)S(1)}, u32[]{:S(2)}, u32[]{:S(2)}) collective-permute-start(bf16[2,128,128]{2,1,0:T(8,128)(2,1)S(1)} %pad_maximum_fusion.12), channel_id=1, source_target_pairs={{0,4},{1,5},{2,6},{3,7},{4,0},{5,1},{6,2},{7,3},{8,12},{9,13},{10,... | collective-permute-start | bytes 196616 | tf_op jit(solution)/shard_map/ppermute | solution.py:20
  74.9 5.2 %collective-permute-start.23 = (bf16[2,128,128]{2,1,0:T(8,128)(2,1)S(1)}, bf16[2,128,128]{2,1,0:T(8,128)(2,1)S(1)}, u32[]{:S(2)}, u32[]{:S(2)}) collective-permute-start(bf16[2,128,128]{2,1,0:T(8,128)(2,1)S(1)} %pad_maximum_fusion.12), channel_id=1, source_target_pairs={{0,2},{1,3},{2,0},{3,1},{4,6},{5,7},{6,4},{7,5},{8,10},{9,11},{10,... | collective-permute-start | bytes 196616 | tf_op jit(solution)/shard_map/ppermute | solution.py:20
  80.5 6.3 %collective-permute-start.30 = (bf16[2,128,128]{2,1,0:T(8,128)(2,1)S(1)}, bf16[2,128,128]{2,1,0:T(8,128)(2,1)S(1)}, u32[]{:S(2)}, u32[]{:S(2)}) collective-permute-start(bf16[2,128,128]{2,1,0:T(8,128)(2,1)S(1)} %bitcast.126), channel_id=1, source_target_pairs={{0,6},{1,7},{2,4},{3,5},{4,2},{5,3},{6,0},{7,1},{8,14},{9,15},{10,... | collective-permute-start | bytes 196616 | tf_op jit(solution)/shard_map/ppermute | solution.py:20
  82.6 5.7 %collective-permute-start.31 = (bf16[2,128,128]{2,1,0:T(8,128)(2,1)S(1)}, bf16[2,128,128]{2,1,0:T(8,128)(2,1)S(1)}, u32[]{:S(2)}, u32[]{:S(2)}) collective-permute-start(bf16[2,128,128]{2,1,0:T(8,128)(2,1)S(1)} %bitcast.127), channel_id=1, source_target_pairs={{0,4},{1,5},{2,6},{3,7},{4,0},{5,1},{6,2},{7,3},{8,12},{9,13},{10,... | collective-permute-start | bytes 196616 | tf_op jit(solution)/shard_map/ppermute | solution.py:20
  82.8 5.6 %collective-permute-start.32 = (bf16[2,128,128]{2,1,0:T(8,128)(2,1)S(1)}, bf16[2,128,128]{2,1,0:T(8,128)(2,1)S(1)}, u32[]{:S(2)}, u32[]{:S(2)}) collective-permute-start(bf16[2,128,128]{2,1,0:T(8,128)(2,1)S(1)} %bitcast.128), channel_id=1, source_target_pairs={{0,2},{1,3},{2,0},{3,1},{4,6},{5,7},{6,4},{7,5},{8,10},{9,11},{10,... | collective-permute-start | bytes 196616 | tf_op jit(solution)/shard_map/ppermute | solution.py:20
  84.9 16.0 %collective-permute-start.24 = (bf16[64,128]{1,0:T(8,128)(2,1)S(1)}, bf16[64,128]{1,0:T(8,128)(2,1)S(1)}, u32[]{:S(2)}, u32[]{:S(2)}) collective-permute-start(bf16[64,128]{1,0:T(8,128)(2,1)S(1)} %constant_dynamic-slice_fusion.17), channel_id=1, source_target_pairs={{0,1},{1,0},{2,3},{3,2},{4,5},{5,4},{6,7},{7,6},{8,9},{9,8},{10,11... | collective-permute-start | bytes 49160 | tf_op jit(solution)/shard_map/ppermute | solution.py:20
  88.8 6.3 %collective-permute-start.33 = (bf16[2,128,128]{2,1,0:T(8,128)(2,1)S(1)}, bf16[2,128,128]{2,1,0:T(8,128)(2,1)S(1)}, u32[]{:S(2)}, u32[]{:S(2)}) collective-permute-start(bf16[2,128,128]{2,1,0:T(8,128)(2,1)S(1)} %pad_maximum_fusion.13), channel_id=1, source_target_pairs={{0,6},{1,7},{2,4},{3,5},{4,2},{5,3},{6,0},{7,1},{8,14},{9,15},{10,... | collective-permute-start | bytes 196616 | tf_op jit(solution)/shard_map/ppermute | solution.py:20
  91.4 5.5 %collective-permute-start.34 = (bf16[2,128,128]{2,1,0:T(8,128)(2,1)S(1)}, bf16[2,128,128]{2,1,0:T(8,128)(2,1)S(1)}, u32[]{:S(2)}, u32[]{:S(2)}) collective-permute-start(bf16[2,128,128]{2,1,0:T(8,128)(2,1)S(1)} %pad_maximum_fusion.13), channel_id=1, source_target_pairs={{0,4},{1,5},{2,6},{3,7},{4,0},{5,1},{6,2},{7,3},{8,12},{9,13},{10,... | collective-permute-start | bytes 196616 | tf_op jit(solution)/shard_map/ppermute | solution.py:20
  91.4 5.5 %collective-permute-start.35 = (bf16[2,128,128]{2,1,0:T(8,128)(2,1)S(1)}, bf16[2,128,128]{2,1,0:T(8,128)(2,1)S(1)}, u32[]{:S(2)}, u32[]{:S(2)}) collective-permute-start(bf16[2,128,128]{2,1,0:T(8,128)(2,1)S(1)} %pad_maximum_fusion.13), channel_id=1, source_target_pairs={{0,2},{1,3},{2,0},{3,1},{4,6},{5,7},{6,4},{7,5},{8,10},{9,11},{10,... | collective-permute-start | bytes 196616 | tf_op jit(solution)/shard_map/ppermute | solution.py:20
  97.4 4.9 %collective-permute-start.36 = (bf16[128,128]{1,0:T(8,128)(2,1)S(1)}, bf16[128,128]{1,0:T(8,128)(2,1)S(1)}, u32[]{:S(2)}, u32[]{:S(2)}) collective-permute-start(bf16[128,128]{1,0:T(8,128)(2,1)S(1)} %get-tuple-element.59), channel_id=1, source_target_pairs={{0,24},{1,25},{2,26},{3,27},{4,28},{5,29},{6,30},{7,31},{8,16},{9,... | collective-permute-start | bytes 98312 | tf_op jit(solution)/shard_map/ppermute | solution.py:20
  (29 other events, 182.0 us)

commit v6 on v5

--- a/solution.py
+++ b/solution.py
@@ -246,12 +246,10 @@
     def top_columns(a, value):
         return leaf_columns(value, k) if a == 0 or send_whole else value[:, 2 * base_width :]
 
-    top_rows = jnp.concatenate(
-        [
-            in_order(top_columns(a, mine), top_columns(a, other))
-            for a, (mine, other) in enumerate(zip(inverse_rows, inverse_others))
-        ]
-    )
+    top_blocks = []
+    for a, (mine, other) in enumerate(zip(inverse_rows, inverse_others)):
+        top_blocks.append(in_order(top_columns(a, mine), top_columns(a, other)))
+    top_rows = jnp.concatenate(top_blocks)
 
     update = -in_order(product(leaf_lower, s_full), product(lower_other, s_full))
     leaf_back = exchange(s_other, 0, 1)

time: 106 us -> 106 us (level)
  no operation moved by 1% of the time
where the time goes in v6:
time: 106 us; the launch traced here: 105 us
  starting transfers between devices  44.3 us (42%)
  waiting for transfers between devices  34.1 us (32%)
  other arithmetic  11.1 us (10%)
  local copies, waits for them, and re-layouts  5.45 us (5%)
  Pallas kernels  5.13 us (5%)
  matrix products  3.85 us (4%)
  between operations  1.48 us (1%)
    ppermute x40, starting transfers between devices, exchange(): return lax.ppermute(value, ('leaf', 'blk'), pairs)  44.3 us
    ppermute x40, waiting for transfers between devices, exchange(): return lax.ppermute(value, ('leaf', 'blk'), pairs)  34.1 us
    select_n x7, other arithmetic, in_order(): first = jnp.where(core == 0, mine, other)  4.38 us
    dot_general x5, matrix products, product(): return jnp.dot(matrix, vectors, preferred_element_type=jnp.float32)  3.85 us
    pallas_call x1, Pallas kernels, leaf_partial(): pl.pallas_call(body, in_specs=vmem_specs(count) + [pl.BlockSpec(memory_sp...  3.56 us
    dynamic_slice x8, local copies, waits for them, and re-layouts, leaf_columns(): lax.dynamic_slice_in_dim(value, top_offset + leaf * base_width, base_widt...  2.72 us
    eq x4, other arithmetic, mix(): hit = (targets == t)[:, :, None, None]  2.34 us
    unnamed x42, local copies, waits for them, and re-layouts  2.25 us
  transfers between devices with their start and end apart: 40, of which 18 were waited for; matrix products, arithmetic and copies ran while one was open for 16% of the time, Pallas kernels for 5%

profile of v6, /device:TPU:0, one launch (start us, length us, event | category | flops | bytes accessed | tf_op | source)
XLA Modules:
  0.0 105.4 jit_solution(1256452224375672293)
XLA Ops:
  0.6 3.0 %collective-permute-start.9 = (bf16[64,3072]{1,0:T(8,128)(2,1)}, bf16[64,3072]{1,0:T(8,128)(2,1)}, u32[]{:S(2)}, u32[]{:S(2)}) collective-permute-start(bf16[64,3072]{1,0:T(8,128)(2,1)} %param.11), channel_id=1, source_target_pairs={{0,8},{1,9},{2,10},{3,11},{4,12},{5,13},{6,14},{7,15},{8,0},{9,1},... | collective-permute-start | bytes 1179656 | tf_op jit(solution)/shard_map/ppermute | solution.py:20
  3.7 1.5 %collective-permute-start.25 = (bf16[64,3072]{1,0:T(8,128)(2,1)}, bf16[64,3072]{1,0:T(8,128)(2,1)}, u32[]{:S(2)}, u32[]{:S(2)}) collective-permute-start(bf16[64,3072]{1,0:T(8,128)(2,1)} %param.11), channel_id=1, source_target_pairs={{0,16},{1,17},{2,18},{3,19},{4,20},{5,21},{6,22},{7,23},{8,24},{9,... | collective-permute-start | bytes 1179656 | tf_op jit(solution)/shard_map/ppermute | solution.py:20
  10.6 2.5 %collective-permute-done.15 = s32[2,2]{1,0:T(2,128)S(1)} collective-permute-done((s32[2,2]{1,0:T(2,128)S(1)}, s32[2,2]{1,0:T(2,128)S(1)}, u32[]{:S(2)}, u32[]{:S(2)}) %collective-permute-start.15) | collective-permute-done | bytes 48 | tf_op jit(solution)/shard_map/ppermute | solution.py:20
  13.7 2.7 %collective-permute-start.27 = (bf16[64,3072]{1,0:T(8,128)(2,1)}, bf16[64,3072]{1,0:T(8,128)(2,1)S(1)}, u32[]{:S(2)}, u32[]{:S(2)}) collective-permute-start(bf16[64,3072]{1,0:T(8,128)(2,1)} %param.11), channel_id=1, source_target_pairs={{0,24},{1,25},{2,26},{3,27},{4,28},{5,29},{6,30},{7,31},{8,16},{9,... | collective-permute-start | bytes 1179656 | tf_op jit(solution)/shard_map/ppermute | solution.py:20
  18.1 1.8 %broadcast_select_fusion.1 = (bf16[128,1024]{1,0:T(8,128)(2,1)}, bf16[128,1024]{1,0:T(8,128)(2,1)}) fusion(bf16[128,1024]{1,0:T(8,128)(2,1)} %param.12, bf16[128,1024]{1,0:T(8,128)(2,1)S(1)} %collective-permute-done.29, pred[]{:T(512)S(6)} %eq.99), kind=kLoop, calls=%fused_computation.11 | loop fusion | flops 262144 | bytes 1048577 | tf_op jit(solution)/shard_map/jit(_where)/select_n | solution.py:182
  22.4 2.5 %collective-permute-start.6 = (bf16[320,128]{1,0:T(8,128)(2,1)S(1)}, bf16[320,128]{1,0:T(8,128)(2,1)S(1)}, u32[]{:S(2)}, u32[]{:S(2)}) collective-permute-start(bf16[320,128]{1,0:T(8,128)(2,1)S(1)} %get-tuple-element.11), channel_id=1, source_target_pairs={{0,5},{1,4},{2,7},{3,6},{4,1},{5,0},{6,3},{7,2},{8,13},{9,12},{10,... | collective-permute-start | bytes 245768 | tf_op jit(solution)/shard_map/ppermute | solution.py:20
  28.4 2.8 %collective-permute-start.5 = (bf16[320,128]{1,0:T(8,128)(2,1)S(1)}, bf16[320,128]{1,0:T(8,128)(2,1)S(1)}, u32[]{:S(2)}, u32[]{:S(2)}) collective-permute-start(bf16[320,128]{1,0:T(8,128)(2,1)S(1)} %get-tuple-element.10.refs_0_), channel_id=1, source_target_pairs={{0,4},{1,5},{2,6},{3,7},{4,0},{5,1},{6,2},{7,3},{8,12},{9,13},{10,... | collective-permute-start | bytes 245768 | tf_op jit(solution)/shard_map/ppermute | solution.py:20
  31.2 1.6 %collective-permute-start = (bf16[320,128]{1,0:T(8,128)(2,1)S(1)}, bf16[320,128]{1,0:T(8,128)(2,1)S(1)}, u32[]{:S(2)}, u32[]{:S(2)}) collective-permute-start(bf16[320,128]{1,0:T(8,128)(2,1)S(1)} %get-tuple-element.10.refs_0_), channel_id=1, source_target_pairs={{0,2},{1,3},{2,0},{3,1},{4,6},{5,7},{6,4},{7,5},{8,10},{9,11},{10,... | collective-permute-start | bytes 245768 | tf_op jit(solution)/shard_map/ppermute | solution.py:20
  35.5 3.8 %collective-permute-start.2 = (bf16[320,128]{1,0:T(8,128)(2,1)S(1)}, bf16[320,128]{1,0:T(8,128)(2,1)S(1)}, u32[]{:S(2)}, u32[]{:S(2)}) collective-permute-start(bf16[320,128]{1,0:T(8,128)(2,1)S(1)} %get-tuple-element.10.refs_0_), channel_id=1, source_target_pairs={{0,6},{1,7},{2,4},{3,5},{4,2},{5,3},{6,0},{7,1},{8,14},{9,15},{10,... | collective-permute-start | bytes 245768 | tf_op jit(solution)/shard_map/ppermute | solution.py:20
  41.7 3.6 %leaf_partial.1 = (f32[2,320,128]{2,1,0:T(8,128)S(1)}, bf16[320,1280]{1,0:T(8,128)(2,1)S(1)}, bf16[320,1280]{1,0:T(8,128)(2,1)S(1)}) custom-call(bf16[320,128]{1,0:T(8,128)(2,1)S(1)} %get-tuple-element.10.refs_0_, bf16[320,128]{1,0:T(8,128)(2,1)S(1)} %collective-permute-done.4.refs_1_, bf16[320,128]{1,0:T(8,128)(2,1)S(1)} %collective-permute-done.5.refs_2_, ...), custom_call_target="tpu_custom_call" | custom-call | flops 419430400 | bytes 3276800 | tf_op jit(solution)/shard_map/leaf_partial/pallas_call | solution.py:75
  45.2 1.7 %collective-permute-start.13 = (bf16[128,128]{1,0:T(8,128)(2,1)S(1)}, bf16[128,128]{1,0:T(8,128)(2,1)S(1)}, u32[]{:S(2)}, u32[]{:S(2)}) collective-permute-start(bf16[128,128]{1,0:T(8,128)(2,1)S(1)} %copy-done.10), channel_id=1, source_target_pairs={{0,8},{1,9},{2,10},{3,11},{4,12},{5,13},{6,14},{7,15},{8,0},{9,1},... | collective-permute-start | bytes 98312 | tf_op jit(solution)/shard_map/ppermute | solution.py:20
  47.6 3.7 %collective-permute-start.17 = (bf16[640,128]{1,0:T(8,128)(2,1)S(1)}, bf16[640,128]{1,0:T(8,128)(2,1)S(1)}, u32[]{:S(2)}, u32[]{:S(2)}) collective-permute-start(bf16[640,128]{1,0:T(8,128)(2,1)S(1)} %get-tuple-element.17), channel_id=1, source_target_pairs={{0,6},{1,7},{2,4},{3,5},{4,2},{5,3},{6,0},{7,1},{8,14},{9,15},{10,... | collective-permute-start | bytes 491528 | tf_op jit(solution)/shard_map/ppermute | solution.py:20
  53.8 8.7 %collective-permute-done.16 = bf16[640,128]{1,0:T(8,128)(2,1)S(1)} collective-permute-done((bf16[640,128]{1,0:T(8,128)(2,1)S(1)}, bf16[640,128]{1,0:T(8,128)(2,1)S(1)}, u32[]{:S(2)}, u32[]{:S(2)}) %collective-permute-start.16) | collective-permute-done | bytes 163872 | tf_op jit(solution)/shard_map/ppermute | solution.py:20
  62.6 2.0 %collective-permute-done.18 = bf16[640,128]{1,0:T(8,128)(2,1)S(1)} collective-permute-done((bf16[640,128]{1,0:T(8,128)(2,1)S(1)}, bf16[640,128]{1,0:T(8,128)(2,1)S(1)}, u32[]{:S(2)}, u32[]{:S(2)}) %collective-permute-start.18) | collective-permute-done | bytes 163872 | tf_op jit(solution)/shard_map/ppermute | solution.py:20
  64.7 1.4 %fusion.28 = f32[128,128]{0,1:T(8,128)S(1)} fusion(bf16[128,2560]{1,0:T(8,128)(2,1)} %collective-permute-done.19, bf16[2560,128]{1,0:T(8,128)(2,1)S(1)} %constant_dynamic-update-slice_fusion.1), kind=kOutput, calls=%fused_computation.144 | convolution fusion | flops 83886080 | bytes 1376256 | tf_op jit(solution)/shard_map/dot_general | solution.py:24
  66.1 1.4 %select_bitcast_fusion.1 = (f32[128,128]{1,0:T(8,128)S(1)}, f32[128,128]{1,0:T(8,128)S(1)}) fusion(f32[128,128]{0,1:T(8,128)S(1)} %fusion.28, pred[]{:T(512)S(6)} %eq.99, bf16[128,2560]{1,0:T(8,128)(2,1)} %param.9, bf16[2560,128]{1,0:T(8,128)(2,1)S(1)} %constant_dynamic-update-slice_fusion.1), kind=kOutput, calls=%fused_computation.85 | convolution fusion | flops 83918848 | bytes 1507329 | tf_op jit(solution)/shard_map/dot_general | solution.py:24
  68.3 3.6 %collective-permute-done.20 = bf16[2,2,64,128]{3,2,1,0:T(8,128)(2,1)S(1)} collective-permute-done((bf16[2,2,64,128]{3,2,1,0:T(8,128)(2,1)S(1)}, bf16[2,2,64,128]{3,2,1,0:T(8,128)(2,1)S(1)}, u32[]{:S(2)}, u32[]{:S(2)}) %collective-permute-start.20) | collective-permute-done | bytes 65568 | tf_op jit(solution)/shard_map/ppermute | solution.py:20
  72.2 1.8 %collective-permute-start.21 = (bf16[2,128,128]{2,1,0:T(8,128)(2,1)S(1)}, bf16[2,128,128]{2,1,0:T(8,128)(2,1)S(1)}, u32[]{:S(2)}, u32[]{:S(2)}) collective-permute-start(bf16[2,128,128]{2,1,0:T(8,128)(2,1)S(1)} %pad_maximum_fusion.12), channel_id=1, source_target_pairs={{0,6},{1,7},{2,4},{3,5},{4,2},{5,3},{6,0},{7,1},{8,14},{9,15},{10,... | collective-permute-start | bytes 196616 | tf_op jit(solution)/shard_map/ppermute | solution.py:20
  74.9 1.7 %collective-permute-start.23 = (bf16[2,128,128]{2,1,0:T(8,128)(2,1)S(1)}, bf16[2,128,128]{2,1,0:T(8,128)(2,1)S(1)}, u32[]{:S(2)}, u32[]{:S(2)}) collective-permute-start(bf16[2,128,128]{2,1,0:T(8,128)(2,1)S(1)} %pad_maximum_fusion.12), channel_id=1, source_target_pairs={{0,2},{1,3},{2,0},{3,1},{4,6},{5,7},{6,4},{7,5},{8,10},{9,11},{10,... | collective-permute-start | bytes 196616 | tf_op jit(solution)/shard_map/ppermute | solution.py:20
  76.7 2.0 %collective-permute-done.21 = bf16[2,128,128]{2,1,0:T(8,128)(2,1)S(1)} collective-permute-done((bf16[2,128,128]{2,1,0:T(8,128)(2,1)S(1)}, bf16[2,128,128]{2,1,0:T(8,128)(2,1)S(1)}, u32[]{:S(2)}, u32[]{:S(2)}) %collective-permute-start.21) | collective-permute-done | bytes 65568 | tf_op jit(solution)/shard_map/ppermute | solution.py:20
  78.7 1.4 %collective-permute-done.22 = bf16[2,128,128]{2,1,0:T(8,128)(2,1)S(1)} collective-permute-done((bf16[2,128,128]{2,1,0:T(8,128)(2,1)S(1)}, bf16[2,128,128]{2,1,0:T(8,128)(2,1)S(1)}, u32[]{:S(2)}, u32[]{:S(2)}) %collective-permute-start.22) | collective-permute-done | bytes 65568 | tf_op jit(solution)/shard_map/ppermute | solution.py:20
  80.5 2.1 %collective-permute-start.30 = (bf16[2,128,128]{2,1,0:T(8,128)(2,1)S(1)}, bf16[2,128,128]{2,1,0:T(8,128)(2,1)S(1)}, u32[]{:S(2)}, u32[]{:S(2)}) collective-permute-start(bf16[2,128,128]{2,1,0:T(8,128)(2,1)S(1)} %bitcast.126), channel_id=1, source_target_pairs={{0,6},{1,7},{2,4},{3,5},{4,2},{5,3},{6,0},{7,1},{8,14},{9,15},{10,... | collective-permute-start | bytes 196616 | tf_op jit(solution)/shard_map/ppermute | solution.py:20
  82.8 2.2 %collective-permute-start.32 = (bf16[2,128,128]{2,1,0:T(8,128)(2,1)S(1)}, bf16[2,128,128]{2,1,0:T(8,128)(2,1)S(1)}, u32[]{:S(2)}, u32[]{:S(2)}) collective-permute-start(bf16[2,128,128]{2,1,0:T(8,128)(2,1)S(1)} %bitcast.128), channel_id=1, source_target_pairs={{0,2},{1,3},{2,0},{3,1},{4,6},{5,7},{6,4},{7,5},{8,10},{9,11},{10,... | collective-permute-start | bytes 196616 | tf_op jit(solution)/shard_map/ppermute | solution.py:20
  85.1 1.7 %collective-permute-done.30 = bf16[2,128,128]{2,1,0:T(8,128)(2,1)S(1)} collective-permute-done((bf16[2,128,128]{2,1,0:T(8,128)(2,1)S(1)}, bf16[2,128,128]{2,1,0:T(8,128)(2,1)S(1)}, u32[]{:S(2)}, u32[]{:S(2)}) %collective-permute-start.30) | collective-permute-done | bytes 65568 | tf_op jit(solution)/shard_map/ppermute | solution.py:20
  86.8 1.5 %collective-permute-done.31 = bf16[2,128,128]{2,1,0:T(8,128)(2,1)S(1)} collective-permute-done((bf16[2,128,128]{2,1,0:T(8,128)(2,1)S(1)}, bf16[2,128,128]{2,1,0:T(8,128)(2,1)S(1)}, u32[]{:S(2)}, u32[]{:S(2)}) %collective-permute-start.31) | collective-permute-done | bytes 65568 | tf_op jit(solution)/shard_map/ppermute | solution.py:20
  88.8 2.6 %collective-permute-start.33 = (bf16[2,128,128]{2,1,0:T(8,128)(2,1)S(1)}, bf16[2,128,128]{2,1,0:T(8,128)(2,1)S(1)}, u32[]{:S(2)}, u32[]{:S(2)}) collective-permute-start(bf16[2,128,128]{2,1,0:T(8,128)(2,1)S(1)} %pad_maximum_fusion.13), channel_id=1, source_target_pairs={{0,6},{1,7},{2,4},{3,5},{4,2},{5,3},{6,0},{7,1},{8,14},{9,15},{10,... | collective-permute-start | bytes 196616 | tf_op jit(solution)/shard_map/ppermute | solution.py:20
  91.4 1.9 %collective-permute-start.35 = (bf16[2,128,128]{2,1,0:T(8,128)(2,1)S(1)}, bf16[2,128,128]{2,1,0:T(8,128)(2,1)S(1)}, u32[]{:S(2)}, u32[]{:S(2)}) collective-permute-start(bf16[2,128,128]{2,1,0:T(8,128)(2,1)S(1)} %pad_maximum_fusion.13), channel_id=1, source_target_pairs={{0,2},{1,3},{2,0},{3,1},{4,6},{5,7},{6,4},{7,5},{8,10},{9,11},{10,... | collective-permute-start | bytes 196616 | tf_op jit(solution)/shard_map/ppermute | solution.py:20
  93.4 1.8 %collective-permute-done.33 = bf16[2,128,128]{2,1,0:T(8,128)(2,1)S(1)} collective-permute-done((bf16[2,128,128]{2,1,0:T(8,128)(2,1)S(1)}, bf16[2,128,128]{2,1,0:T(8,128)(2,1)S(1)}, u32[]{:S(2)}, u32[]{:S(2)}) %collective-permute-start.33) | collective-permute-done | bytes 65568 | tf_op jit(solution)/shard_map/ppermute | solution.py:20
  95.2 1.8 %collective-permute-done.34 = bf16[2,128,128]{2,1,0:T(8,128)(2,1)S(1)} collective-permute-done((bf16[2,128,128]{2,1,0:T(8,128)(2,1)S(1)}, bf16[2,128,128]{2,1,0:T(8,128)(2,1)S(1)}, u32[]{:S(2)}, u32[]{:S(2)}) %collective-permute-start.34) | collective-permute-done | bytes 65568 | tf_op jit(solution)/shard_map/ppermute | solution.py:20
  97.4 1.6 %collective-permute-start.36 = (bf16[128,128]{1,0:T(8,128)(2,1)S(1)}, bf16[128,128]{1,0:T(8,128)(2,1)S(1)}, u32[]{:S(2)}, u32[]{:S(2)}) collective-permute-start(bf16[128,128]{1,0:T(8,128)(2,1)S(1)} %get-tuple-element.59), channel_id=1, source_target_pairs={{0,24},{1,25},{2,26},{3,27},{4,28},{5,29},{6,30},{7,31},{8,16},{9,... | collective-permute-start | bytes 98312 | tf_op jit(solution)/shard_map/ppermute | solution.py:20
  99.5 1.5 %collective-permute-start.38 = (bf16[128,128]{1,0:T(8,128)(2,1)S(1)}, bf16[128,128]{1,0:T(8,128)(2,1)S(1)}, u32[]{:S(2)}, u32[]{:S(2)}) collective-permute-start(bf16[128,128]{1,0:T(8,128)(2,1)S(1)} %get-tuple-element.60), channel_id=1, source_target_pairs={{0,8},{1,9},{2,10},{3,11},{4,12},{5,13},{6,14},{7,15},{8,0},{9,1},... | collective-permute-start | bytes 98312 | tf_op jit(solution)/shard_map/ppermute | solution.py:20
  101.0 1.3 %collective-permute-done.36 = bf16[128,128]{1,0:T(8,128)(2,1)S(1)} collective-permute-done((bf16[128,128]{1,0:T(8,128)(2,1)S(1)}, bf16[128,128]{1,0:T(8,128)(2,1)S(1)}, u32[]{:S(2)}, u32[]{:S(2)}) %collective-permute-start.36) | collective-permute-done | bytes 32800 | tf_op jit(solution)/shard_map/ppermute | solution.py:20
  (167 shorter events, 28.8 us)
Async XLA Ops:
  0.6 20.5 %collective-permute-start.9 = (bf16[64,3072]{1,0:T(8,128)(2,1)}, bf16[64,3072]{1,0:T(8,128)(2,1)}, u32[]{:S(2)}, u32[]{:S(2)}) collective-permute-start(bf16[64,3072]{1,0:T(8,128)(2,1)} %param.11), channel_id=1, source_target_pairs={{0,8},{1,9},{2,10},{3,11},{4,12},{5,13},{6,14},{7,15},{8,0},{9,1},... | collective-permute-start | bytes 1179656 | tf_op jit(solution)/shard_map/ppermute | solution.py:20
  3.7 16.2 %collective-permute-start.11 = (bf16[64,3072]{1,0:T(8,128)(2,1)}, bf16[64,3072]{1,0:T(8,128)(2,1)S(1)}, u32[]{:S(2)}, u32[]{:S(2)}) collective-permute-start(bf16[64,3072]{1,0:T(8,128)(2,1)} %param.11), channel_id=1, source_target_pairs={{0,1},{1,0},{2,3},{3,2},{4,5},{5,4},{6,7},{7,6},{8,9},{9,8},{10,11... | collective-permute-start | bytes 1179656 | tf_op jit(solution)/shard_map/ppermute | solution.py:20
  3.7 18.7 %collective-permute-start.25 = (bf16[64,3072]{1,0:T(8,128)(2,1)}, bf16[64,3072]{1,0:T(8,128)(2,1)}, u32[]{:S(2)}, u32[]{:S(2)}) collective-permute-start(bf16[64,3072]{1,0:T(8,128)(2,1)} %param.11), channel_id=1, source_target_pairs={{0,16},{1,17},{2,18},{3,19},{4,20},{5,21},{6,22},{7,23},{8,24},{9,... | collective-permute-start | bytes 1179656 | tf_op jit(solution)/shard_map/ppermute | solution.py:20
  5.4 8.3 %collective-permute-start.12 = (bf16[2,64,256]{2,1,0:T(8,128)(2,1)}, bf16[2,64,256]{2,1,0:T(8,128)(2,1)S(1)}, u32[]{:S(2)}, u32[]{:S(2)}) collective-permute-start(bf16[2,64,256]{2,1,0:T(8,128)(2,1)} %param.10), channel_id=1, source_target_pairs={{0,1},{1,0},{2,3},{3,2},{4,5},{5,4},{6,7},{7,6},{8,9},{9,8},{10,11... | collective-permute-start | bytes 196616 | tf_op jit(solution)/shard_map/ppermute | solution.py:20
  13.1 4.7 %collective-permute-start.29 = (bf16[128,1024]{1,0:T(8,128)(2,1)}, bf16[128,1024]{1,0:T(8,128)(2,1)S(1)}, u32[]{:S(2)}, u32[]{:S(2)}) collective-permute-start(bf16[128,1024]{1,0:T(8,128)(2,1)} %param.12), channel_id=1, source_target_pairs={{0,1},{1,0},{2,3},{3,2},{4,5},{5,4},{6,7},{7,6},{8,9},{9,8},{10,11... | collective-permute-start | bytes 786440 | tf_op jit(solution)/shard_map/ppermute | solution.py:20
  13.7 12.7 %collective-permute-start.27 = (bf16[64,3072]{1,0:T(8,128)(2,1)}, bf16[64,3072]{1,0:T(8,128)(2,1)S(1)}, u32[]{:S(2)}, u32[]{:S(2)}) collective-permute-start(bf16[64,3072]{1,0:T(8,128)(2,1)} %param.11), channel_id=1, source_target_pairs={{0,24},{1,25},{2,26},{3,27},{4,28},{5,29},{6,30},{7,31},{8,16},{9,... | collective-permute-start | bytes 1179656 | tf_op jit(solution)/shard_map/ppermute | solution.py:20
  17.8 17.0 %collective-permute-start.4 = (bf16[320,128]{1,0:T(8,128)(2,1)S(1)}, bf16[320,128]{1,0:T(8,128)(2,1)S(1)}, u32[]{:S(2)}, u32[]{:S(2)}) collective-permute-start(bf16[320,128]{1,0:T(8,128)(2,1)S(1)} %get-tuple-element.11), channel_id=1, source_target_pairs={{0,1},{1,0},{2,3},{3,2},{4,5},{5,4},{6,7},{7,6},{8,9},{9,8},{10,11... | collective-permute-start | bytes 245768 | tf_op jit(solution)/shard_map/ppermute | solution.py:20
  19.9 19.5 %collective-permute-start.7 = (bf16[320,2560]{1,0:T(8,128)(2,1)S(1)}, bf16[320,2560]{1,0:T(8,128)(2,1)S(1)}, u32[]{:S(2)}, u32[]{:S(2)}) collective-permute-start(bf16[320,2560]{1,0:T(8,128)(2,1)S(1)} %copy-done), channel_id=1, source_target_pairs={{0,1},{1,0},{2,3},{3,2},{4,5},{5,4},{6,7},{7,6},{8,9},{9,8},{10,11... | collective-permute-start | bytes 4915208 | tf_op jit(solution)/shard_map/ppermute | solution.py:20
  21.2 5.3 %collective-permute-start.10 = (bf16[64,3072]{1,0:T(8,128)(2,1)}, bf16[64,3072]{1,0:T(8,128)(2,1)S(1)}, u32[]{:S(2)}, u32[]{:S(2)}) collective-permute-start(bf16[64,3072]{1,0:T(8,128)(2,1)} %collective-permute-done.9), channel_id=1, source_target_pairs={{0,1},{1,0},{2,3},{3,2},{4,5},{5,4},{6,7},{7,6},{8,9},{9,8},{10,11... | collective-permute-start | bytes 1179656 | tf_op jit(solution)/shard_map/ppermute | solution.py:20
  22.4 16.9 %collective-permute-start.6 = (bf16[320,128]{1,0:T(8,128)(2,1)S(1)}, bf16[320,128]{1,0:T(8,128)(2,1)S(1)}, u32[]{:S(2)}, u32[]{:S(2)}) collective-permute-start(bf16[320,128]{1,0:T(8,128)(2,1)S(1)} %get-tuple-element.11), channel_id=1, source_target_pairs={{0,5},{1,4},{2,7},{3,6},{4,1},{5,0},{6,3},{7,2},{8,13},{9,12},{10,... | collective-permute-start | bytes 245768 | tf_op jit(solution)/shard_map/ppermute | solution.py:20
  26.4 4.8 %collective-permute-start.28 = (bf16[64,3072]{1,0:T(8,128)(2,1)S(1)}, bf16[64,3072]{1,0:T(8,128)(2,1)S(1)}, u32[]{:S(2)}, u32[]{:S(2)}) collective-permute-start(bf16[64,3072]{1,0:T(8,128)(2,1)S(1)} %collective-permute-done.27), channel_id=1, source_target_pairs={{0,1},{1,0},{2,3},{3,2},{4,5},{5,4},{6,7},{7,6},{8,9},{9,8},{10,11... | collective-permute-start | bytes 1179656 | tf_op jit(solution)/shard_map/ppermute | solution.py:20
  28.4 7.1 %collective-permute-start.5 = (bf16[320,128]{1,0:T(8,128)(2,1)S(1)}, bf16[320,128]{1,0:T(8,128)(2,1)S(1)}, u32[]{:S(2)}, u32[]{:S(2)}) collective-permute-start(bf16[320,128]{1,0:T(8,128)(2,1)S(1)} %get-tuple-element.10.refs_0_), channel_id=1, source_target_pairs={{0,4},{1,5},{2,6},{3,7},{4,0},{5,1},{6,2},{7,3},{8,12},{9,13},{10,... | collective-permute-start | bytes 245768 | tf_op jit(solution)/shard_map/ppermute | solution.py:20
  31.2 14.0 %collective-permute-start = (bf16[320,128]{1,0:T(8,128)(2,1)S(1)}, bf16[320,128]{1,0:T(8,128)(2,1)S(1)}, u32[]{:S(2)}, u32[]{:S(2)}) collective-permute-start(bf16[320,128]{1,0:T(8,128)(2,1)S(1)} %get-tuple-element.10.refs_0_), channel_id=1, source_target_pairs={{0,2},{1,3},{2,0},{3,1},{4,6},{5,7},{6,4},{7,5},{8,10},{9,11},{10,... | collective-permute-start | bytes 245768 | tf_op jit(solution)/shard_map/ppermute | solution.py:20
  34.8 12.1 %collective-permute-start.1 = (bf16[320,128]{1,0:T(8,128)(2,1)S(1)}, bf16[320,128]{1,0:T(8,128)(2,1)S(1)}, u32[]{:S(2)}, u32[]{:S(2)}) collective-permute-start(bf16[320,128]{1,0:T(8,128)(2,1)S(1)} %get-tuple-element.11), channel_id=1, source_target_pairs={{0,3},{1,2},{2,1},{3,0},{4,7},{5,6},{6,5},{7,4},{8,11},{9,10},{10,... | collective-permute-start | bytes 245768 | tf_op jit(solution)/shard_map/ppermute | solution.py:20
  35.5 11.4 %collective-permute-start.2 = (bf16[320,128]{1,0:T(8,128)(2,1)S(1)}, bf16[320,128]{1,0:T(8,128)(2,1)S(1)}, u32[]{:S(2)}, u32[]{:S(2)}) collective-permute-start(bf16[320,128]{1,0:T(8,128)(2,1)S(1)} %get-tuple-element.10.refs_0_), channel_id=1, source_target_pairs={{0,6},{1,7},{2,4},{3,5},{4,2},{5,3},{6,0},{7,1},{8,14},{9,15},{10,... | collective-permute-start | bytes 245768 | tf_op jit(solution)/shard_map/ppermute | solution.py:20
  39.3 7.6 %collective-permute-start.3 = (bf16[320,128]{1,0:T(8,128)(2,1)S(1)}, bf16[320,128]{1,0:T(8,128)(2,1)S(1)}, u32[]{:S(2)}, u32[]{:S(2)}) collective-permute-start(bf16[320,128]{1,0:T(8,128)(2,1)S(1)} %get-tuple-element.11), channel_id=1, source_target_pairs={{0,7},{1,6},{2,5},{3,4},{4,3},{5,2},{6,1},{7,0},{8,15},{9,14},{10,... | collective-permute-start | bytes 245768 | tf_op jit(solution)/shard_map/ppermute | solution.py:20
  41.5 23.2 %collective-permute-start.19 = (bf16[128,2560]{1,0:T(8,128)(2,1)}, bf16[128,2560]{1,0:T(8,128)(2,1)}, u32[]{:S(2)}, u32[]{:S(2)}) collective-permute-start(bf16[128,2560]{1,0:T(8,128)(2,1)} %param.9), channel_id=1, source_target_pairs={{0,1},{1,0},{2,3},{3,2},{4,5},{5,4},{6,7},{7,6},{8,9},{9,8},{10,11... | collective-permute-start | bytes 1966088 | tf_op jit(solution)/shard_map/ppermute | solution.py:20
  45.2 26.8 %collective-permute-start.13 = (bf16[128,128]{1,0:T(8,128)(2,1)S(1)}, bf16[128,128]{1,0:T(8,128)(2,1)S(1)}, u32[]{:S(2)}, u32[]{:S(2)}) collective-permute-start(bf16[128,128]{1,0:T(8,128)(2,1)S(1)} %copy-done.10), channel_id=1, source_target_pairs={{0,8},{1,9},{2,10},{3,11},{4,12},{5,13},{6,14},{7,15},{8,0},{9,1},... | collective-permute-start | bytes 98312 | tf_op jit(solution)/shard_map/ppermute | solution.py:20
  47.6 15.0 %collective-permute-start.16 = (bf16[640,128]{1,0:T(8,128)(2,1)S(1)}, bf16[640,128]{1,0:T(8,128)(2,1)S(1)}, u32[]{:S(2)}, u32[]{:S(2)}) collective-permute-start(bf16[640,128]{1,0:T(8,128)(2,1)S(1)} %get-tuple-element.17), channel_id=1, source_target_pairs={{0,4},{1,5},{2,6},{3,7},{4,0},{5,1},{6,2},{7,3},{8,12},{9,13},{10,... | collective-permute-start | bytes 491528 | tf_op jit(solution)/shard_map/ppermute | solution.py:20
  47.6 15.0 %collective-permute-start.17 = (bf16[640,128]{1,0:T(8,128)(2,1)S(1)}, bf16[640,128]{1,0:T(8,128)(2,1)S(1)}, u32[]{:S(2)}, u32[]{:S(2)}) collective-permute-start(bf16[640,128]{1,0:T(8,128)(2,1)S(1)} %get-tuple-element.17), channel_id=1, source_target_pairs={{0,6},{1,7},{2,4},{3,5},{4,2},{5,3},{6,0},{7,1},{8,14},{9,15},{10,... | collective-permute-start | bytes 491528 | tf_op jit(solution)/shard_map/ppermute | solution.py:20
  52.7 11.9 %collective-permute-start.18 = (bf16[640,128]{1,0:T(8,128)(2,1)S(1)}, bf16[640,128]{1,0:T(8,128)(2,1)S(1)}, u32[]{:S(2)}, u32[]{:S(2)}) collective-permute-start(bf16[640,128]{1,0:T(8,128)(2,1)S(1)} %get-tuple-element.17), channel_id=1, source_target_pairs={{0,2},{1,3},{2,0},{3,1},{4,6},{5,7},{6,4},{7,5},{8,10},{9,11},{10,... | collective-permute-start | bytes 491528 | tf_op jit(solution)/shard_map/ppermute | solution.py:20
  72.2 6.5 %collective-permute-start.21 = (bf16[2,128,128]{2,1,0:T(8,128)(2,1)S(1)}, bf16[2,128,128]{2,1,0:T(8,128)(2,1)S(1)}, u32[]{:S(2)}, u32[]{:S(2)}) collective-permute-start(bf16[2,128,128]{2,1,0:T(8,128)(2,1)S(1)} %pad_maximum_fusion.12), channel_id=1, source_target_pairs={{0,6},{1,7},{2,4},{3,5},{4,2},{5,3},{6,0},{7,1},{8,14},{9,15},{10,... | collective-permute-start | bytes 196616 | tf_op jit(solution)/shard_map/ppermute | solution.py:20
  73.9 6.2 %collective-permute-start.22 = (bf16[2,128,128]{2,1,0:T(8,128)(2,1)S(1)}, bf16[2,128,128]{2,1,0:T(8,128)(2,1)S(1)}, u32[]{:S(2)}, u32[]{:S(2)}) collective-permute-start(bf16[2,128,128]{2,1,0:T(8,128)(2,1)S(1)} %pad_maximum_fusion.12), channel_id=1, source_target_pairs={{0,4},{1,5},{2,6},{3,7},{4,0},{5,1},{6,2},{7,3},{8,12},{9,13},{10,... | collective-permute-start | bytes 196616 | tf_op jit(solution)/shard_map/ppermute | solution.py:20
  74.9 5.2 %collective-permute-start.23 = (bf16[2,128,128]{2,1,0:T(8,128)(2,1)S(1)}, bf16[2,128,128]{2,1,0:T(8,128)(2,1)S(1)}, u32[]{:S(2)}, u32[]{:S(2)}) collective-permute-start(bf16[2,128,128]{2,1,0:T(8,128)(2,1)S(1)} %pad_maximum_fusion.12), channel_id=1, source_target_pairs={{0,2},{1,3},{2,0},{3,1},{4,6},{5,7},{6,4},{7,5},{8,10},{9,11},{10,... | collective-permute-start | bytes 196616 | tf_op jit(solution)/shard_map/ppermute | solution.py:20
  80.5 6.3 %collective-permute-start.30 = (bf16[2,128,128]{2,1,0:T(8,128)(2,1)S(1)}, bf16[2,128,128]{2,1,0:T(8,128)(2,1)S(1)}, u32[]{:S(2)}, u32[]{:S(2)}) collective-permute-start(bf16[2,128,128]{2,1,0:T(8,128)(2,1)S(1)} %bitcast.126), channel_id=1, source_target_pairs={{0,6},{1,7},{2,4},{3,5},{4,2},{5,3},{6,0},{7,1},{8,14},{9,15},{10,... | collective-permute-start | bytes 196616 | tf_op jit(solution)/shard_map/ppermute | solution.py:20
  82.6 5.7 %collective-permute-start.31 = (bf16[2,128,128]{2,1,0:T(8,128)(2,1)S(1)}, bf16[2,128,128]{2,1,0:T(8,128)(2,1)S(1)}, u32[]{:S(2)}, u32[]{:S(2)}) collective-permute-start(bf16[2,128,128]{2,1,0:T(8,128)(2,1)S(1)} %bitcast.127), channel_id=1, source_target_pairs={{0,4},{1,5},{2,6},{3,7},{4,0},{5,1},{6,2},{7,3},{8,12},{9,13},{10,... | collective-permute-start | bytes 196616 | tf_op jit(solution)/shard_map/ppermute | solution.py:20
  82.8 5.6 %collective-permute-start.32 = (bf16[2,128,128]{2,1,0:T(8,128)(2,1)S(1)}, bf16[2,128,128]{2,1,0:T(8,128)(2,1)S(1)}, u32[]{:S(2)}, u32[]{:S(2)}) collective-permute-start(bf16[2,128,128]{2,1,0:T(8,128)(2,1)S(1)} %bitcast.128), channel_id=1, source_target_pairs={{0,2},{1,3},{2,0},{3,1},{4,6},{5,7},{6,4},{7,5},{8,10},{9,11},{10,... | collective-permute-start | bytes 196616 | tf_op jit(solution)/shard_map/ppermute | solution.py:20
  84.9 16.0 %collective-permute-start.24 = (bf16[64,128]{1,0:T(8,128)(2,1)S(1)}, bf16[64,128]{1,0:T(8,128)(2,1)S(1)}, u32[]{:S(2)}, u32[]{:S(2)}) collective-permute-start(bf16[64,128]{1,0:T(8,128)(2,1)S(1)} %constant_dynamic-slice_fusion.17), channel_id=1, source_target_pairs={{0,1},{1,0},{2,3},{3,2},{4,5},{5,4},{6,7},{7,6},{8,9},{9,8},{10,11... | collective-permute-start | bytes 49160 | tf_op jit(solution)/shard_map/ppermute | solution.py:20
  88.8 6.3 %collective-permute-start.33 = (bf16[2,128,128]{2,1,0:T(8,128)(2,1)S(1)}, bf16[2,128,128]{2,1,0:T(8,128)(2,1)S(1)}, u32[]{:S(2)}, u32[]{:S(2)}) collective-permute-start(bf16[2,128,128]{2,1,0:T(8,128)(2,1)S(1)} %pad_maximum_fusion.13), channel_id=1, source_target_pairs={{0,6},{1,7},{2,4},{3,5},{4,2},{5,3},{6,0},{7,1},{8,14},{9,15},{10,... | collective-permute-start | bytes 196616 | tf_op jit(solution)/shard_map/ppermute | solution.py:20
  91.4 5.5 %collective-permute-start.34 = (bf16[2,128,128]{2,1,0:T(8,128)(2,1)S(1)}, bf16[2,128,128]{2,1,0:T(8,128)(2,1)S(1)}, u32[]{:S(2)}, u32[]{:S(2)}) collective-permute-start(bf16[2,128,128]{2,1,0:T(8,128)(2,1)S(1)} %pad_maximum_fusion.13), channel_id=1, source_target_pairs={{0,4},{1,5},{2,6},{3,7},{4,0},{5,1},{6,2},{7,3},{8,12},{9,13},{10,... | collective-permute-start | bytes 196616 | tf_op jit(solution)/shard_map/ppermute | solution.py:20
  91.4 5.5 %collective-permute-start.35 = (bf16[2,128,128]{2,1,0:T(8,128)(2,1)S(1)}, bf16[2,128,128]{2,1,0:T(8,128)(2,1)S(1)}, u32[]{:S(2)}, u32[]{:S(2)}) collective-permute-start(bf16[2,128,128]{2,1,0:T(8,128)(2,1)S(1)} %pad_maximum_fusion.13), channel_id=1, source_target_pairs={{0,2},{1,3},{2,0},{3,1},{4,6},{5,7},{6,4},{7,5},{8,10},{9,11},{10,... | collective-permute-start | bytes 196616 | tf_op jit(solution)/shard_map/ppermute | solution.py:20
  97.4 4.9 %collective-permute-start.36 = (bf16[128,128]{1,0:T(8,128)(2,1)S(1)}, bf16[128,128]{1,0:T(8,128)(2,1)S(1)}, u32[]{:S(2)}, u32[]{:S(2)}) collective-permute-start(bf16[128,128]{1,0:T(8,128)(2,1)S(1)} %get-tuple-element.59), channel_id=1, source_target_pairs={{0,24},{1,25},{2,26},{3,27},{4,28},{5,29},{6,30},{7,31},{8,16},{9,... | collective-permute-start | bytes 98312 | tf_op jit(solution)/shard_map/ppermute | solution.py:20
  (29 other events, 182.0 us)

commit v7 on v6

--- a/solution.py
+++ b/solution.py
@@ -249,9 +249,10 @@
     top_blocks = []
     for a, (mine, other) in enumerate(zip(inverse_rows, inverse_others)):
         top_blocks.append(in_order(top_columns(a, mine), top_columns(a, other)))
-    top_rows = jnp.concatenate(top_blocks)
-
-    update = -in_order(product(leaf_lower, s_full), product(lower_other, s_full))
+    top_rows = jnp.concatenate(top_blocks[1:])
+
+    lower_chip = in_order(leaf_lower, lower_other)
+    update = -product(lower_chip, s_full)
     leaf_back = exchange(s_other, 0, 1)
     leaf_solution = in_order(s_mine, leaf_back, 1)
 
@@ -334,11 +335,11 @@
     own = own + seps[levels - 1].astype(jnp.float32)
     parts = gather_z(jnp.stack([own, sent]).astype(dtype))
     contributions = jnp.swapaxes(parts, 0, 1).reshape(-1, half)
-    partial = product(top_rows, contributions).reshape(leaves, 2 * pivots, half)
-    rounded = partial.astype(dtype)
-    total = partial[0]
+    sent_rows = product(top_rows, contributions)
+    rounded = sent_rows.astype(dtype).reshape(leaves - 1, 2 * pivots, half)
+    total = product(top_blocks[0], contributions)
     for a in range(leaves - 1, 0, -1):
-        total = total + exchange(rounded[a], a, 0).astype(jnp.float32)
+        total = total + exchange(rounded[a - 1], a, 0).astype(jnp.float32)
     solutions.append(total.astype(dtype))
 
     outs = []

time: 106 us -> 104 us (0.981)
  waiting for transfers between devices: 34.1 us -> 38.6 us
  matrix products: 3.85 us -> 1.65 us
  other arithmetic: 11.1 us -> 9.17 us
  starting transfers between devices: 44.3 us -> 43.2 us
    ppermute x40, waiting for transfers between devices: 34.1 us -> 38.6 us  [exchange(): return lax.ppermute(value, ('leaf', 'blk'), pairs)]
    eq x4, other arithmetic: 2.34 us -> 0.04 us  [mix(): hit = (targets == t)[:, :, None, None]]
    dot_general x5, matrix products: 3.85 us -> 1.65 us  [product(): return jnp.dot(matrix, vectors, preferred_element_type=jnp.float32)]
    ppermute x40, starting transfers between devices: 44.3 us -> 43.2 us  [exchange(): return lax.ppermute(value, ('leaf', 'blk'), pairs)]
    select_n x7 -> x9, other arithmetic: 4.38 us -> 5.44 us  [in_order(): first = jnp.where(core == 0, mine, other)]
    unnamed x42 -> x30, local copies, waits for them, and re-layouts: 2.25 us -> 2.15 us
  transfers between devices with their start and end apart: 40 -> 40, of which waited for: 18 -> 20; matrix products, arithmetic and copies ran while one was open for 16% -> 11% of each run, Pallas kernels for 5% -> 5%
where the time goes in v7:
time: 104 us
  starting transfers between devices  43.2 us (42%)
  waiting for transfers between devices  38.6 us (37%)
  other arithmetic  9.17 us (9%)
  Pallas kernels  5.13 us (5%)
  local copies, waits for them, and re-layouts  4.46 us (4%)
  matrix products  1.65 us (2%)
  between operations  1.43 us (1%)
    ppermute x40, starting transfers between devices, exchange(): return lax.ppermute(value, ('leaf', 'blk'), pairs)  43.2 us
    ppermute x40, waiting for transfers between devices, exchange(): return lax.ppermute(value, ('leaf', 'blk'), pairs)  38.6 us
    select_n x9, other arithmetic, in_order(): first = jnp.where(core == 0, mine, other)  5.44 us
    pallas_call x1, Pallas kernels, leaf_partial(): pl.pallas_call(body, in_specs=vmem_specs(count) + [pl.BlockSpec(memory_sp...  3.56 us
    unnamed x30, local copies, waits for them, and re-layouts  2.15 us
  transfers between devices with their start and end apart: 40, of which 20 were waited for; matrix products, arithmetic and copies ran while one was open for 11% of the time, Pallas kernels for 5%

profile of v7, /device:TPU:0, one launch (start us, length us, event | category | flops | bytes accessed | tf_op | source)
XLA Modules:
  0.0 103.6 jit_solution(16570300013312596519)
XLA Ops:
  0.7 3.0 %collective-permute-start.9 = (bf16[64,3072]{1,0:T(8,128)(2,1)}, bf16[64,3072]{1,0:T(8,128)(2,1)S(1)}, u32[]{:S(2)}, u32[]{:S(2)}) collective-permute-start(bf16[64,3072]{1,0:T(8,128)(2,1)} %param.11), channel_id=1, source_target_pairs={{0,8},{1,9},{2,10},{3,11},{4,12},{5,13},{6,14},{7,15},{8,0},{9,1},... | collective-permute-start | bytes 1179656 | tf_op jit(solution)/shard_map/ppermute | solution.py:20
  3.7 1.5 %collective-permute-start.32 = (bf16[64,3072]{1,0:T(8,128)(2,1)}, bf16[64,3072]{1,0:T(8,128)(2,1)}, u32[]{:S(2)}, u32[]{:S(2)}) collective-permute-start(bf16[64,3072]{1,0:T(8,128)(2,1)} %param.11), channel_id=1, source_target_pairs={{0,16},{1,17},{2,18},{3,19},{4,20},{5,21},{6,22},{7,23},{8,24},{9,... | collective-permute-start | bytes 1179656 | tf_op jit(solution)/shard_map/ppermute | solution.py:20
  9.0 4.1 %collective-permute-done.15 = s32[2,2]{1,0:T(2,128)S(1)} collective-permute-done((s32[2,2]{1,0:T(2,128)S(1)}, s32[2,2]{1,0:T(2,128)S(1)}, u32[]{:S(2)}, u32[]{:S(2)}) %collective-permute-start.15) | collective-permute-done | bytes 48 | tf_op jit(solution)/shard_map/ppermute | solution.py:20
  13.1 2.8 %collective-permute-start.34 = (bf16[64,3072]{1,0:T(8,128)(2,1)}, bf16[64,3072]{1,0:T(8,128)(2,1)S(1)}, u32[]{:S(2)}, u32[]{:S(2)}) collective-permute-start(bf16[64,3072]{1,0:T(8,128)(2,1)} %param.11), channel_id=1, source_target_pairs={{0,24},{1,25},{2,26},{3,27},{4,28},{5,29},{6,30},{7,31},{8,16},{9,... | collective-permute-start | bytes 1179656 | tf_op jit(solution)/shard_map/ppermute | solution.py:20
  17.0 1.8 %broadcast_select_fusion.3 = (bf16[128,1024]{1,0:T(8,128)(2,1)}, bf16[128,1024]{1,0:T(8,128)(2,1)}) fusion(bf16[128,1024]{1,0:T(8,128)(2,1)} %param.12, bf16[128,1024]{1,0:T(8,128)(2,1)S(1)} %collective-permute-done.25, pred[]{:T(512)S(6)} %eq.99), kind=kLoop, calls=%fused_computation.26 | loop fusion | flops 262144 | bytes 1048577 | tf_op jit(solution)/shard_map/jit(_where)/select_n | solution.py:182
  18.8 2.5 %collective-permute-start.6 = (bf16[320,128]{1,0:T(8,128)(2,1)S(1)}, bf16[320,128]{1,0:T(8,128)(2,1)S(1)}, u32[]{:S(2)}, u32[]{:S(2)}) collective-permute-start(bf16[320,128]{1,0:T(8,128)(2,1)S(1)} %get-tuple-element.11), channel_id=1, source_target_pairs={{0,5},{1,4},{2,7},{3,6},{4,1},{5,0},{6,3},{7,2},{8,13},{9,12},{10,... | collective-permute-start | bytes 245768 | tf_op jit(solution)/shard_map/ppermute | solution.py:20
  22.5 3.4 %collective-permute-done.34 = bf16[64,3072]{1,0:T(8,128)(2,1)S(1)} collective-permute-done((bf16[64,3072]{1,0:T(8,128)(2,1)}, bf16[64,3072]{1,0:T(8,128)(2,1)S(1)}, u32[]{:S(2)}, u32[]{:S(2)}) %collective-permute-start.34) | collective-permute-done | bytes 393248 | tf_op jit(solution)/shard_map/ppermute | solution.py:20
  30.5 2.8 %collective-permute-start.5 = (bf16[320,128]{1,0:T(8,128)(2,1)S(1)}, bf16[320,128]{1,0:T(8,128)(2,1)S(1)}, u32[]{:S(2)}, u32[]{:S(2)}) collective-permute-start(bf16[320,128]{1,0:T(8,128)(2,1)S(1)} %get-tuple-element.10.refs_0_), channel_id=1, source_target_pairs={{0,4},{1,5},{2,6},{3,7},{4,0},{5,1},{6,2},{7,3},{8,12},{9,13},{10,... | collective-permute-start | bytes 245768 | tf_op jit(solution)/shard_map/ppermute | solution.py:20
  33.4 1.6 %collective-permute-start = (bf16[320,128]{1,0:T(8,128)(2,1)S(1)}, bf16[320,128]{1,0:T(8,128)(2,1)S(1)}, u32[]{:S(2)}, u32[]{:S(2)}) collective-permute-start(bf16[320,128]{1,0:T(8,128)(2,1)S(1)} %get-tuple-element.10.refs_0_), channel_id=1, source_target_pairs={{0,2},{1,3},{2,0},{3,1},{4,6},{5,7},{6,4},{7,5},{8,10},{9,11},{10,... | collective-permute-start | bytes 245768 | tf_op jit(solution)/shard_map/ppermute | solution.py:20
  36.1 1.7 %collective-permute-done.5.refs_2_ = bf16[320,128]{1,0:T(8,128)(2,1)S(1)} collective-permute-done((bf16[320,128]{1,0:T(8,128)(2,1)S(1)}, bf16[320,128]{1,0:T(8,128)(2,1)S(1)}, u32[]{:S(2)}, u32[]{:S(2)}) %collective-permute-start.5) | collective-permute-done | bytes 81952 | tf_op jit(solution)/shard_map/ppermute | solution.py:20
  37.9 3.5 %collective-permute-start.2 = (bf16[320,128]{1,0:T(8,128)(2,1)S(1)}, bf16[320,128]{1,0:T(8,128)(2,1)S(1)}, u32[]{:S(2)}, u32[]{:S(2)}) collective-permute-start(bf16[320,128]{1,0:T(8,128)(2,1)S(1)} %get-tuple-element.10.refs_0_), channel_id=1, source_target_pairs={{0,6},{1,7},{2,4},{3,5},{4,2},{5,3},{6,0},{7,1},{8,14},{9,15},{10,... | collective-permute-start | bytes 245768 | tf_op jit(solution)/shard_map/ppermute | solution.py:20
  42.3 1.2 %copy-done.1 = bf16[320,2560]{1,0:T(8,128)(2,1)} copy-done((bf16[320,2560]{1,0:T(8,128)(2,1)}, bf16[320,2560]{1,0:T(8,128)(2,1)S(1)}, u32[]{:S(2)}) %copy-start.1) | copy-done | bytes 1638424
  43.6 1.5 %collective-permute-start.13 = (bf16[128,128]{1,0:T(8,128)(2,1)S(1)}, bf16[128,128]{1,0:T(8,128)(2,1)S(1)}, u32[]{:S(2)}, u32[]{:S(2)}) collective-permute-start(bf16[128,128]{1,0:T(8,128)(2,1)S(1)} %fusion.28), channel_id=1, source_target_pairs={{0,8},{1,9},{2,10},{3,11},{4,12},{5,13},{6,14},{7,15},{8,0},{9,1},... | collective-permute-start | bytes 98312 | tf_op jit(solution)/shard_map/ppermute | solution.py:20
  45.0 3.6 %leaf_partial.1 = (f32[2,320,128]{2,1,0:T(8,128)S(1)}, bf16[320,1280]{1,0:T(8,128)(2,1)S(1)}, bf16[320,1280]{1,0:T(8,128)(2,1)S(1)}) custom-call(bf16[320,128]{1,0:T(8,128)(2,1)S(1)} %get-tuple-element.10.refs_0_, bf16[320,128]{1,0:T(8,128)(2,1)S(1)} %collective-permute-done.4.refs_1_, bf16[320,128]{1,0:T(8,128)(2,1)S(1)} %collective-permute-done.5.refs_2_, ...), custom_call_target="tpu_custom_call" | custom-call | flops 419430400 | bytes 3276800 | tf_op jit(solution)/shard_map/leaf_partial/pallas_call | solution.py:75
  49.4 3.2 %collective-permute-start.18 = (bf16[640,128]{1,0:T(8,128)(2,1)S(1)}, bf16[640,128]{1,0:T(8,128)(2,1)S(1)}, u32[]{:S(2)}, u32[]{:S(2)}) collective-permute-start(bf16[640,128]{1,0:T(8,128)(2,1)S(1)} %get-tuple-element.17), channel_id=1, source_target_pairs={{0,6},{1,7},{2,4},{3,5},{4,2},{5,3},{6,0},{7,1},{8,14},{9,15},{10,... | collective-permute-start | bytes 491528 | tf_op jit(solution)/shard_map/ppermute | solution.py:20
  55.0 9.4 %collective-permute-done.17 = bf16[640,128]{1,0:T(8,128)(2,1)S(1)} collective-permute-done((bf16[640,128]{1,0:T(8,128)(2,1)S(1)}, bf16[640,128]{1,0:T(8,128)(2,1)S(1)}, u32[]{:S(2)}, u32[]{:S(2)}) %collective-permute-start.17) | collective-permute-done | bytes 163872 | tf_op jit(solution)/shard_map/ppermute | solution.py:20
  66.2 3.7 %collective-permute-done.20 = bf16[2,2,64,128]{3,2,1,0:T(8,128)(2,1)S(1)} collective-permute-done((bf16[2,2,64,128]{3,2,1,0:T(8,128)(2,1)S(1)}, bf16[2,2,64,128]{3,2,1,0:T(8,128)(2,1)S(1)}, u32[]{:S(2)}, u32[]{:S(2)}) %collective-permute-start.20) | collective-permute-done | bytes 65568 | tf_op jit(solution)/shard_map/ppermute | solution.py:20
  70.1 2.4 %collective-permute-start.21 = (bf16[2,128,128]{2,1,0:T(8,128)(2,1)S(1)}, bf16[2,128,128]{2,1,0:T(8,128)(2,1)S(1)}, u32[]{:S(2)}, u32[]{:S(2)}) collective-permute-start(bf16[2,128,128]{2,1,0:T(8,128)(2,1)S(1)} %pad_maximum_fusion.12), channel_id=1, source_target_pairs={{0,6},{1,7},{2,4},{3,5},{4,2},{5,3},{6,0},{7,1},{8,14},{9,15},{10,... | collective-permute-start | bytes 196616 | tf_op jit(solution)/shard_map/ppermute | solution.py:20
  72.5 1.9 %collective-permute-start.22 = (bf16[2,128,128]{2,1,0:T(8,128)(2,1)S(1)}, bf16[2,128,128]{2,1,0:T(8,128)(2,1)S(1)}, u32[]{:S(2)}, u32[]{:S(2)}) collective-permute-start(bf16[2,128,128]{2,1,0:T(8,128)(2,1)S(1)} %pad_maximum_fusion.12), channel_id=1, source_target_pairs={{0,4},{1,5},{2,6},{3,7},{4,0},{5,1},{6,2},{7,3},{8,12},{9,13},{10,... | collective-permute-start | bytes 196616 | tf_op jit(solution)/shard_map/ppermute | solution.py:20
  74.7 2.2 %collective-permute-done.21 = bf16[2,128,128]{2,1,0:T(8,128)(2,1)S(1)} collective-permute-done((bf16[2,128,128]{2,1,0:T(8,128)(2,1)S(1)}, bf16[2,128,128]{2,1,0:T(8,128)(2,1)S(1)}, u32[]{:S(2)}, u32[]{:S(2)}) %collective-permute-start.21) | collective-permute-done | bytes 65568 | tf_op jit(solution)/shard_map/ppermute | solution.py:20
  76.9 1.7 %collective-permute-done.22 = bf16[2,128,128]{2,1,0:T(8,128)(2,1)S(1)} collective-permute-done((bf16[2,128,128]{2,1,0:T(8,128)(2,1)S(1)}, bf16[2,128,128]{2,1,0:T(8,128)(2,1)S(1)}, u32[]{:S(2)}, u32[]{:S(2)}) %collective-permute-start.22) | collective-permute-done | bytes 65568 | tf_op jit(solution)/shard_map/ppermute | solution.py:20
  79.5 1.5 %collective-permute-start.26 = (bf16[2,128,128]{2,1,0:T(8,128)(2,1)S(1)}, bf16[2,128,128]{2,1,0:T(8,128)(2,1)S(1)}, u32[]{:S(2)}, u32[]{:S(2)}) collective-permute-start(bf16[2,128,128]{2,1,0:T(8,128)(2,1)S(1)} %bitcast.120), channel_id=1, source_target_pairs={{0,6},{1,7},{2,4},{3,5},{4,2},{5,3},{6,0},{7,1},{8,14},{9,15},{10,... | collective-permute-start | bytes 196616 | tf_op jit(solution)/shard_map/ppermute | solution.py:20
  81.2 2.8 %collective-permute-start.28 = (bf16[2,128,128]{2,1,0:T(8,128)(2,1)S(1)}, bf16[2,128,128]{2,1,0:T(8,128)(2,1)S(1)}, u32[]{:S(2)}, u32[]{:S(2)}) collective-permute-start(bf16[2,128,128]{2,1,0:T(8,128)(2,1)S(1)} %bitcast.122), channel_id=1, source_target_pairs={{0,2},{1,3},{2,0},{3,1},{4,6},{5,7},{6,4},{7,5},{8,10},{9,11},{10,... | collective-permute-start | bytes 196616 | tf_op jit(solution)/shard_map/ppermute | solution.py:20
  84.2 1.5 %collective-permute-done.26 = bf16[2,128,128]{2,1,0:T(8,128)(2,1)S(1)} collective-permute-done((bf16[2,128,128]{2,1,0:T(8,128)(2,1)S(1)}, bf16[2,128,128]{2,1,0:T(8,128)(2,1)S(1)}, u32[]{:S(2)}, u32[]{:S(2)}) %collective-permute-start.26) | collective-permute-done | bytes 65568 | tf_op jit(solution)/shard_map/ppermute | solution.py:20
  85.7 1.4 %collective-permute-done.27 = bf16[2,128,128]{2,1,0:T(8,128)(2,1)S(1)} collective-permute-done((bf16[2,128,128]{2,1,0:T(8,128)(2,1)S(1)}, bf16[2,128,128]{2,1,0:T(8,128)(2,1)S(1)}, u32[]{:S(2)}, u32[]{:S(2)}) %collective-permute-start.27) | collective-permute-done | bytes 65568 | tf_op jit(solution)/shard_map/ppermute | solution.py:20
  87.6 1.6 %collective-permute-start.29 = (bf16[2,128,128]{2,1,0:T(8,128)(2,1)S(1)}, bf16[2,128,128]{2,1,0:T(8,128)(2,1)S(1)}, u32[]{:S(2)}, u32[]{:S(2)}) collective-permute-start(bf16[2,128,128]{2,1,0:T(8,128)(2,1)S(1)} %pad_maximum_fusion.13), channel_id=1, source_target_pairs={{0,6},{1,7},{2,4},{3,5},{4,2},{5,3},{6,0},{7,1},{8,14},{9,15},{10,... | collective-permute-start | bytes 196616 | tf_op jit(solution)/shard_map/ppermute | solution.py:20
  90.3 1.8 %collective-permute-start.31 = (bf16[2,128,128]{2,1,0:T(8,128)(2,1)S(1)}, bf16[2,128,128]{2,1,0:T(8,128)(2,1)S(1)}, u32[]{:S(2)}, u32[]{:S(2)}) collective-permute-start(bf16[2,128,128]{2,1,0:T(8,128)(2,1)S(1)} %pad_maximum_fusion.13), channel_id=1, source_target_pairs={{0,2},{1,3},{2,0},{3,1},{4,6},{5,7},{6,4},{7,5},{8,10},{9,11},{10,... | collective-permute-start | bytes 196616 | tf_op jit(solution)/shard_map/ppermute | solution.py:20
  92.1 1.6 %collective-permute-done.29 = bf16[2,128,128]{2,1,0:T(8,128)(2,1)S(1)} collective-permute-done((bf16[2,128,128]{2,1,0:T(8,128)(2,1)S(1)}, bf16[2,128,128]{2,1,0:T(8,128)(2,1)S(1)}, u32[]{:S(2)}, u32[]{:S(2)}) %collective-permute-start.29) | collective-permute-done | bytes 65568 | tf_op jit(solution)/shard_map/ppermute | solution.py:20
  93.7 1.5 %collective-permute-done.30 = bf16[2,128,128]{2,1,0:T(8,128)(2,1)S(1)} collective-permute-done((bf16[2,128,128]{2,1,0:T(8,128)(2,1)S(1)}, bf16[2,128,128]{2,1,0:T(8,128)(2,1)S(1)}, u32[]{:S(2)}, u32[]{:S(2)}) %collective-permute-start.30) | collective-permute-done | bytes 65568 | tf_op jit(solution)/shard_map/ppermute | solution.py:20
  95.7 1.4 %collective-permute-start.36 = (bf16[128,128]{1,0:T(8,128)(2,1)S(1)}, bf16[128,128]{1,0:T(8,128)(2,1)S(1)}, u32[]{:S(2)}, u32[]{:S(2)}) collective-permute-start(bf16[128,128]{1,0:T(8,128)(2,1)S(1)} %get-tuple-element.65), channel_id=1, source_target_pairs={{0,24},{1,25},{2,26},{3,27},{4,28},{5,29},{6,30},{7,31},{8,16},{9,... | collective-permute-start | bytes 98312 | tf_op jit(solution)/shard_map/ppermute | solution.py:20
  97.5 1.8 %collective-permute-start.38 = (bf16[128,128]{1,0:T(8,128)(2,1)S(1)}, bf16[128,128]{1,0:T(8,128)(2,1)S(1)}, u32[]{:S(2)}, u32[]{:S(2)}) collective-permute-start(bf16[128,128]{1,0:T(8,128)(2,1)S(1)} %get-tuple-element.66), channel_id=1, source_target_pairs={{0,8},{1,9},{2,10},{3,11},{4,12},{5,13},{6,14},{7,15},{8,0},{9,1},... | collective-permute-start | bytes 98312 | tf_op jit(solution)/shard_map/ppermute | solution.py:20
  99.3 1.3 %collective-permute-done.36 = bf16[128,128]{1,0:T(8,128)(2,1)S(1)} collective-permute-done((bf16[128,128]{1,0:T(8,128)(2,1)S(1)}, bf16[128,128]{1,0:T(8,128)(2,1)S(1)}, u32[]{:S(2)}, u32[]{:S(2)}) %collective-permute-start.36) | collective-permute-done | bytes 32800 | tf_op jit(solution)/shard_map/ppermute | solution.py:20
  (153 shorter events, 24.6 us)
Async XLA Ops:
  0.7 18.1 %collective-permute-start.9 = (bf16[64,3072]{1,0:T(8,128)(2,1)}, bf16[64,3072]{1,0:T(8,128)(2,1)S(1)}, u32[]{:S(2)}, u32[]{:S(2)}) collective-permute-start(bf16[64,3072]{1,0:T(8,128)(2,1)} %param.11), channel_id=1, source_target_pairs={{0,8},{1,9},{2,10},{3,11},{4,12},{5,13},{6,14},{7,15},{8,0},{9,1},... | collective-permute-start | bytes 1179656 | tf_op jit(solution)/shard_map/ppermute | solution.py:20
  3.7 22.2 %collective-permute-start.11 = (bf16[64,3072]{1,0:T(8,128)(2,1)}, bf16[64,3072]{1,0:T(8,128)(2,1)S(1)}, u32[]{:S(2)}, u32[]{:S(2)}) collective-permute-start(bf16[64,3072]{1,0:T(8,128)(2,1)} %param.11), channel_id=1, source_target_pairs={{0,1},{1,0},{2,3},{3,2},{4,5},{5,4},{6,7},{7,6},{8,9},{9,8},{10,11... | collective-permute-start | bytes 1179656 | tf_op jit(solution)/shard_map/ppermute | solution.py:20
  3.7 17.6 %collective-permute-start.32 = (bf16[64,3072]{1,0:T(8,128)(2,1)}, bf16[64,3072]{1,0:T(8,128)(2,1)}, u32[]{:S(2)}, u32[]{:S(2)}) collective-permute-start(bf16[64,3072]{1,0:T(8,128)(2,1)} %param.11), channel_id=1, source_target_pairs={{0,16},{1,17},{2,18},{3,19},{4,20},{5,21},{6,22},{7,23},{8,24},{9,... | collective-permute-start | bytes 1179656 | tf_op jit(solution)/shard_map/ppermute | solution.py:20
  5.4 7.7 %collective-permute-start.12 = (bf16[2,64,256]{2,1,0:T(8,128)(2,1)}, bf16[2,64,256]{2,1,0:T(8,128)(2,1)S(1)}, u32[]{:S(2)}, u32[]{:S(2)}) collective-permute-start(bf16[2,64,256]{2,1,0:T(8,128)(2,1)} %param.10), channel_id=1, source_target_pairs={{0,1},{1,0},{2,3},{3,2},{4,5},{5,4},{6,7},{7,6},{8,9},{9,8},{10,11... | collective-permute-start | bytes 196616 | tf_op jit(solution)/shard_map/ppermute | solution.py:20
  8.4 4.7 %collective-permute-start.15 = (s32[2,2]{1,0:T(2,128)S(1)}, s32[2,2]{1,0:T(2,128)S(1)}, u32[]{:S(2)}, u32[]{:S(2)}) collective-permute-start(s32[2,2]{1,0:T(2,128)S(1)} %get-tuple-element.32), channel_id=1, source_target_pairs={{0,8},{1,9},{2,10},{3,11},{4,12},{5,13},{6,14},{7,15},{8,0},{9,1},... | collective-permute-start | bytes 56 | tf_op jit(solution)/shard_map/ppermute | solution.py:20
  13.1 12.8 %collective-permute-start.34 = (bf16[64,3072]{1,0:T(8,128)(2,1)}, bf16[64,3072]{1,0:T(8,128)(2,1)S(1)}, u32[]{:S(2)}, u32[]{:S(2)}) collective-permute-start(bf16[64,3072]{1,0:T(8,128)(2,1)} %param.11), channel_id=1, source_target_pairs={{0,24},{1,25},{2,26},{3,27},{4,28},{5,29},{6,30},{7,31},{8,16},{9,... | collective-permute-start | bytes 1179656 | tf_op jit(solution)/shard_map/ppermute | solution.py:20
  16.7 19.4 %collective-permute-start.4 = (bf16[320,128]{1,0:T(8,128)(2,1)S(1)}, bf16[320,128]{1,0:T(8,128)(2,1)S(1)}, u32[]{:S(2)}, u32[]{:S(2)}) collective-permute-start(bf16[320,128]{1,0:T(8,128)(2,1)S(1)} %get-tuple-element.11), channel_id=1, source_target_pairs={{0,1},{1,0},{2,3},{3,2},{4,5},{5,4},{6,7},{7,6},{8,9},{9,8},{10,11... | collective-permute-start | bytes 245768 | tf_op jit(solution)/shard_map/ppermute | solution.py:20
  18.8 22.6 %collective-permute-start.6 = (bf16[320,128]{1,0:T(8,128)(2,1)S(1)}, bf16[320,128]{1,0:T(8,128)(2,1)S(1)}, u32[]{:S(2)}, u32[]{:S(2)}) collective-permute-start(bf16[320,128]{1,0:T(8,128)(2,1)S(1)} %get-tuple-element.11), channel_id=1, source_target_pairs={{0,5},{1,4},{2,7},{3,6},{4,1},{5,0},{6,3},{7,2},{8,13},{9,12},{10,... | collective-permute-start | bytes 245768 | tf_op jit(solution)/shard_map/ppermute | solution.py:20
  21.3 6.8 %collective-permute-start.16 = (bf16[128,2560]{1,0:T(8,128)(2,1)S(1)}, bf16[128,2560]{1,0:T(8,128)(2,1)S(1)}, u32[]{:S(2)}, u32[]{:S(2)}) collective-permute-start(bf16[128,2560]{1,0:T(8,128)(2,1)S(1)} %copy-done.4), channel_id=1, source_target_pairs={{0,1},{1,0},{2,3},{3,2},{4,5},{5,4},{6,7},{7,6},{8,9},{9,8},{10,11... | collective-permute-start | bytes 1966088 | tf_op jit(solution)/shard_map/ppermute | solution.py:20
  25.9 15.6 %collective-permute-start.7 = (bf16[320,2560]{1,0:T(8,128)(2,1)S(1)}, bf16[320,2560]{1,0:T(8,128)(2,1)S(1)}, u32[]{:S(2)}, u32[]{:S(2)}) collective-permute-start(bf16[320,2560]{1,0:T(8,128)(2,1)S(1)} %copy-done), channel_id=1, source_target_pairs={{0,1},{1,0},{2,3},{3,2},{4,5},{5,4},{6,7},{7,6},{8,9},{9,8},{10,11... | collective-permute-start | bytes 4915208 | tf_op jit(solution)/shard_map/ppermute | solution.py:20
  25.9 4.0 %collective-permute-start.10 = (bf16[64,3072]{1,0:T(8,128)(2,1)S(1)}, bf16[64,3072]{1,0:T(8,128)(2,1)S(1)}, u32[]{:S(2)}, u32[]{:S(2)}) collective-permute-start(bf16[64,3072]{1,0:T(8,128)(2,1)S(1)} %collective-permute-done.9), channel_id=1, source_target_pairs={{0,1},{1,0},{2,3},{3,2},{4,5},{5,4},{6,7},{7,6},{8,9},{9,8},{10,11... | collective-permute-start | bytes 1179656 | tf_op jit(solution)/shard_map/ppermute | solution.py:20
  30.5 7.4 %collective-permute-start.5 = (bf16[320,128]{1,0:T(8,128)(2,1)S(1)}, bf16[320,128]{1,0:T(8,128)(2,1)S(1)}, u32[]{:S(2)}, u32[]{:S(2)}) collective-permute-start(bf16[320,128]{1,0:T(8,128)(2,1)S(1)} %get-tuple-element.10.refs_0_), channel_id=1, source_target_pairs={{0,4},{1,5},{2,6},{3,7},{4,0},{5,1},{6,2},{7,3},{8,12},{9,13},{10,... | collective-permute-start | bytes 245768 | tf_op jit(solution)/shard_map/ppermute | solution.py:20
  33.4 15.2 %collective-permute-start = (bf16[320,128]{1,0:T(8,128)(2,1)S(1)}, bf16[320,128]{1,0:T(8,128)(2,1)S(1)}, u32[]{:S(2)}, u32[]{:S(2)}) collective-permute-start(bf16[320,128]{1,0:T(8,128)(2,1)S(1)} %get-tuple-element.10.refs_0_), channel_id=1, source_target_pairs={{0,2},{1,3},{2,0},{3,1},{4,6},{5,7},{6,4},{7,5},{8,10},{9,11},{10,... | collective-permute-start | bytes 245768 | tf_op jit(solution)/shard_map/ppermute | solution.py:20
  36.1 12.6 %collective-permute-start.1 = (bf16[320,128]{1,0:T(8,128)(2,1)S(1)}, bf16[320,128]{1,0:T(8,128)(2,1)S(1)}, u32[]{:S(2)}, u32[]{:S(2)}) collective-permute-start(bf16[320,128]{1,0:T(8,128)(2,1)S(1)} %get-tuple-element.11), channel_id=1, source_target_pairs={{0,3},{1,2},{2,1},{3,0},{4,7},{5,6},{6,5},{7,4},{8,11},{9,10},{10,... | collective-permute-start | bytes 245768 | tf_op jit(solution)/shard_map/ppermute | solution.py:20
  37.9 10.8 %collective-permute-start.2 = (bf16[320,128]{1,0:T(8,128)(2,1)S(1)}, bf16[320,128]{1,0:T(8,128)(2,1)S(1)}, u32[]{:S(2)}, u32[]{:S(2)}) collective-permute-start(bf16[320,128]{1,0:T(8,128)(2,1)S(1)} %get-tuple-element.10.refs_0_), channel_id=1, source_target_pairs={{0,6},{1,7},{2,4},{3,5},{4,2},{5,3},{6,0},{7,1},{8,14},{9,15},{10,... | collective-permute-start | bytes 245768 | tf_op jit(solution)/shard_map/ppermute | solution.py:20
  41.4 7.2 %collective-permute-start.3 = (bf16[320,128]{1,0:T(8,128)(2,1)S(1)}, bf16[320,128]{1,0:T(8,128)(2,1)S(1)}, u32[]{:S(2)}, u32[]{:S(2)}) collective-permute-start(bf16[320,128]{1,0:T(8,128)(2,1)S(1)} %get-tuple-element.11), channel_id=1, source_target_pairs={{0,7},{1,6},{2,5},{3,4},{4,3},{5,2},{6,1},{7,0},{8,15},{9,14},{10,... | collective-permute-start | bytes 245768 | tf_op jit(solution)/shard_map/ppermute | solution.py:20
  43.6 26.5 %collective-permute-start.13 = (bf16[128,128]{1,0:T(8,128)(2,1)S(1)}, bf16[128,128]{1,0:T(8,128)(2,1)S(1)}, u32[]{:S(2)}, u32[]{:S(2)}) collective-permute-start(bf16[128,128]{1,0:T(8,128)(2,1)S(1)} %fusion.28), channel_id=1, source_target_pairs={{0,8},{1,9},{2,10},{3,11},{4,12},{5,13},{6,14},{7,15},{8,0},{9,1},... | collective-permute-start | bytes 98312 | tf_op jit(solution)/shard_map/ppermute | solution.py:20
  49.3 15.1 %collective-permute-start.17 = (bf16[640,128]{1,0:T(8,128)(2,1)S(1)}, bf16[640,128]{1,0:T(8,128)(2,1)S(1)}, u32[]{:S(2)}, u32[]{:S(2)}) collective-permute-start(bf16[640,128]{1,0:T(8,128)(2,1)S(1)} %get-tuple-element.17), channel_id=1, source_target_pairs={{0,4},{1,5},{2,6},{3,7},{4,0},{5,1},{6,2},{7,3},{8,12},{9,13},{10,... | collective-permute-start | bytes 491528 | tf_op jit(solution)/shard_map/ppermute | solution.py:20
  49.4 15.1 %collective-permute-start.18 = (bf16[640,128]{1,0:T(8,128)(2,1)S(1)}, bf16[640,128]{1,0:T(8,128)(2,1)S(1)}, u32[]{:S(2)}, u32[]{:S(2)}) collective-permute-start(bf16[640,128]{1,0:T(8,128)(2,1)S(1)} %get-tuple-element.17), channel_id=1, source_target_pairs={{0,6},{1,7},{2,4},{3,5},{4,2},{5,3},{6,0},{7,1},{8,14},{9,15},{10,... | collective-permute-start | bytes 491528 | tf_op jit(solution)/shard_map/ppermute | solution.py:20
  52.6 12.4 %collective-permute-start.19 = (bf16[640,128]{1,0:T(8,128)(2,1)S(1)}, bf16[640,128]{1,0:T(8,128)(2,1)S(1)}, u32[]{:S(2)}, u32[]{:S(2)}) collective-permute-start(bf16[640,128]{1,0:T(8,128)(2,1)S(1)} %get-tuple-element.17), channel_id=1, source_target_pairs={{0,2},{1,3},{2,0},{3,1},{4,6},{5,7},{6,4},{7,5},{8,10},{9,11},{10,... | collective-permute-start | bytes 491528 | tf_op jit(solution)/shard_map/ppermute | solution.py:20
  65.6 4.3 %collective-permute-start.20 = (bf16[2,2,64,128]{3,2,1,0:T(8,128)(2,1)S(1)}, bf16[2,2,64,128]{3,2,1,0:T(8,128)(2,1)S(1)}, u32[]{:S(2)}, u32[]{:S(2)}) collective-permute-start(bf16[2,2,64,128]{3,2,1,0:T(8,128)(2,1)S(1)} %get-tuple-element.83), channel_id=1, source_target_pairs={{0,8},{1,9},{2,10},{3,11},{4,12},{5,13},{6,14},{7,15},{8,0},{9,1},... | collective-permute-start | bytes 196616 | tf_op jit(solution)/shard_map/ppermute | solution.py:20
  70.1 6.8 %collective-permute-start.21 = (bf16[2,128,128]{2,1,0:T(8,128)(2,1)S(1)}, bf16[2,128,128]{2,1,0:T(8,128)(2,1)S(1)}, u32[]{:S(2)}, u32[]{:S(2)}) collective-permute-start(bf16[2,128,128]{2,1,0:T(8,128)(2,1)S(1)} %pad_maximum_fusion.12), channel_id=1, source_target_pairs={{0,6},{1,7},{2,4},{3,5},{4,2},{5,3},{6,0},{7,1},{8,14},{9,15},{10,... | collective-permute-start | bytes 196616 | tf_op jit(solution)/shard_map/ppermute | solution.py:20
  72.5 6.1 %collective-permute-start.22 = (bf16[2,128,128]{2,1,0:T(8,128)(2,1)S(1)}, bf16[2,128,128]{2,1,0:T(8,128)(2,1)S(1)}, u32[]{:S(2)}, u32[]{:S(2)}) collective-permute-start(bf16[2,128,128]{2,1,0:T(8,128)(2,1)S(1)} %pad_maximum_fusion.12), channel_id=1, source_target_pairs={{0,4},{1,5},{2,6},{3,7},{4,0},{5,1},{6,2},{7,3},{8,12},{9,13},{10,... | collective-permute-start | bytes 196616 | tf_op jit(solution)/shard_map/ppermute | solution.py:20
  74.3 4.9 %collective-permute-start.23 = (bf16[2,128,128]{2,1,0:T(8,128)(2,1)S(1)}, bf16[2,128,128]{2,1,0:T(8,128)(2,1)S(1)}, u32[]{:S(2)}, u32[]{:S(2)}) collective-permute-start(bf16[2,128,128]{2,1,0:T(8,128)(2,1)S(1)} %pad_maximum_fusion.12), channel_id=1, source_target_pairs={{0,2},{1,3},{2,0},{3,1},{4,6},{5,7},{6,4},{7,5},{8,10},{9,11},{10,... | collective-permute-start | bytes 196616 | tf_op jit(solution)/shard_map/ppermute | solution.py:20
  79.5 6.2 %collective-permute-start.26 = (bf16[2,128,128]{2,1,0:T(8,128)(2,1)S(1)}, bf16[2,128,128]{2,1,0:T(8,128)(2,1)S(1)}, u32[]{:S(2)}, u32[]{:S(2)}) collective-permute-start(bf16[2,128,128]{2,1,0:T(8,128)(2,1)S(1)} %bitcast.120), channel_id=1, source_target_pairs={{0,6},{1,7},{2,4},{3,5},{4,2},{5,3},{6,0},{7,1},{8,14},{9,15},{10,... | collective-permute-start | bytes 196616 | tf_op jit(solution)/shard_map/ppermute | solution.py:20
  81.1 6.0 %collective-permute-start.27 = (bf16[2,128,128]{2,1,0:T(8,128)(2,1)S(1)}, bf16[2,128,128]{2,1,0:T(8,128)(2,1)S(1)}, u32[]{:S(2)}, u32[]{:S(2)}) collective-permute-start(bf16[2,128,128]{2,1,0:T(8,128)(2,1)S(1)} %bitcast.121), channel_id=1, source_target_pairs={{0,4},{1,5},{2,6},{3,7},{4,0},{5,1},{6,2},{7,3},{8,12},{9,13},{10,... | collective-permute-start | bytes 196616 | tf_op jit(solution)/shard_map/ppermute | solution.py:20
  81.2 5.9 %collective-permute-start.28 = (bf16[2,128,128]{2,1,0:T(8,128)(2,1)S(1)}, bf16[2,128,128]{2,1,0:T(8,128)(2,1)S(1)}, u32[]{:S(2)}, u32[]{:S(2)}) collective-permute-start(bf16[2,128,128]{2,1,0:T(8,128)(2,1)S(1)} %bitcast.122), channel_id=1, source_target_pairs={{0,2},{1,3},{2,0},{3,1},{4,6},{5,7},{6,4},{7,5},{8,10},{9,11},{10,... | collective-permute-start | bytes 196616 | tf_op jit(solution)/shard_map/ppermute | solution.py:20
  84.0 15.2 %collective-permute-start.24 = (bf16[64,128]{1,0:T(8,128)(2,1)S(1)}, bf16[64,128]{1,0:T(8,128)(2,1)S(1)}, u32[]{:S(2)}, u32[]{:S(2)}) collective-permute-start(bf16[64,128]{1,0:T(8,128)(2,1)S(1)} %constant_dynamic-slice_fusion.17), channel_id=1, source_target_pairs={{0,1},{1,0},{2,3},{3,2},{4,5},{5,4},{6,7},{7,6},{8,9},{9,8},{10,11... | collective-permute-start | bytes 49160 | tf_op jit(solution)/shard_map/ppermute | solution.py:20
  87.6 6.1 %collective-permute-start.29 = (bf16[2,128,128]{2,1,0:T(8,128)(2,1)S(1)}, bf16[2,128,128]{2,1,0:T(8,128)(2,1)S(1)}, u32[]{:S(2)}, u32[]{:S(2)}) collective-permute-start(bf16[2,128,128]{2,1,0:T(8,128)(2,1)S(1)} %pad_maximum_fusion.13), channel_id=1, source_target_pairs={{0,6},{1,7},{2,4},{3,5},{4,2},{5,3},{6,0},{7,1},{8,14},{9,15},{10,... | collective-permute-start | bytes 196616 | tf_op jit(solution)/shard_map/ppermute | solution.py:20
  89.2 6.0 %collective-permute-start.30 = (bf16[2,128,128]{2,1,0:T(8,128)(2,1)S(1)}, bf16[2,128,128]{2,1,0:T(8,128)(2,1)S(1)}, u32[]{:S(2)}, u32[]{:S(2)}) collective-permute-start(bf16[2,128,128]{2,1,0:T(8,128)(2,1)S(1)} %pad_maximum_fusion.13), channel_id=1, source_target_pairs={{0,4},{1,5},{2,6},{3,7},{4,0},{5,1},{6,2},{7,3},{8,12},{9,13},{10,... | collective-permute-start | bytes 196616 | tf_op jit(solution)/shard_map/ppermute | solution.py:20
  90.3 5.0 %collective-permute-start.31 = (bf16[2,128,128]{2,1,0:T(8,128)(2,1)S(1)}, bf16[2,128,128]{2,1,0:T(8,128)(2,1)S(1)}, u32[]{:S(2)}, u32[]{:S(2)}) collective-permute-start(bf16[2,128,128]{2,1,0:T(8,128)(2,1)S(1)} %pad_maximum_fusion.13), channel_id=1, source_target_pairs={{0,2},{1,3},{2,0},{3,1},{4,6},{5,7},{6,4},{7,5},{8,10},{9,11},{10,... | collective-permute-start | bytes 196616 | tf_op jit(solution)/shard_map/ppermute | solution.py:20
  95.7 4.9 %collective-permute-start.36 = (bf16[128,128]{1,0:T(8,128)(2,1)S(1)}, bf16[128,128]{1,0:T(8,128)(2,1)S(1)}, u32[]{:S(2)}, u32[]{:S(2)}) collective-permute-start(bf16[128,128]{1,0:T(8,128)(2,1)S(1)} %get-tuple-element.65), channel_id=1, source_target_pairs={{0,24},{1,25},{2,26},{3,27},{4,28},{5,29},{6,30},{7,31},{8,16},{9,... | collective-permute-start | bytes 98312 | tf_op jit(solution)/shard_map/ppermute | solution.py:20
  (23 other events, 206.2 us)
